TPU v7x, 32 devices: a whole 2x2x4 slice. The times are simulated.
32 devices in a mesh: section: 4 (over z), dp: 2 (over x), space: 4 (over y, core).
Axes of the slice: x: 2, y: 2, z: 4, core: 2. Of those that a mesh axis runs over, the one named last changes fastest.
Arguments:
- enc_input: bfloat16 [4, 2, 32, 8, 8, 128], P('section', 'dp', None, 'space'), may hold values from -6 to 6
- dec_input: bfloat16 [4, 2, 32, 8, 8, 128], P('section', 'dp', None, None, 'space'), may hold values from -6 to 6
- dec_cotangent: bfloat16 [4, 2, 32, 8, 8, 128], P('section', 'dp', None, None, 'space'), may hold values from -6 to 6
- deep_cotangent: bfloat16 [4, 2, 32, 8, 8, 128], P('section', 'dp', None, 'space'), may hold values from -6 to 6
- enc_weight: bfloat16 [4, 27, 32, 32], P('section'), may hold values from -0.21875 to 0.21875
- dec_weight: bfloat16 [4, 27, 32, 64], P('section'), may hold values from -0.15625 to 0.15625
- enc_gain: float32 [4, 32], P('section'), may hold values from 0.25 to 1.75
- enc_bias: float32 [4, 32], P('section'), may hold values from -2 to 2
- dec_gain: float32 [4, 32], P('section'), may hold values from 0.25 to 1.75
- dec_bias: float32 [4, 32], P('section'), may hold values from -2 to 2
Outputs:
- enc_handoff: bfloat16 [4, 2, 32, 8, 8, 128], P('section', 'dp', None, 'space')
- dec_handoff: bfloat16 [4, 2, 32, 8, 8, 128], P('section', 'dp', None, None, 'space')
- enc_weight_grad: float32 [4, 27648], P('section', ('dp', 'space'))
- dec_weight_grad: float32 [4, 55296], P('section', ('dp', 'space'))
All inputs are finite; a program needn't handle non-finite values.
Results may differ from a plain program's by a relative error of at most 0.0075.
Values may be sent and summed in bfloat16 or wider, within the bound.
No kernel may reach another device: no remote copies, remote signals or barrier semaphores. Data moves between devices by JAX's collectives and lax.ppermute only.
A program may use at most 64 MiB of HBM per device.

v0:
```python
import math

import jax
import jax.numpy as jnp
from jax import lax
from jax.sharding import PartitionSpec as P

EPS = 1e-05


def padded_2(cells, sides, width):
    for axis, dim in sides:
        count = lax.axis_size(axis)
        ends = count - 1
        head = lax.slice_in_dim(cells, 0, width, axis=dim)
        tail = lax.slice_in_dim(cells, cells.shape[dim] - width, cells.shape[dim], axis=dim)
        cells = jnp.concatenate(
            [
                lax.ppermute(tail, axis, [(i, (i + 1) % count) for i in range(ends)]),
                cells,
                lax.ppermute(head, axis, [((i + 1) % count, i) for i in range(ends)]),
            ],
            axis=dim,
        )
    return cells


def shifted_2(block, axis, distance):
    devices = range(lax.axis_size(axis))
    route = [(i - distance, i) for i in devices if i - distance in devices]
    return lax.ppermute(block, axis, route)


def convolve(padded, weights):
    depth_cells = padded.shape[1] - 2
    height_cells = padded.shape[2] - 2
    width_cells = padded.shape[3] - 2
    summed = jnp.zeros((weights.shape[1], depth_cells, height_cells, width_cells), jnp.float32)
    for depth_tap in range(3):
        for height_tap in range(3):
            shifted = jnp.stack(
                [
                    padded[
                        :,
                        depth_tap : depth_tap + depth_cells,
                        height_tap : height_tap + height_cells,
                        width_tap : width_tap + width_cells,
                    ]
                    for width_tap in range(3)
                ]
            )
            first = depth_tap * 9 + height_tap * 3
            tap_weights = weights[first : first + 3]
            summed = summed + jnp.einsum(
                "koi,kidhw->odhw", tap_weights, shifted, preferred_element_type=jnp.float32
            )
    return summed


def weight_terms(padded, cotangent):
    depth_cells = cotangent.shape[1]
    height_cells = cotangent.shape[2]
    width_cells = cotangent.shape[3]
    pieces = []
    for depth_tap in range(3):
        for height_tap in range(3):
            shifted = jnp.stack(
                [
                    padded[
                        :,
                        depth_tap : depth_tap + depth_cells,
                        height_tap : height_tap + height_cells,
                        width_tap : width_tap + width_cells,
                    ]
                    for width_tap in range(3)
                ]
            )
            pieces.append(
                jnp.einsum(
                    "odhw,kidhw->koi", cotangent, shifted, preferred_element_type=jnp.float32
                )
            )
    return jnp.concatenate(pieces, axis=0)


def channel_view(values):
    return values[:, None, None, None]


def body(
    enc_input,
    dec_input,
    dec_cotangent,
    deep_cotangent,
    enc_weight,
    dec_weight,
    enc_gain,
    enc_bias,
    dec_gain,
    dec_bias,
):
    volume = enc_input[0, 0]
    channels = volume.shape[0]
    slabs = lax.axis_size("space")
    voxels = volume.shape[1] * slabs * volume.shape[2] * volume.shape[3]
    grad_scale = 1.0 / math.sqrt(lax.axis_size("dp") * voxels)
    enc_rimmed = padded_2(volume, (("space", 1),), 1)
    enc_padded = jnp.pad(enc_rimmed, ((0, 0), (0, 0), (1, 1), (1, 1)))
    enc_pre = convolve(enc_padded, enc_weight[0])
    enc_sums, enc_squares = lax.psum(
        (jnp.sum(enc_pre, axis=(1, 2, 3)), jnp.sum(enc_pre * enc_pre, axis=(1, 2, 3))), "space"
    )
    enc_mean = enc_sums / voxels
    enc_scale = lax.rsqrt(enc_squares / voxels - enc_mean * enc_mean + EPS)
    enc_hat = (enc_pre - channel_view(enc_mean)) * channel_view(enc_scale)
    enc_normed = channel_view(enc_gain[0]) * enc_hat + channel_view(enc_bias[0])
    skip_act = jnp.maximum(enc_normed, 0.0).astype(jnp.bfloat16)
    enc_handoff = shifted_2(skip_act[None, None], "section", 1)
    skip_high = lax.all_to_all(skip_act, "space", split_axis=2, concat_axis=1, tiled=True)
    joined = jnp.concatenate([dec_input[0, 0], skip_high], axis=0)
    dec_rimmed = padded_2(joined, (("space", 2),), 1)
    dec_padded = jnp.pad(dec_rimmed, ((0, 0), (1, 1), (0, 0), (1, 1)))
    dec_pre = convolve(dec_padded, dec_weight[0])
    dec_sums, dec_squares = lax.psum(
        (jnp.sum(dec_pre, axis=(1, 2, 3)), jnp.sum(dec_pre * dec_pre, axis=(1, 2, 3))), "space"
    )
    dec_mean = dec_sums / voxels
    dec_scale = lax.rsqrt(dec_squares / voxels - dec_mean * dec_mean + EPS)
    dec_hat = (dec_pre - channel_view(dec_mean)) * channel_view(dec_scale)
    dec_act = jnp.maximum(
        channel_view(dec_gain[0]) * dec_hat + channel_view(dec_bias[0]), 0.0
    ).astype(jnp.bfloat16)
    dec_handoff = shifted_2(dec_act[None, None], "section", -1)
    cotangent = dec_cotangent[0, 0]
    dec_grad = weight_terms(dec_padded, cotangent).reshape(-1) * grad_scale
    flipped = jnp.swapaxes(dec_weight[0][::-1, :, channels:], 1, 2)
    cot_low = lax.all_to_all(cotangent, "space", split_axis=1, concat_axis=2, tiled=True)
    cot_rimmed = padded_2(cot_low, (("space", 1),), 1)
    cot_padded = jnp.pad(cot_rimmed, ((0, 0), (0, 0), (1, 1), (1, 1)))
    skip_grad = convolve(cot_padded, flipped).astype(jnp.bfloat16)
    upstream = skip_grad.astype(jnp.float32) + deep_cotangent[0, 0].astype(jnp.float32)
    gated = jnp.where(enc_normed > 0, upstream, 0.0) * channel_view(enc_gain[0])
    first_sum, second_sum = lax.psum(
        (jnp.sum(gated, axis=(1, 2, 3)), jnp.sum(gated * enc_hat, axis=(1, 2, 3))), "space"
    )
    enc_pre_grad = (
        (gated - channel_view(first_sum / voxels) - enc_hat * channel_view(second_sum / voxels))
        * channel_view(enc_scale)
    ).astype(jnp.bfloat16)
    enc_grad = weight_terms(enc_padded, enc_pre_grad).reshape(-1) * grad_scale
    enc_part, dec_part = (
        lax.psum_scatter(enc_grad, ("dp", "space"), scatter_dimension=0, tiled=True),
        lax.psum_scatter(dec_grad, ("dp", "space"), scatter_dimension=0, tiled=True),
    )
    return (enc_handoff, dec_handoff, enc_part[None], dec_part[None])


def solution(mesh):
    in_specs = (
        P("section", "dp", None, "space", None, None),
        P("section", "dp", None, None, "space", None),
        P("section", "dp", None, None, "space", None),
        P("section", "dp", None, "space", None, None),
        P("section", None, None, None),
        P("section", None, None, None),
        P("section", None),
        P("section", None),
        P("section", None),
        P("section", None),
    )
    out_specs = (
        P("section", "dp", None, "space", None, None),
        P("section", "dp", None, None, "space", None),
        P("section", ("dp", "space")),
        P("section", ("dp", "space")),
    )
    return jax.shard_map(body, mesh=mesh, in_specs=in_specs, out_specs=out_specs, check_vma=False)
```

profile of v0, /device:TPU:0, one launch (start us, length us, event | category | flops | bytes accessed | tf_op | source)
XLA Modules:
  0.0 158.7 jit_solution(9240933483759177448)
XLA Ops:
  8.1 2.4 %collective-permute-start = (bf16[32,1,8,128]{3,0,2,1:T(8,128)(2,1)S(1)}, bf16[32,1,8,128]{3,0,2,1:T(8,128)(2,1)S(1)}, u32[]{:S(2)}, u32[]{:S(2)}) collective-permute-start(bf16[32,1,8,128]{3,0,2,1:T(8,128)(2,1)S(1)} %get-tuple-element.116), channel_id=1, source_target_pairs={{0,1},{1,2},{2,3},{4,5},{5,6},{6,7},{8,9},{9,10},{10,11},{12,13},{... | collective-permute-start | bytes 196616 | tf_op jit(solution)/shard_map/ppermute | solution.py:19
  10.5 1.3 collective-permute-start.1
  11.8 1.7 %copy.403 = bf16[1,1,32,8,2,128]{5,4,2,3,1,0:T(2,128)(2,1)} copy(bf16[1,1,32,8,2,128]{5,4,3,2,1,0:T(2,128)(2,1)} %param.12) | data formatting | bytes 262144 | tf_op args[2]
  13.5 6.1 %all-to-all-start.1 = ((bf16[32,8,2,128]{3,2,0,1:T(2,128)(2,1)}), bf16[32,8,2,128]{3,2,0,1:T(2,128)(2,1)S(1)}, u32[]{:S(2)}, u32[]{:S(2)}) async-start(bf16[32,8,2,128]{3,2,0,1:T(2,128)(2,1)} %bitcast.775), calls=%async_computation.1 | async-start | bytes 262144 | tf_op jit(solution)/shard_map/all_to_all | solution.py:137
  19.6 1.2 copy.160
  26.2 7.4 %all-reduce.7 = (f32[32]{0:T(128)S(1)}, f32[32]{0:T(128)S(1)}) all-reduce(f32[32]{0:T(128)S(1)} %get-tuple-element.21, f32[32]{0:T(128)S(1)} %get-tuple-element.20), channel_id=1, replica_groups=mesh['section'=4,'dp'=2,'space'=4] {'space'}, use_global_device_ids=true, to_apply=%region_3.4 | all-reduce | flops 64 | bytes 512 | tf_op jit(solution)/shard_map/psum | solution.py:110
  33.7 1.3 collective-permute-start.6
  35.0 1.3 collective-permute-start.7
  36.3 2.4 %collective-permute-done.7 = bf16[32,1,8,128]{3,0,2,1:T(8,128)(2,1)S(1)} collective-permute-done((bf16[32,1,8,128]{3,0,2,1:T(8,128)(2,1)S(1)}, bf16[32,1,8,128]{3,0,2,1:T(8,128)(2,1)S(1)}, u32[]{:S(2)}, u32[]{:S(2)}) %collective-permute-start.7) | collective-permute-done | bytes 65568 | tf_op jit(solution)/shard_map/ppermute | solution.py:21
  42.6 1.7 %fusion.171 = (f32[32]{0:T(128)}, f32[32]{0:T(128)}, bf16[32,2,8,128]{3,0,2,1:T(8,128)(2,1)}, f32[32,2,8,128]{3,0,2,1:T(8,128)S(1)}) fusion(f32[32]{0:T(128)S(1)} %get-tuple-element.121, f32[2,8,128,32]{2,3,1,0:T(8,128)S(1)} %get-tuple-element.122, f32[32]{0:T(128)S(1)} %get-tuple-element.120, f32[32]{0:T(128)S(1)} %bitcast.807, f32[32]{0:T(128)S(1)} %bitcast.808, ...), kind=kOutput, calls=%fused_computation.371 | convolution fusion | flops 15335360 | bytes 3303680 | tf_op jit(solution)/shard_map/koi,kidhw->odhw/dot_general | solution.py:54
  44.3 1.6 copy.136
  45.9 4.2 %all-to-all-start = ((bf16[32,2,8,128]{3,0,1,2:T(8,128)(2,1)}), bf16[32,2,8,128]{3,0,1,2:T(8,128)(2,1)S(1)}, u32[]{:S(2)}, u32[]{:S(2)}) async-start(bf16[32,2,8,128]{3,0,1,2:T(8,128)(2,1)} %copy.136), calls=%async_computation | async-start | bytes 262144 | tf_op jit(solution)/shard_map/all_to_all | solution.py:119
  50.1 4.6 %all-to-all-done = bf16[32,2,8,128]{3,0,1,2:T(8,128)(2,1)S(1)} async-done(((bf16[32,2,8,128]{3,0,1,2:T(8,128)(2,1)}), bf16[32,2,8,128]{3,0,1,2:T(8,128)(2,1)S(1)}, u32[]{:S(2)}, u32[]{:S(2)}) %all-to-all-start) | async-done | bytes 131104 | tf_op jit(solution)/shard_map/all_to_all | solution.py:119
  54.7 1.4 collective-permute-start.3
  56.1 1.3 collective-permute-start.4
  57.4 4.1 %collective-permute-start.2 = (bf16[1,1,32,2,8,128]{5,2,4,3,1,0:T(8,128)(2,1)}, bf16[1,1,32,2,8,128]{5,2,4,3,1,0:T(8,128)(2,1)}, u32[]{:S(2)}, u32[]{:S(2)}) collective-permute-start(bf16[1,1,32,2,8,128]{5,2,4,3,1,0:T(8,128)(2,1)} %bitcast.70), channel_id=1, source_target_pairs={{0,8},{8,16},{16,24},{1,9},{9,17},{17,25},{2,10},{10,18},{18,26},{... | collective-permute-start | bytes 393224 | tf_op jit(solution)/shard_map/ppermute | solution.py:31
  62.6 1.4 slice_bitcast_fusion.20
  64.0 1.0 convolution_bitcast_fusion.16
  65.9 1.0 convolution_bitcast_fusion.15
  67.5 1.0 convolution_bitcast_fusion.14
  68.9 1.0 convolution_bitcast_fusion.13
  70.4 1.0 convolution_bitcast_fusion.12
  73.2 1.0 convolution_bitcast_fusion.10
  74.7 1.0 convolution_bitcast_fusion.9
  77.0 2.9 %fusion.172 = (f32[32]{0:T(128)S(1)}, f32[32]{0:T(128)S(1)}, f32[8,2,128,32]{2,3,1,0:T(8,128)}) fusion(f32[8,2,128,32]{2,3,0,1:T(8,128)} %convolution_bitcast_fusion.9, f32[8,2,128,32]{2,3,0,1:T(8,128)} %convolution_bitcast_fusion.10, f32[8,2,128,32]{2,3,0,1:T(8,128)} %convolution_bitcast_fusion.11, f32[8,2,128,32]{2,3,0,1:T(8,128)} %convolution_bitcast_fusion.12, ...), kind=kOutput, calls=%fused_computation.372 | convolution fusion | flops 28245952 | bytes 3170560 | tf_op jit(solution)/shard_map/koi,kidhw->odhw/dot_general | solution.py:54
  80.0 8.1 %all-reduce.6 = (f32[32]{0:T(128)S(1)}, f32[32]{0:T(128)S(1)}, f32[32]{0:T(128)S(1)}, f32[32]{0:T(128)S(1)}) all-reduce(f32[32]{0:T(128)S(1)} %get-tuple-element.19, f32[32]{0:T(128)S(1)} %get-tuple-element.18, f32[32]{0:T(128)S(1)} %copy-done.26, f32[32]{0:T(128)S(1)} %copy-done.25), channel_id=1, replica_groups=mesh['section'=4,'dp'=2,'space'=4] {'space'}, use_global_device_ids=true, to_apply=%region_7.8 | all-reduce | flops 128 | bytes 1024 | tf_op jit(solution)/shard_map/psum | solution.py:124
  88.3 1.2 fusion.58
  89.5 1.1 fusion.57
  94.1 1.3 collective-permute-start.5
  97.3 1.6 %copy.204 = bf16[1,1,32,2,8,128]{5,4,3,2,1,0:T(8,128)(2,1)} copy(bf16[1,1,32,2,8,128]{5,2,4,3,1,0:T(8,128)(2,1)} %collective-permute-done.2) | data formatting | bytes 262144
  98.9 2.3 %collective-permute-done.5 = bf16[1,1,32,8,2,128]{5,2,4,3,1,0:T(8,128)(2,1)S(1)} collective-permute-done((bf16[1,1,32,8,2,128]{5,2,4,3,1,0:T(8,128)(2,1)S(1)}, bf16[1,1,32,8,2,128]{5,2,4,3,1,0:T(8,128)(2,1)S(1)}, u32[]{:S(2)}, u32[]{:S(2)}) %collective-permute-start.5) | collective-permute-done | bytes 131104 | tf_op jit(solution)/shard_map/ppermute | solution.py:31
  102.0 47.0 %all-reduce.10.cloned.1.call-done = (f32[27648]{0:T(1024)}, f32[55296]{0:T(1024)}) async-done(((f32[27648]{0:T(1024)}, f32[55296]{0:T(1024)}), (f32[27648]{0:T(1024)}, f32[55296]{0:T(1024)})) %all-reduce.10.cloned.1.call-update) | async-done | bytes 331792
  (152 shorter events, 24.4 us)
Async XLA Ops:
  8.1 12.7 %collective-permute-start = (bf16[32,1,8,128]{3,0,2,1:T(8,128)(2,1)S(1)}, bf16[32,1,8,128]{3,0,2,1:T(8,128)(2,1)S(1)}, u32[]{:S(2)}, u32[]{:S(2)}) collective-permute-start(bf16[32,1,8,128]{3,0,2,1:T(8,128)(2,1)S(1)} %get-tuple-element.116), channel_id=1, source_target_pairs={{0,1},{1,2},{2,3},{4,5},{5,6},{6,7},{8,9},{9,10},{10,11},{12,13},{... | collective-permute-start | bytes 196616 | tf_op jit(solution)/shard_map/ppermute | solution.py:19
  10.5 10.3 %collective-permute-start.1 = (bf16[32,1,8,128]{3,0,2,1:T(8,128)(2,1)S(1)}, bf16[32,1,8,128]{3,0,2,1:T(8,128)(2,1)S(1)}, u32[]{:S(2)}, u32[]{:S(2)}) collective-permute-start(bf16[32,1,8,128]{3,0,2,1:T(8,128)(2,1)S(1)} %get-tuple-element.117), channel_id=1, source_target_pairs={{1,0},{2,1},{3,2},{5,4},{6,5},{7,6},{9,8},{10,9},{11,10},{13,12},{... | collective-permute-start | bytes 196616 | tf_op jit(solution)/shard_map/ppermute | solution.py:21
  13.5 20.2 %all-to-all-start.1 = ((bf16[32,8,2,128]{3,2,0,1:T(2,128)(2,1)}), bf16[32,8,2,128]{3,2,0,1:T(2,128)(2,1)S(1)}, u32[]{:S(2)}, u32[]{:S(2)}) async-start(bf16[32,8,2,128]{3,2,0,1:T(2,128)(2,1)} %bitcast.775), calls=%async_computation.1 | async-start | bytes 262144 | tf_op jit(solution)/shard_map/all_to_all | solution.py:137
  21.7 4.0 %copy-start.4 = (bf16[1,32,2,8,128]{4,1,0,3,2:T(8,128)(2,1)}, bf16[1,32,2,8,128]{4,1,0,3,2:T(8,128)(2,1)S(1)}, u32[]{:S(2)}) copy-start(bf16[1,32,2,8,128]{4,1,0,3,2:T(8,128)(2,1)S(1)} %get-tuple-element.78) | copy-start | bytes 393220
  22.0 3.1 %copy-start.6 = (bf16[1,32,2,8,128]{4,1,3,2,0:T(8,128)(2,1)}, bf16[1,32,2,8,128]{4,1,3,2,0:T(8,128)(2,1)S(1)}, u32[]{:S(2)}) copy-start(bf16[1,32,2,8,128]{4,1,3,2,0:T(8,128)(2,1)S(1)} %get-tuple-element.98) | copy-start | bytes 393220
  22.0 3.1 %copy-start.8 = (bf16[1,32,2,8,128]{4,1,3,2,0:T(8,128)(2,1)}, bf16[1,32,2,8,128]{4,1,3,2,0:T(8,128)(2,1)S(1)}, u32[]{:S(2)}) copy-start(bf16[1,32,2,8,128]{4,1,3,2,0:T(8,128)(2,1)S(1)} %get-tuple-element.99) | copy-start | bytes 393220
  22.0 3.7 %copy-start.10 = (bf16[1,32,2,8,128]{4,1,0,3,2:T(8,128)(2,1)}, bf16[1,32,2,8,128]{4,1,0,3,2:T(8,128)(2,1)S(1)}, u32[]{:S(2)}) copy-start(bf16[1,32,2,8,128]{4,1,0,3,2:T(8,128)(2,1)S(1)} %get-tuple-element.97) | copy-start | bytes 393220
  22.0 3.7 %copy-start.12 = (bf16[1,32,2,8,128]{4,1,0,3,2:T(8,128)(2,1)}, bf16[1,32,2,8,128]{4,1,0,3,2:T(8,128)(2,1)S(1)}, u32[]{:S(2)}) copy-start(bf16[1,32,2,8,128]{4,1,0,3,2:T(8,128)(2,1)S(1)} %get-tuple-element.100) | copy-start | bytes 393220
  23.3 1.7 %copy-start.15 = (bf16[1,32,2,8,128]{4,1,3,2,0:T(8,128)(2,1)}, bf16[1,32,2,8,128]{4,1,3,2,0:T(8,128)(2,1)S(1)}, u32[]{:S(2)}) copy-start(bf16[1,32,2,8,128]{4,1,3,2,0:T(8,128)(2,1)S(1)} %get-tuple-element.112) | copy-start | bytes 393220
  33.7 2.6 %collective-permute-start.6 = (bf16[32,1,8,128]{3,0,2,1:T(8,128)(2,1)S(1)}, bf16[32,1,8,128]{3,0,2,1:T(8,128)(2,1)S(1)}, u32[]{:S(2)}, u32[]{:S(2)}) collective-permute-start(bf16[32,1,8,128]{3,0,2,1:T(8,128)(2,1)S(1)} %get-tuple-element.110), channel_id=1, source_target_pairs={{0,1},{1,2},{2,3},{4,5},{5,6},{6,7},{8,9},{9,10},{10,11},{12,13},{... | collective-permute-start | bytes 196616 | tf_op jit(solution)/shard_map/ppermute | solution.py:19
  35.0 3.8 %collective-permute-start.7 = (bf16[32,1,8,128]{3,0,2,1:T(8,128)(2,1)S(1)}, bf16[32,1,8,128]{3,0,2,1:T(8,128)(2,1)S(1)}, u32[]{:S(2)}, u32[]{:S(2)}) collective-permute-start(bf16[32,1,8,128]{3,0,2,1:T(8,128)(2,1)S(1)} %get-tuple-element.111), channel_id=1, source_target_pairs={{1,0},{2,1},{3,2},{5,4},{6,5},{7,6},{9,8},{10,9},{11,10},{13,12},{... | collective-permute-start | bytes 196616 | tf_op jit(solution)/shard_map/ppermute | solution.py:21
  42.6 7.5 %copy-start.22 = (bf16[1,1,32,8,2,128]{5,4,3,2,1,0:T(2,128)(2,1)S(1)}, bf16[1,1,32,8,2,128]{5,4,3,2,1,0:T(2,128)(2,1)}, u32[]{:S(2)}) copy-start(bf16[1,1,32,8,2,128]{5,4,3,2,1,0:T(2,128)(2,1)} %param.11) | copy-start | bytes 393220
  45.9 8.8 %all-to-all-start = ((bf16[32,2,8,128]{3,0,1,2:T(8,128)(2,1)}), bf16[32,2,8,128]{3,0,1,2:T(8,128)(2,1)S(1)}, u32[]{:S(2)}, u32[]{:S(2)}) async-start(bf16[32,2,8,128]{3,0,1,2:T(8,128)(2,1)} %copy.136), calls=%async_computation | async-start | bytes 262144 | tf_op jit(solution)/shard_map/all_to_all | solution.py:119
  50.1 98.9 %all-reduce.10.cloned.1.call-start = ((), (), s32[]{:S(2)}) async-start(), calls=%async_computation.2 | async-start | bytes 663552
  54.7 6.8 %collective-permute-start.3 = (bf16[64,8,1,128]{3,0,2,1:T(8,128)(2,1)S(1)}, bf16[64,8,1,128]{3,0,2,1:T(8,128)(2,1)S(1)}, u32[]{:S(2)}, u32[]{:S(2)}) collective-permute-start(bf16[64,8,1,128]{3,0,2,1:T(8,128)(2,1)S(1)} %get-tuple-element.106), channel_id=1, source_target_pairs={{0,1},{1,2},{2,3},{4,5},{5,6},{6,7},{8,9},{9,10},{10,11},{12,13},{... | collective-permute-start | bytes 393224 | tf_op jit(solution)/shard_map/ppermute | solution.py:19
  56.1 5.4 %collective-permute-start.4 = (bf16[64,8,1,128]{3,0,2,1:T(8,128)(2,1)S(1)}, bf16[64,8,1,128]{3,0,2,1:T(8,128)(2,1)S(1)}, u32[]{:S(2)}, u32[]{:S(2)}) collective-permute-start(bf16[64,8,1,128]{3,0,2,1:T(8,128)(2,1)S(1)} %get-tuple-element.107), channel_id=1, source_target_pairs={{1,0},{2,1},{3,2},{5,4},{6,5},{7,6},{9,8},{10,9},{11,10},{13,12},{... | collective-permute-start | bytes 393224 | tf_op jit(solution)/shard_map/ppermute | solution.py:21
  57.4 39.9 %collective-permute-start.2 = (bf16[1,1,32,2,8,128]{5,2,4,3,1,0:T(8,128)(2,1)}, bf16[1,1,32,2,8,128]{5,2,4,3,1,0:T(8,128)(2,1)}, u32[]{:S(2)}, u32[]{:S(2)}) collective-permute-start(bf16[1,1,32,2,8,128]{5,2,4,3,1,0:T(8,128)(2,1)} %bitcast.70), channel_id=1, source_target_pairs={{0,8},{8,16},{16,24},{1,9},{9,17},{17,25},{2,10},{10,18},{18,26},{... | collective-permute-start | bytes 393224 | tf_op jit(solution)/shard_map/ppermute | solution.py:31
  62.6 2.5 %copy-start.16 = (bf16[1,64,8,2,128]{4,1,0,3,2:T(8,128)(2,1)}, bf16[1,64,8,2,128]{4,1,0,3,2:T(8,128)(2,1)S(1)}, u32[]{:S(2)}) copy-start(bf16[1,64,8,2,128]{4,1,0,3,2:T(8,128)(2,1)S(1)} %get-tuple-element.50) | copy-start | bytes 786436
  62.6 2.4 %copy-start.17 = (bf16[1,64,8,2,128]{4,1,0,3,2:T(8,128)(2,1)}, bf16[1,64,8,2,128]{4,1,0,3,2:T(8,128)(2,1)S(1)}, u32[]{:S(2)}) copy-start(bf16[1,64,8,2,128]{4,1,0,3,2:T(8,128)(2,1)S(1)} %get-tuple-element.51) | copy-start | bytes 786436
  62.6 2.4 %copy-start.18 = (bf16[1,64,8,2,128]{4,1,0,3,2:T(8,128)(2,1)}, bf16[1,64,8,2,128]{4,1,0,3,2:T(8,128)(2,1)S(1)}, u32[]{:S(2)}) copy-start(bf16[1,64,8,2,128]{4,1,0,3,2:T(8,128)(2,1)S(1)} %get-tuple-element.52) | copy-start | bytes 786436
  62.6 1.4 copy-start.20
  77.0 3.0 %copy-start.25 = (f32[32]{0:T(128)S(1)}, f32[32]{0:T(128)}, u32[]{:S(2)}) copy-start(f32[32]{0:T(128)} %get-tuple-element.16) | copy-start | bytes 388
  77.0 3.0 %copy-start.26 = (f32[32]{0:T(128)S(1)}, f32[32]{0:T(128)}, u32[]{:S(2)}) copy-start(f32[32]{0:T(128)} %get-tuple-element.17) | copy-start | bytes 388
  77.0 11.3 %copy-start.5 = (bf16[1,32,2,8,128]{4,1,0,3,2:T(8,128)(2,1)S(1)}, bf16[1,32,2,8,128]{4,1,0,3,2:T(8,128)(2,1)}, u32[]{:S(2)}) copy-start(bf16[1,32,2,8,128]{4,1,0,3,2:T(8,128)(2,1)} %copy-done.4) | copy-start | bytes 393220
  77.0 11.3 %copy-start.11 = (bf16[1,32,2,8,128]{4,1,0,3,2:T(8,128)(2,1)S(1)}, bf16[1,32,2,8,128]{4,1,0,3,2:T(8,128)(2,1)}, u32[]{:S(2)}) copy-start(bf16[1,32,2,8,128]{4,1,0,3,2:T(8,128)(2,1)} %copy-done.10) | copy-start | bytes 393220
  79.9 9.6 %copy-start.7 = (bf16[1,32,2,8,128]{4,1,3,2,0:T(8,128)(2,1)S(1)}, bf16[1,32,2,8,128]{4,1,3,2,0:T(8,128)(2,1)}, u32[]{:S(2)}) copy-start(bf16[1,32,2,8,128]{4,1,3,2,0:T(8,128)(2,1)} %copy-done.6) | copy-start | bytes 393220
  79.9 9.6 %copy-start.9 = (bf16[1,32,2,8,128]{4,1,3,2,0:T(8,128)(2,1)S(1)}, bf16[1,32,2,8,128]{4,1,3,2,0:T(8,128)(2,1)}, u32[]{:S(2)}) copy-start(bf16[1,32,2,8,128]{4,1,3,2,0:T(8,128)(2,1)} %copy-done.8) | copy-start | bytes 393220
  88.3 2.4 %copy-start.1 = (bf16[1,32,2,8,128]{4,1,3,2,0:T(8,128)(2,1)S(1)}, bf16[1,32,2,8,128]{4,1,3,2,0:T(8,128)(2,1)}, u32[]{:S(2)}) copy-start(bf16[1,32,2,8,128]{4,1,3,2,0:T(8,128)(2,1)} %copy-done) | copy-start | bytes 393220
  88.3 2.4 %copy-start.3 = (bf16[1,32,2,8,128]{4,1,3,2,0:T(8,128)(2,1)S(1)}, bf16[1,32,2,8,128]{4,1,3,2,0:T(8,128)(2,1)}, u32[]{:S(2)}) copy-start(bf16[1,32,2,8,128]{4,1,3,2,0:T(8,128)(2,1)} %copy-done.2) | copy-start | bytes 393220
  92.8 1.1 copy-start.19
  92.9 2.5 %copy-start.31 = (u32[32]{0:T(128)S(1)}, u32[32]{0:T(128)}, u32[]{:S(2)}) copy-start(u32[32]{0:T(128)} %constant.38) | copy-start | bytes 388
  94.1 7.1 %collective-permute-start.5 = (bf16[1,1,32,8,2,128]{5,2,4,3,1,0:T(8,128)(2,1)S(1)}, bf16[1,1,32,8,2,128]{5,2,4,3,1,0:T(8,128)(2,1)S(1)}, u32[]{:S(2)}, u32[]{:S(2)}) collective-permute-start(bf16[1,1,32,8,2,128]{5,2,4,3,1,0:T(8,128)(2,1)S(1)} %fusion.97), channel_id=1, source_target_pairs={{8,0},{16,8},{24,16},{9,1},{17,9},{25,17},{10,2},{18,10},{26,18},{... | collective-permute-start | bytes 393224 | tf_op jit(solution)/shard_map/ppermute | solution.py:31
  (11 other events, 9.9 us)
Sparse Core Ops, SparseCore 0:
  94.0 54.8 all-reduce.9
where the time goes:
time: 160 us; the launch traced here: 159 us
  waiting for transfers between devices  56.3 us (35%)
  matrix products  25 us (16%)
  starting transfers between devices  24.7 us (15%)
  local copies, waits for them, and re-layouts  18.5 us (12%)
  between operations  16.2 us (10%)
  blocking collectives  15.6 us (10%)
  other arithmetic  2.4 us (2%)
    unnamed x2, waiting for transfers between devices  47 us
    dot_general x27, matrix products, convolve(): jnp.einsum('koi,kidhw->odhw', tap_weights, shifted, preferred_element_typ...  17.3 us
    unnamed x73, local copies, waits for them, and re-layouts  10.5 us
    psum x1, blocking collectives, body(): lax.psum((jnp.sum(dec_pre, axis=(1, 2, 3)), jnp.sum(dec_pre * dec_pre, ax...  8.14 us
    dot_general x18, matrix products, weight_terms(): jnp.einsum('odhw,kidhw->koi', cotangent, shifted, preferred_element_type=...  7.76 us
    psum x1, blocking collectives, body(): lax.psum((jnp.sum(enc_pre, axis=(1, 2, 3)), jnp.sum(enc_pre * enc_pre, ax...  7.43 us
    all_to_all x1, starting transfers between devices, body(): lax.all_to_all(cotangent, 'space', split_axis=1, concat_axis=2, tiled=True)  6.13 us
    ppermute x2, starting transfers between devices, shifted_2(): return lax.ppermute(block, axis, route)  5.43 us
  transfers between devices with their start and end apart: 11, of which 4 were waited for; matrix products, arithmetic and copies ran while one was open for 21% of the time, Pallas kernels for 0%

commit v1 on v0

v1 whole, which is shorter than its diff:
```python
import functools
import math

import jax
import jax.numpy as jnp
from jax import lax
from jax.experimental import pallas as pl
from jax.experimental.pallas import tpu as pltpu
from jax.sharding import PartitionSpec as P

EPS = 1e-05
TAPS = 3
LIMIT = 20 * 1024 * 1024
BF16 = jnp.bfloat16
F32 = jnp.float32


def vmem():
    return pl.BlockSpec(memory_space=pltpu.VMEM)


def smem():
    return pl.BlockSpec(memory_space=pltpu.SMEM)


def call(body, outs, scratch, flops, name):
    return pl.pallas_call(
        body,
        out_shape=outs,
        scratch_shapes=scratch,
        compiler_params=pltpu.CompilerParams(vmem_limit_bytes=LIMIT),
        cost_estimate=pl.CostEstimate(flops=flops, bytes_accessed=1 << 20, transcendentals=0),
        name=name,
    )


def width_shifts(rows):
    width = rows.shape[1]
    lane = lax.broadcasted_iota(jnp.int32, rows.shape, 1)
    wide = rows.astype(F32)
    left = jnp.where(lane == 0, 0.0, pltpu.roll(wide, 1, 1)).astype(BF16)
    right = jnp.where(lane == width - 1, 0.0, pltpu.roll(wide, width - 1, 1)).astype(BF16)
    return (left, rows, right)


def weights_kernel(channels, heights, strips_ref, out_ref):
    rows = channels * heights
    lanes = strips_ref.shape[-1]
    lane = lax.broadcasted_iota(jnp.int32, (channels, lanes), 1)

    @pl.loop(0, strips_ref.shape[0] * TAPS)
    def _(step):
        kind = step // TAPS
        depth_tap = step % TAPS
        for width_tap in range(TAPS):
            strip = strips_ref[kind, depth_tap, width_tap].astype(F32)
            turned = {}
            for height in range(heights):
                offset = channels * (height - 1)
                turn = offset % lanes
                if turn not in turned:
                    turned[turn] = pltpu.roll(strip, turn, 1) if turn else strip
                for tile in range(rows // lanes):
                    place = lane + (lanes * tile - offset)
                    block = jnp.where((place >= 0) & (place < TAPS * channels), turned[turn], 0.0)
                    first = pl.multiple_of(depth_tap * rows + channels * height, channels)
                    out_ref[
                        kind,
                        pl.ds(first, channels),
                        width_tap * rows + tile * lanes : width_tap * rows + (tile + 1) * lanes,
                    ] = block.astype(BF16)


def spread_depth(me, pieces, shifted_ref):
    rows = shifted_ref.shape[1] // TAPS
    depth = pieces[0].shape[0] // rows
    for distance, piece in enumerate(pieces):
        owner = me ^ distance
        for layer in range(depth):
            for tap, block in enumerate(width_shifts(piece[layer * rows : (layer + 1) * rows, :])):
                shifted_ref[owner * depth + layer, tap * rows : (tap + 1) * rows, :] = block


def spread_height(me, pieces, shifted_ref):
    depth = shifted_ref.shape[0]
    rows = shifted_ref.shape[1] // TAPS
    part = pieces[0].shape[0] // depth
    for distance, piece in enumerate(pieces):
        owner = me ^ distance

        @pl.loop(0, depth)
        def _(layer, piece=piece, owner=owner):
            cells = piece[pl.ds(pl.multiple_of(layer * part, part), part), :]
            for tap, block in enumerate(width_shifts(cells)):
                first = pl.multiple_of(tap * rows + owner * part, part)
                shifted_ref[layer, pl.ds(first, part), :] = block


def taps_product(pairs, parts_ref):
    depth = parts_ref.shape[0] - 2
    rows = parts_ref.shape[2]
    width = parts_ref.shape[3]
    for tap in range(TAPS):
        parts_ref[0, tap] = jnp.zeros((rows, width), F32)
        parts_ref[depth + 1, tap] = jnp.zeros((rows, width), F32)

    @pl.loop(0, depth // 2)
    def _(step):
        total = None
        for weights_ref, kind, shifted_ref in pairs:
            cells = jnp.concatenate([shifted_ref[2 * step], shifted_ref[2 * step + 1]], axis=1)
            product = jnp.dot(weights_ref[kind], cells, preferred_element_type=F32)
            total = product if total is None else total + product
        for tap in range(TAPS):
            block = total[tap * rows : (tap + 1) * rows]
            parts_ref[2 * step + 1, tap] = block[:, :width]
            parts_ref[2 * step + 2, tap] = block[:, width:]


def combined(parts_ref, layer):
    total = parts_ref[layer, 0]
    for tap in range(1, TAPS):
        total = total + parts_ref[layer + tap, tap]
    return total


def over_channels(sums, channels):
    total = sums[:channels]
    for first in range(channels, sums.shape[0], channels):
        total = total + sums[first : first + channels]
    return jnp.sum(total, axis=1, keepdims=True)


def tiled(values, count):
    return jnp.concatenate([values] * count, axis=0)


def normalized(parts_ref, pre_ref, sums_ref, channels):
    depth, rows, width = pre_ref.shape
    sums_ref[...] = jnp.zeros_like(sums_ref)

    @pl.loop(0, depth)
    def _(layer):
        pre = combined(parts_ref, layer)
        pre_ref[layer] = pre
        sums_ref[0] += pre
        sums_ref[1] += pre * pre

    cells = depth * (rows // channels) * width
    mean = over_channels(sums_ref[0], channels) * (1.0 / cells)
    square = over_channels(sums_ref[1], channels) * (1.0 / cells)
    return mean, lax.rsqrt(square - mean * mean + EPS)


def enc_kernel(
    channels, me_ref, p0, p1, p2, p3, weights_ref, gain_ref, bias_ref,
    shifted_ref, hat_ref, skip_ref, own_ref, scale_ref, parts_ref, pre_ref, sums_ref,
):
    me = me_ref[0]
    depth, rows, width = pre_ref.shape
    spread_depth(me, (p0, p1, p2, p3), shifted_ref)
    taps_product([(weights_ref, 0, shifted_ref)], parts_ref)
    mean, scale = normalized(parts_ref, pre_ref, sums_ref, channels)
    scale_ref[...] = jnp.broadcast_to(scale, scale_ref.shape)
    count = rows // channels
    means, scales = tiled(mean, count), tiled(scale, count)
    gains, biases = tiled(gain_ref[:, :1], count), tiled(bias_ref[:, :1], count)

    @pl.loop(0, depth)
    def _(layer):
        hat = (pre_ref[layer] - means) * scales
        hat_ref[layer] = hat
        skip_ref[layer] = jnp.maximum(gains * hat + biases, 0.0).astype(BF16)

    layers = own_ref.shape[0]
    for layer in range(layers):
        own_ref[layer] = skip_ref[me * layers + layer]


def skip_grad_kernel(me_ref, p0, p1, p2, p3, weights_ref, grad_ref, cot_ref, shifted_ref, parts_ref):
    rows = grad_ref.shape[1]
    spread_height(me_ref[0], (p0, p1, p2, p3), shifted_ref)
    taps_product([(weights_ref, 3, shifted_ref)], parts_ref)

    @pl.loop(0, grad_ref.shape[0])
    def _(layer):
        grad_ref[layer] = combined(parts_ref, layer).astype(BF16)
        cot_ref[layer] = shifted_ref[layer, rows : 2 * rows, :]


def dec_kernel(
    channels, me_ref, p0, p1, p2, p3, skip_ref, weights_ref, gain_ref, bias_ref,
    own_ref, up_ref, down_ref, parts_ref, pre_ref, sums_ref,
):
    me = me_ref[0]
    depth, rows, width = pre_ref.shape
    spread_height(me, (p0, p1, p2, p3), up_ref)

    @pl.loop(0, depth)
    def _(layer):
        for tap, block in enumerate(width_shifts(skip_ref[layer])):
            down_ref[layer, tap * rows : (tap + 1) * rows, :] = block

    taps_product([(weights_ref, 1, up_ref), (weights_ref, 2, down_ref)], parts_ref)
    mean, scale = normalized(parts_ref, pre_ref, sums_ref, channels)
    part = own_ref.shape[1]
    count = part // channels
    means, scales = tiled(mean, count), tiled(scale, count)
    gains, biases = tiled(gain_ref[:, :1], count), tiled(bias_ref[:, :1], count)

    @pl.loop(0, depth)
    def _(layer):
        pre = pre_ref[layer, pl.ds(pl.multiple_of(me * part, part), part), :]
        hat = (pre - means) * scales
        own_ref[layer] = jnp.maximum(gains * hat + biases, 0.0).astype(BF16)


def outer_sums(channels, padded_ref, shifted_refs, sums_ref):
    depth = shifted_refs[0].shape[0]
    rows = shifted_refs[0].shape[1] // TAPS
    lanes = len(shifted_refs) * TAPS * channels

    @pl.loop(0, rows // channels)
    def _(height):
        left = []
        for depth_tap in range(TAPS):
            for height_tap in range(TAPS):
                first = pl.multiple_of((height + 2 - height_tap) * channels, channels)
                left.append(
                    jnp.concatenate(
                        [
                            padded_ref[layer + 2 - depth_tap, pl.ds(first, channels), :]
                            for layer in range(depth)
                        ],
                        axis=1,
                    )
                )
        right = []
        for width_tap in range(TAPS):
            for shifted_ref in shifted_refs:
                first = pl.multiple_of(width_tap * rows + height * channels, channels)
                right.append(
                    jnp.concatenate(
                        [shifted_ref[layer, pl.ds(first, channels), :] for layer in range(depth)], axis=1
                    )
                )
        product = lax.dot_general(
            jnp.concatenate(left, axis=0),
            jnp.concatenate(right, axis=0),
            (((1,), (1,)), ((), ())),
            preferred_element_type=F32,
        )

        for tile in range(sums_ref.shape[0]):
            block = product[:, tile * 128 : min(lanes, (tile + 1) * 128)]
            old = sums_ref[tile, :, : block.shape[1]]
            sums_ref[tile, :, : block.shape[1]] = jnp.where(height == 0, 0.0, old) + block


def flattened(channels, sources, factor, sums_ref, flat_ref):
    lanes = flat_ref.shape[1]
    span = sources * channels
    merged = lanes // span
    count = channels // merged
    lane = lax.broadcasted_iota(jnp.int32, (count, lanes), 1)
    for outer in range(TAPS * TAPS):
        for width_tap in range(TAPS):
            first = width_tap * span
            tile, inner = first // lanes, first % lanes
            total = None
            for row in range(merged):
                block = sums_ref[tile, pl.ds(outer * channels + row, count, stride=merged), :]
                turn = (row * span - inner) % lanes
                block = pltpu.roll(block, turn, 1) if turn else block
                total = block if total is None else jnp.where(lane >= row * span, block, total)
            start = (outer * TAPS + width_tap) * count
            flat_ref[start : start + count, :] = total * factor


def padded_cells(channels, cells_ref, padded_ref):
    depth, rows, width = cells_ref.shape
    padded_ref[...] = jnp.zeros_like(padded_ref)

    @pl.loop(0, depth)
    def _(layer):
        padded_ref[layer + 1, channels : channels + rows, :] = cells_ref[layer]


def dec_grad_kernel(channels, factor, cot_ref, up_ref, down_ref, flat_ref, padded_ref, sums_ref):
    padded_cells(channels, cot_ref, padded_ref)
    outer_sums(channels, padded_ref, (up_ref, down_ref), sums_ref)
    flattened(channels, 2, factor, sums_ref, flat_ref)


def enc_grad_kernel(
    channels, factor, me_ref, p0, p1, p2, p3, grad_ref, hat_ref, scale_ref, gain_ref, bias_ref, shifted_ref,
    flat_ref, gated_ref, acc_ref, padded_ref, sums_ref,
):
    me = me_ref[0]
    depth, rows, width = hat_ref.shape
    count = rows // channels
    gains, biases = tiled(gain_ref[:, :1], count), tiled(bias_ref[:, :1], count)
    acc_ref[...] = jnp.zeros_like(acc_ref)
    layers = p0.shape[0] // rows
    for distance, piece in enumerate((p0, p1, p2, p3)):
        owner = me ^ distance
        for inner in range(layers):
            layer = owner * layers + inner
            hat = hat_ref[layer]
            upstream = grad_ref[layer].astype(F32) + piece[inner * rows : (inner + 1) * rows, :].astype(F32)
            gated = jnp.where(gains * hat + biases > 0, upstream, 0.0) * gains
            gated_ref[layer] = gated
            acc_ref[0] += gated
            acc_ref[1] += gated * hat
    cells = depth * count * width
    first = tiled(over_channels(acc_ref[0], channels) * (1.0 / cells), count)
    second = tiled(over_channels(acc_ref[1], channels) * (1.0 / cells), count)
    scales = tiled(scale_ref[:, :1], count)
    padded_ref[...] = jnp.zeros_like(padded_ref)

    @pl.loop(0, depth)
    def _(layer):
        grad = (gated_ref[layer] - first - hat_ref[layer] * second) * scales
        padded_ref[layer + 1, channels : channels + rows, :] = grad.astype(BF16)

    outer_sums(channels, padded_ref, (shifted_ref,), sums_ref)
    flattened(channels, 1, factor, sums_ref, flat_ref)


def gathered(piece, axis):
    count = lax.axis_size(axis)
    pieces = {0: piece}
    distance = count // 2
    while distance:
        route = [(i, i ^ distance) for i in range(count)]
        for known in list(pieces):
            pieces[known ^ distance] = lax.ppermute(pieces[known], axis, route)
        distance //= 2
    return [pieces[i] for i in range(count)]


def shifted_2(block, axis, distance):
    devices = range(lax.axis_size(axis))
    route = [(i - distance, i) for i in devices if i - distance in devices]
    return lax.ppermute(block, axis, route)


def strips(weights, channels):
    grouped = weights.reshape(TAPS, TAPS, TAPS, channels, channels).transpose(0, 2, 3, 1, 4)
    grouped = grouped.reshape(TAPS, TAPS, channels, TAPS * channels)
    return jnp.pad(grouped, ((0, 0), (0, 0), (0, 0), (0, channels)))


def summed_part(flat, name_dp, name_space):
    count, slabs = lax.axis_size(name_dp), lax.axis_size(name_space)
    parts = flat.reshape(count, slabs, -1)
    mine = lax.dynamic_index_in_dim(parts, lax.axis_index(name_space), 1, keepdims=False)
    if count != 2:
        return lax.psum_scatter(mine, name_dp, scatter_dimension=0, tiled=True)
    me = lax.axis_index(name_dp)
    kept = lax.dynamic_index_in_dim(mine, me, 0)
    sent = lax.dynamic_index_in_dim(mine, 1 - me, 0)
    return kept + lax.ppermute(sent, name_dp, [(0, 1), (1, 0)])


def body(
    enc_input, dec_input, dec_cotangent, deep_cotangent, enc_weight, dec_weight,
    enc_gain, enc_bias, dec_gain, dec_bias,
):
    _, _, channels, slab_depth, height, width = enc_input.shape
    slabs = lax.axis_size("space")
    depth = slab_depth * slabs
    slab_height = height // slabs
    rows = channels * height
    voxels = depth * height * width
    factor = 1.0 / math.sqrt(lax.axis_size("dp") * voxels)
    me = lax.axis_index("space").reshape(1).astype(jnp.int32)

    def canonical(cells):
        return cells[0, 0].transpose(1, 2, 0, 3).reshape(-1, width)

    enc_pieces = gathered(canonical(enc_input), "space")
    cot_pieces = gathered(canonical(dec_cotangent), "space")
    dec_pieces = gathered(canonical(dec_input), "space")
    deep_pieces = gathered(canonical(deep_cotangent), "space")

    flipped = jnp.swapaxes(dec_weight[0][::-1, :, channels:], 1, 2)
    all_strips = jnp.stack(
        [
            strips(enc_weight[0], channels),
            strips(dec_weight[0][:, :, :channels], channels),
            strips(dec_weight[0][:, :, channels:], channels),
            strips(flipped, channels),
        ]
    )
    shape = jax.ShapeDtypeStruct
    banded = call(
        functools.partial(weights_kernel, channels, height),
        shape((all_strips.shape[0], TAPS * rows, TAPS * rows), BF16),
        [],
        1 << 20,
        "weights",
    )(all_strips)

    def spread(values):
        return jnp.broadcast_to(values[0][:, None], (channels, 128))

    shifted_shape = (depth, TAPS * rows, width)
    cell_shape = (depth, rows, width)
    parts = pltpu.VMEM((depth + 2, TAPS, rows, width), F32)
    padded = pltpu.VMEM((depth + 2, rows + 2 * channels, width), BF16)
    conv_flops = 2 * depth * width * (TAPS * rows) ** 2
    gains, biases = spread(enc_gain), spread(enc_bias)
    enc_shifted, hat, skip, skip_own, scale = call(
        functools.partial(enc_kernel, channels),
        (
            shape(shifted_shape, BF16),
            shape(cell_shape, F32),
            shape(cell_shape, BF16),
            shape((slab_depth, rows, width), BF16),
            shape((channels, 128), F32),
        ),
        [parts, pltpu.VMEM(cell_shape, F32), pltpu.VMEM((2, rows, width), F32)],
        conv_flops,
        "enc",
    )(me, *enc_pieces, banded, gains, biases)
    enc_moved = shifted_2(skip_own, "section", 1)

    skip_grad, cot = call(
        skip_grad_kernel,
        (shape(cell_shape, BF16), shape(cell_shape, BF16)),
        [pltpu.VMEM(shifted_shape, BF16), parts],
        conv_flops,
        "skip_grad",
    )(me, *cot_pieces, banded)

    dec_own, up, down = call(
        functools.partial(dec_kernel, channels),
        (
            shape((depth, slab_height * channels, width), BF16),
            shape(shifted_shape, BF16),
            shape(shifted_shape, BF16),
        ),
        [parts, pltpu.VMEM(cell_shape, F32), pltpu.VMEM((2, rows, width), F32)],
        2 * conv_flops,
        "dec",
    )(me, *dec_pieces, skip, banded, spread(dec_gain), spread(dec_bias))
    dec_moved = shifted_2(dec_own, "section", -1)

    sums = pltpu.VMEM((2, TAPS * TAPS * channels, 128), F32)
    taps = TAPS * TAPS * TAPS
    dec_flat = call(
        functools.partial(dec_grad_kernel, channels, factor),
        shape((taps * channels * 2 * channels // 128, 128), F32),
        [padded, sums],
        conv_flops,
        "dec_grad",
    )(cot, up, down)
    dec_part = summed_part(dec_flat, "dp", "space")

    enc_flat = call(
        functools.partial(enc_grad_kernel, channels, factor),
        shape((taps * channels * channels // 128, 128), F32),
        [pltpu.VMEM(cell_shape, F32), pltpu.VMEM((2, rows, width), F32), padded, pltpu.VMEM((1, TAPS * TAPS * channels, 128), F32)],
        conv_flops,
        "enc_grad",
    )(me, *deep_pieces, skip_grad, hat, scale, gains, biases, enc_shifted)
    enc_part = summed_part(enc_flat, "dp", "space")

    enc_handoff = enc_moved.reshape(slab_depth, height, channels, width).transpose(2, 0, 1, 3)
    dec_handoff = dec_moved.reshape(depth, slab_height, channels, width).transpose(2, 0, 1, 3)
    return (enc_handoff[None, None], dec_handoff[None, None], enc_part.reshape(1, -1), dec_part.reshape(1, -1))


def solution(mesh):
    in_specs = (
        P("section", "dp", None, "space", None, None),
        P("section", "dp", None, None, "space", None),
        P("section", "dp", None, None, "space", None),
        P("section", "dp", None, "space", None, None),
        P("section", None, None, None),
        P("section", None, None, None),
        P("section", None),
        P("section", None),
        P("section", None),
        P("section", None),
    )
    out_specs = (
        P("section", "dp", None, "space", None, None),
        P("section", "dp", None, None, "space", None),
        P("section", ("dp", "space")),
        P("section", ("dp", "space")),
    )
    return jax.shard_map(body, mesh=mesh, in_specs=in_specs, out_specs=out_specs, check_vma=False)
```

time: 160 us -> 56 us (0.35)
  waiting for transfers between devices: 56.3 us -> 3.12 us
  matrix products: 25 us -> 0 us
  Pallas kernels: 0 us -> 24.7 us
  blocking collectives: 15.6 us -> 0 us
  between operations: 16.2 us -> 1 us
  starting transfers between devices: 24.7 us -> 15.9 us
  local copies, waits for them, and re-layouts: 18.5 us -> 9.75 us
    unnamed x2 -> x0, waiting for transfers between devices: 47 us -> none
    dot_general x45 -> x0, matrix products: 25 us -> none  [the longest x27 17.3 us: convolve(): jnp.einsum('koi,kidhw->odhw', tap_weights, shifted, preferred_element_typ...]
    pallas_call x0 -> x6, Pallas kernels: none -> 24.7 us  [the longest x1 7.7 us: body(): call(functools.partial(dec_kernel, channels), (shape((depth, slab_height...]
    psum x2 -> x0, blocking collectives: 15.6 us -> none  [the longest x1 8.14 us: body(): lax.psum((jnp.sum(dec_pre, axis=(1, 2, 3)), jnp.sum(dec_pre * dec_pre, ax...]
    all_to_all x2 -> x0, starting transfers between devices: 10.3 us -> none  [the longest x1 6.13 us: body(): lax.all_to_all(cotangent, 'space', split_axis=1, concat_axis=2, tiled=True)]
    unnamed x73 -> x16, local copies, waits for them, and re-layouts: 10.5 us -> 2.38 us
    all_to_all x2 -> x0, waiting for transfers between devices: 4.56 us -> none  [the longest x1 4.56 us: body(): lax.all_to_all(skip_act, 'space', split_axis=2, concat_axis=1, tiled=True)]
    another operation x6 -> x3, local copies, waits for them, and re-layouts: 3.32 us -> 0.22 us  [the longest x1 0.15 us: strips(): weights.reshape(TAPS, TAPS, TAPS, channels, channels)]
  transfers between devices with their start and end apart: 11 -> 16, of which waited for: 4 -> 2; matrix products, arithmetic and copies ran while one was open for 21% -> 12% of each run, Pallas kernels for 0% -> 25%
where the time goes in v1:
time: 56 us; the launch traced here: 55.7 us
  Pallas kernels  24.7 us (44%)
  starting transfers between devices  15.9 us (28%)
  local copies, waits for them, and re-layouts  9.75 us (17%)
  waiting for transfers between devices  3.12 us (6%)
  other arithmetic  1.31 us (2%)
  between operations  1 us (2%)
    ppermute x12, starting transfers between devices, gathered(): pieces[known ^ distance] = lax.ppermute(pieces[known], axis, route)  7.88 us
    pallas_call x1, Pallas kernels, body(): call(functools.partial(dec_kernel, channels), (shape((depth, slab_height...  7.7 us
    ppermute x2, starting transfers between devices, shifted_2(): return lax.ppermute(block, axis, route)  5.83 us
    pallas_call x1, Pallas kernels, body(): call(skip_grad_kernel, (shape(cell_shape, BF16), shape(cell_shape, BF16))...  4.78 us
    pallas_call x1, Pallas kernels, body(): call(functools.partial(enc_grad_kernel, channels, factor), shape((taps *...  4.13 us
    pallas_call x1, Pallas kernels, body(): call(functools.partial(enc_kernel, channels), (shape(shifted_shape, BF16)...  3.51 us
    pallas_call x1, Pallas kernels, body(): call(functools.partial(dec_grad_kernel, channels, factor), shape((taps *...  2.97 us
    transpose x4, local copies, waits for them, and re-layouts, canonical(): return cells[0, 0].transpose(1, 2, 0, 3).reshape(-1, width)  2.89 us
  transfers between devices with their start and end apart: 16, of which 2 were waited for; matrix products, arithmetic and copies ran while one was open for 12% of the time, Pallas kernels for 25%

profile of v1, /device:TPU:0, one launch (start us, length us, event | category | flops | bytes accessed | tf_op | source)
XLA Modules:
  0.0 55.7 jit_solution(6559841361279794761)
XLA Ops:
  0.6 1.0 %copy.33 = bf16[8,2,32,128]{3,2,1,0:T(8,128)(2,1)S(1)} copy(bf16[8,2,32,128]{3,1,0,2:T(2,128)(2,1)} %bitcast.87) | data formatting | bytes 262144 | tf_op jit(solution)/shard_map/transpose | solution.py:380
  1.6 3.1 %collective-permute-start.12 = (bf16[512,128]{1,0:T(8,128)(2,1)S(1)}, bf16[512,128]{1,0:T(8,128)(2,1)S(1)}, u32[]{:S(2)}, u32[]{:S(2)}) collective-permute-start(bf16[512,128]{1,0:T(8,128)(2,1)S(1)} %bitcast.69), channel_id=1, source_target_pairs={{0,2},{1,3},{2,0},{3,1},{4,6},{5,7},{6,4},{7,5},{8,10},{9,11},{10,... | collective-permute-start | bytes 393224 | tf_op jit(solution)/shard_map/ppermute | solution.py:337
  4.7 0.9 %copy.24 = bf16[2,8,32,128]{3,2,1,0:T(8,128)(2,1)S(1)} copy(bf16[2,8,32,128]{3,1,0,2:T(8,128)(2,1)} %bitcast.88) | data formatting | bytes 262144 | tf_op jit(solution)/shard_map/transpose | solution.py:380
  5.8 0.5 collective-permute-start
  6.3 0.9 %copy.32 = bf16[2,8,32,128]{3,2,1,0:T(8,128)(2,1)S(1)} copy(bf16[2,8,32,128]{3,1,0,2:T(8,128)(2,1)} %bitcast.89) | data formatting | bytes 262144 | tf_op jit(solution)/shard_map/transpose | solution.py:380
  7.2 1.7 %collective-permute-start.9 = (bf16[512,128]{1,0:T(8,128)(2,1)S(1)}, bf16[512,128]{1,0:T(8,128)(2,1)S(1)}, u32[]{:S(2)}, u32[]{:S(2)}) collective-permute-start(bf16[512,128]{1,0:T(8,128)(2,1)S(1)} %bitcast.72), channel_id=1, source_target_pairs={{0,2},{1,3},{2,0},{3,1},{4,6},{5,7},{6,4},{7,5},{8,10},{9,11},{10,... | collective-permute-start | bytes 393224 | tf_op jit(solution)/shard_map/ppermute | solution.py:337
  9.0 1.2 %fusion = (bf16[27,32,32]{2,1,0:T(8,128)(2,1)S(1)}, bf16[27,32,32]{2,1,0:T(8,128)(2,1)S(1)}) fusion(bf16[27,32,64]{2,1,0:T(8,128)(2,1)} %bitcast.84), kind=kLoop, calls=%fused_computation.14 | loop fusion | bytes 221184 | tf_op jit(solution)/shard_map/slice | solution.py:391
  10.3 0.2 reshape.66
  10.6 0.2 reshape.68
  10.9 0.2 copy.28
  11.1 0.2 reshape.72
  11.4 0.2 reshape.70
  11.8 2.6 %collective-permute-done.9.p2 = bf16[512,128]{1,0:T(8,128)(2,1)S(1)} collective-permute-done((bf16[512,128]{1,0:T(8,128)(2,1)S(1)}, bf16[512,128]{1,0:T(8,128)(2,1)S(1)}, u32[]{:S(2)}, u32[]{:S(2)}) %collective-permute-start.9) | collective-permute-done | bytes 131104 | tf_op jit(solution)/shard_map/ppermute | solution.py:337
  14.4 1.1 %collective-permute-start.5 = (bf16[512,128]{1,0:T(8,128)(2,1)S(1)}, bf16[512,128]{1,0:T(8,128)(2,1)S(1)}, u32[]{:S(2)}, u32[]{:S(2)}) collective-permute-start(bf16[512,128]{1,0:T(8,128)(2,1)S(1)} %bitcast.75), channel_id=1, source_target_pairs={{0,2},{1,3},{2,0},{3,1},{4,6},{5,7},{6,4},{7,5},{8,10},{9,11},{10,... | collective-permute-start | bytes 393224 | tf_op jit(solution)/shard_map/ppermute | solution.py:337
  15.6 1.6 %weights.1.weights_ref = bf16[4,768,768]{2,1,0:T(8,128)(2,1)S(1)} custom-call(bf16[4,3,3,32,128]{4,3,2,1,0:T(8,128)(2,1)S(1)} %pad_maximum_fusion.strips_ref), custom_call_target="tpu_custom_call" | custom-call | flops 1048576 | bytes 1048576 | tf_op jit(solution)/shard_map/weights/pallas_call | solution.py:397
  17.2 0.6 %collective-permute-start.8 = (bf16[512,128]{1,0:T(8,128)(2,1)S(1)}, bf16[512,128]{1,0:T(8,128)(2,1)S(1)}, u32[]{:S(2)}, u32[]{:S(2)}) collective-permute-start(bf16[512,128]{1,0:T(8,128)(2,1)S(1)} %bitcast.73), channel_id=1, source_target_pairs={{0,1},{1,0},{2,3},{3,2},{4,5},{5,4},{6,7},{7,6},{8,9},{9,8},{10,11... | collective-permute-start | bytes 393224 | tf_op jit(solution)/shard_map/ppermute | solution.py:337
  17.9 4.8 %skip_grad.1 = (bf16[8,256,128]{2,1,0:T(8,128)(2,1)S(1)}, bf16[8,256,128]{2,1,0:T(8,128)(2,1)S(1)}) custom-call(s32[1]{0:T(128)} %bitcast.me_ref, bf16[512,128]{1,0:T(8,128)(2,1)S(1)} %bitcast.71, bf16[512,128]{1,0:T(8,128)(2,1)S(1)} %collective-permute-done.11.p1, bf16[512,128]{1,0:T(8,128)(2,1)S(1)} %collective-permute-done.12.p2, ...), custom_call_target="tpu_custom_call" | custom-call | flops 1207959552 | bytes 1048576 | tf_op jit(solution)/shard_map/skip_grad/pallas_call | solution.py:429
  22.7 0.5 collective-permute-start.4
  23.4 3.5 %enc.1 = (bf16[8,768,128]{2,1,0:T(8,128)(2,1)S(1)}, f32[8,256,128]{2,1,0:T(8,128)S(1)}, bf16[8,256,128]{2,1,0:T(8,128)(2,1)S(1)}, bf16[2,256,128]{2,1,0:T(8,128)(2,1)S(1)}, f32[32,128]{1,0:T(8,128)S(1)}) custom-call(s32[1]{0:T(128)} %bitcast.me_ref, bf16[512,128]{1,0:T(8,128)(2,1)S(1)} %bitcast.68, bf16[512,128]{1,0:T(8,128)(2,1)S(1)} %collective-permute-done.p1, ...), custom_call_target="tpu_custom_call" | custom-call | flops 1207959552 | bytes 1048576 | tf_op jit(solution)/shard_map/enc/pallas_call | solution.py:414
  27.0 4.1 %enc_grad.1 = f32[216,128]{1,0:T(8,128)S(1)} custom-call(s32[1]{0:T(128)} %bitcast.me_ref, bf16[512,128]{1,0:T(8,128)(2,1)S(1)} %bitcast.74, bf16[512,128]{1,0:T(8,128)(2,1)S(1)} %collective-permute-done.8.p1, bf16[512,128]{1,0:T(8,128)(2,1)S(1)} %collective-permute-done.9.p2, bf16[512,128]{1,0:T(8,128)(2,1)S(1)} %collective-permute-done.10.p3, ...), custom_call_target="tpu_custom_call" | custom-call | flops 1207959552 | bytes 1048576 | tf_op jit(solution)/shard_map/enc_grad/pallas_call | solution.py:461
  31.3 2.3 %copy-done.1 = bf16[4,768,768]{2,1,0:T(8,128)(2,1)S(1)} copy-done((bf16[4,768,768]{2,1,0:T(8,128)(2,1)S(1)}, bf16[4,768,768]{2,1,0:T(8,128)(2,1)}, u32[]{:S(2)}) %copy-start.1) | copy-done | bytes 4718616
  33.7 7.7 %dec.1 = (bf16[8,64,128]{2,1,0:T(8,128)(2,1)S(1)}, bf16[8,768,128]{2,1,0:T(8,128)(2,1)S(1)}, bf16[8,768,128]{2,1,0:T(8,128)(2,1)S(1)}) custom-call(s32[1]{0:T(128)} %bitcast.me_ref, bf16[512,128]{1,0:T(8,128)(2,1)S(1)} %bitcast.77, bf16[512,128]{1,0:T(8,128)(2,1)S(1)} %collective-permute-done.4.p1, bf16[512,128]{1,0:T(8,128)(2,1)S(1)} %collective-permute-done.5.p2, ...), custom_call_target="tpu_custom_call" | custom-call | flops 2415919104 | bytes 1048576 | tf_op jit(solution)/shard_map/dec/pallas_call | solution.py:437
  41.4 3.0 %dec_grad.1 = f32[432,128]{1,0:T(8,128)S(1)} custom-call(bf16[8,256,128]{2,1,0:T(8,128)(2,1)S(1)} %get-tuple-element.21.cot_ref, bf16[8,768,128]{2,1,0:T(8,128)(2,1)S(1)} %get-tuple-element.22.up_ref, bf16[8,768,128]{2,1,0:T(8,128)(2,1)S(1)} %get-tuple-element.23.down_ref), custom_call_target="tpu_custom_call" | custom-call | flops 1207959552 | bytes 1048576 | tf_op jit(solution)/shard_map/dec_grad/pallas_call | solution.py:452
  44.5 1.6 %collective-permute-start.14 = (f32[1,3456]{1,0:T(1,128)S(1)}, f32[1,3456]{1,0:T(1,128)S(1)}, u32[]{:S(2)}, u32[]{:S(2)}) collective-permute-start(f32[1,3456]{1,0:T(1,128)S(1)} %dynamic-slice_bitcast_fusion.1), channel_id=1, source_target_pairs={{0,4},{4,0},{1,5},{5,1},{2,6},{6,2},{3,7},{7,3},{8,12},{12,8},{9,1... | collective-permute-start | bytes 41480 | tf_op jit(solution)/shard_map/ppermute | solution.py:363
  46.1 0.6 %collective-permute-start.15 = (f32[1,6912]{1,0:T(1,128)S(1)}, f32[1,6912]{1,0:T(1,128)S(1)}, u32[]{:S(2)}, u32[]{:S(2)}) collective-permute-start(f32[1,6912]{1,0:T(1,128)S(1)} %dynamic-slice_bitcast_fusion), channel_id=1, source_target_pairs={{0,4},{4,0},{1,5},{5,1},{2,6},{6,2},{3,7},{7,3},{8,12},{12,8},{9,1... | collective-permute-start | bytes 82952 | tf_op jit(solution)/shard_map/ppermute | solution.py:363
  46.7 1.3 %collective-permute-start.7 = (bf16[8,64,128]{2,1,0:T(8,128)(2,1)S(1)}, bf16[8,64,128]{2,1,0:T(8,128)(2,1)S(1)}, u32[]{:S(2)}, u32[]{:S(2)}) collective-permute-start(bf16[8,64,128]{2,1,0:T(8,128)(2,1)S(1)} %get-tuple-element.16), channel_id=1, source_target_pairs={{8,0},{16,8},{24,16},{9,1},{17,9},{25,17},{10,2},{18,10},{26,18},{... | collective-permute-start | bytes 393224 | tf_op jit(solution)/shard_map/ppermute | solution.py:345
  47.9 4.6 %collective-permute-start.3 = (bf16[2,256,128]{2,1,0:T(8,128)(2,1)S(1)}, bf16[2,256,128]{2,1,0:T(8,128)(2,1)S(1)}, u32[]{:S(2)}, u32[]{:S(2)}) collective-permute-start(bf16[2,256,128]{2,1,0:T(8,128)(2,1)S(1)} %get-tuple-element.14), channel_id=1, source_target_pairs={{0,8},{8,16},{16,24},{1,9},{9,17},{17,25},{2,10},{10,18},{18,26},{... | collective-permute-start | bytes 393224 | tf_op jit(solution)/shard_map/ppermute | solution.py:345
  52.5 0.6 %bitcast_add_fusion.1 = f32[1,3456]{1,0:T(1,128)} fusion(f32[1,3456]{1,0:T(1,128)S(1)} %collective-permute-done.14, f32[2,4,3456]{2,1,0:T(4,128)S(1)} %reshape.78, s32[]{:T(128)S(6)} %select_n.23, s32[]{:T(128)S(6)} %select_n.25), kind=kLoop, calls=%fused_computation.12 | loop fusion | flops 3456 | bytes 41480 | tf_op jit(solution)/shard_map/add | solution.py:363
  53.1 0.6 %bitcast_add_fusion = f32[1,6912]{1,0:T(1,128)} fusion(f32[1,6912]{1,0:T(1,128)S(1)} %collective-permute-done.15, f32[2,4,6912]{2,1,0:T(4,128)S(1)} %reshape.79, s32[]{:T(128)S(6)} %select_n.23, s32[]{:T(128)S(6)} %select_n.25), kind=kLoop, calls=%fused_computation.10 | loop fusion | flops 6912 | bytes 82952 | tf_op jit(solution)/shard_map/add | solution.py:363
  53.8 0.8 %copy.42 = bf16[8,2,32,128]{3,1,0,2:T(2,128)(2,1)} copy(bf16[8,2,32,128]{3,2,1,0:T(8,128)(2,1)S(1)} %bitcast.92) | data formatting | bytes 262144 | tf_op jit(solution)/shard_map/reshape | solution.py:471
  54.6 0.4 collective-permute-done.3
  55.0 0.7 %copy.43 = bf16[2,8,32,128]{3,1,0,2:T(8,128)(2,1)} copy(bf16[2,8,32,128]{3,2,1,0:T(8,128)(2,1)S(1)} %bitcast.91) | data formatting | bytes 262144 | tf_op jit(solution)/shard_map/reshape | solution.py:470
  (51 shorter events, 1.6 us)
Async XLA Ops:
  0.6 9.5 %copy-start.2 = (bf16[1,27,32,32]{3,2,1,0:T(8,128)(2,1)S(1)}, bf16[1,27,32,32]{3,2,1,0:T(8,128)(2,1)}, u32[]{:S(2)}) copy-start(bf16[1,27,32,32]{3,2,1,0:T(8,128)(2,1)} %param.14) | copy-start | bytes 165892
  1.6 10.0 %collective-permute-start.12 = (bf16[512,128]{1,0:T(8,128)(2,1)S(1)}, bf16[512,128]{1,0:T(8,128)(2,1)S(1)}, u32[]{:S(2)}, u32[]{:S(2)}) collective-permute-start(bf16[512,128]{1,0:T(8,128)(2,1)S(1)} %bitcast.69), channel_id=1, source_target_pairs={{0,2},{1,3},{2,0},{3,1},{4,6},{5,7},{6,4},{7,5},{8,10},{9,11},{10,... | collective-permute-start | bytes 393224 | tf_op jit(solution)/shard_map/ppermute | solution.py:337
  4.7 12.5 %collective-permute-start.11 = (bf16[512,128]{1,0:T(8,128)(2,1)S(1)}, bf16[512,128]{1,0:T(8,128)(2,1)S(1)}, u32[]{:S(2)}, u32[]{:S(2)}) collective-permute-start(bf16[512,128]{1,0:T(8,128)(2,1)S(1)} %bitcast.70), channel_id=1, source_target_pairs={{0,1},{1,0},{2,3},{3,2},{4,5},{5,4},{6,7},{7,6},{8,9},{9,8},{10,11... | collective-permute-start | bytes 393224 | tf_op jit(solution)/shard_map/ppermute | solution.py:337
  5.6 9.9 %collective-permute-start.1 = (bf16[512,128]{1,0:T(8,128)(2,1)S(1)}, bf16[512,128]{1,0:T(8,128)(2,1)S(1)}, u32[]{:S(2)}, u32[]{:S(2)}) collective-permute-start(bf16[512,128]{1,0:T(8,128)(2,1)S(1)} %bitcast.66), channel_id=1, source_target_pairs={{0,2},{1,3},{2,0},{3,1},{4,6},{5,7},{6,4},{7,5},{8,10},{9,11},{10,... | collective-permute-start | bytes 393224 | tf_op jit(solution)/shard_map/ppermute | solution.py:337
  5.8 17.4 %collective-permute-start = (bf16[512,128]{1,0:T(8,128)(2,1)S(1)}, bf16[512,128]{1,0:T(8,128)(2,1)S(1)}, u32[]{:S(2)}, u32[]{:S(2)}) collective-permute-start(bf16[512,128]{1,0:T(8,128)(2,1)S(1)} %bitcast.67), channel_id=1, source_target_pairs={{0,1},{1,0},{2,3},{3,2},{4,5},{5,4},{6,7},{7,6},{8,9},{9,8},{10,11... | collective-permute-start | bytes 393224 | tf_op jit(solution)/shard_map/ppermute | solution.py:337
  7.2 7.2 %collective-permute-start.9 = (bf16[512,128]{1,0:T(8,128)(2,1)S(1)}, bf16[512,128]{1,0:T(8,128)(2,1)S(1)}, u32[]{:S(2)}, u32[]{:S(2)}) collective-permute-start(bf16[512,128]{1,0:T(8,128)(2,1)S(1)} %bitcast.72), channel_id=1, source_target_pairs={{0,2},{1,3},{2,0},{3,1},{4,6},{5,7},{6,4},{7,5},{8,10},{9,11},{10,... | collective-permute-start | bytes 393224 | tf_op jit(solution)/shard_map/ppermute | solution.py:337
  10.6 1.1 %copy-start.3 = (bf16[1,1,32,8,2,128]{5,4,3,2,1,0:T(2,128)(2,1)S(1)}, bf16[1,1,32,8,2,128]{5,4,3,2,1,0:T(2,128)(2,1)}, u32[]{:S(2)}) copy-start(bf16[1,1,32,8,2,128]{5,4,3,2,1,0:T(2,128)(2,1)} %param.11) | copy-start | bytes 393220
  11.6 6.2 %collective-permute-start.13 = (bf16[512,128]{1,0:T(8,128)(2,1)S(1)}, bf16[512,128]{1,0:T(8,128)(2,1)S(1)}, u32[]{:S(2)}, u32[]{:S(2)}) collective-permute-start(bf16[512,128]{1,0:T(8,128)(2,1)S(1)} %collective-permute-done.12.p2), channel_id=1, source_target_pairs={{0,1},{1,0},{2,3},{3,2},{4,5},{5,4},{6,7},{7,6},{8,9},{9,8},{10,11... | collective-permute-start | bytes 393224 | tf_op jit(solution)/shard_map/ppermute | solution.py:337
  14.4 8.2 %collective-permute-start.5 = (bf16[512,128]{1,0:T(8,128)(2,1)S(1)}, bf16[512,128]{1,0:T(8,128)(2,1)S(1)}, u32[]{:S(2)}, u32[]{:S(2)}) collective-permute-start(bf16[512,128]{1,0:T(8,128)(2,1)S(1)} %bitcast.75), channel_id=1, source_target_pairs={{0,2},{1,3},{2,0},{3,1},{4,6},{5,7},{6,4},{7,5},{8,10},{9,11},{10,... | collective-permute-start | bytes 393224 | tf_op jit(solution)/shard_map/ppermute | solution.py:337
  15.5 7.7 %collective-permute-start.2 = (bf16[512,128]{1,0:T(8,128)(2,1)S(1)}, bf16[512,128]{1,0:T(8,128)(2,1)S(1)}, u32[]{:S(2)}, u32[]{:S(2)}) collective-permute-start(bf16[512,128]{1,0:T(8,128)(2,1)S(1)} %collective-permute-done.1.p2), channel_id=1, source_target_pairs={{0,1},{1,0},{2,3},{3,2},{4,5},{5,4},{6,7},{7,6},{8,9},{9,8},{10,11... | collective-permute-start | bytes 393224 | tf_op jit(solution)/shard_map/ppermute | solution.py:337
  17.2 6.2 %copy-start = (bf16[4,768,768]{2,1,0:T(8,128)(2,1)}, bf16[4,768,768]{2,1,0:T(8,128)(2,1)S(1)}, u32[]{:S(2)}) copy-start(bf16[4,768,768]{2,1,0:T(8,128)(2,1)S(1)} %weights.1.weights_ref) | copy-start | bytes 14155780
  17.2 9.7 %collective-permute-start.8 = (bf16[512,128]{1,0:T(8,128)(2,1)S(1)}, bf16[512,128]{1,0:T(8,128)(2,1)S(1)}, u32[]{:S(2)}, u32[]{:S(2)}) collective-permute-start(bf16[512,128]{1,0:T(8,128)(2,1)S(1)} %bitcast.73), channel_id=1, source_target_pairs={{0,1},{1,0},{2,3},{3,2},{4,5},{5,4},{6,7},{7,6},{8,9},{9,8},{10,11... | collective-permute-start | bytes 393224 | tf_op jit(solution)/shard_map/ppermute | solution.py:337
  17.8 9.2 %collective-permute-start.10 = (bf16[512,128]{1,0:T(8,128)(2,1)S(1)}, bf16[512,128]{1,0:T(8,128)(2,1)S(1)}, u32[]{:S(2)}, u32[]{:S(2)}) collective-permute-start(bf16[512,128]{1,0:T(8,128)(2,1)S(1)} %collective-permute-done.9.p2), channel_id=1, source_target_pairs={{0,1},{1,0},{2,3},{3,2},{4,5},{5,4},{6,7},{7,6},{8,9},{9,8},{10,11... | collective-permute-start | bytes 393224 | tf_op jit(solution)/shard_map/ppermute | solution.py:337
  17.9 5.4 %copy-start.4 = (f32[1,32]{1,0:T(1,128)S(1)}, f32[1,32]{1,0:T(1,128)}, u32[]{:S(2)}) copy-start(f32[1,32]{1,0:T(1,128)} %param.16) | copy-start | bytes 388
  17.9 5.5 %copy-start.5 = (f32[1,32]{1,0:T(1,128)S(1)}, f32[1,32]{1,0:T(1,128)}, u32[]{:S(2)}) copy-start(f32[1,32]{1,0:T(1,128)} %param.17) | copy-start | bytes 388
  22.7 8.5 %collective-permute-start.4 = (bf16[512,128]{1,0:T(8,128)(2,1)S(1)}, bf16[512,128]{1,0:T(8,128)(2,1)S(1)}, u32[]{:S(2)}, u32[]{:S(2)}) collective-permute-start(bf16[512,128]{1,0:T(8,128)(2,1)S(1)} %bitcast.76), channel_id=1, source_target_pairs={{0,1},{1,0},{2,3},{3,2},{4,5},{5,4},{6,7},{7,6},{8,9},{9,8},{10,11... | collective-permute-start | bytes 393224 | tf_op jit(solution)/shard_map/ppermute | solution.py:337
  23.1 8.0 %collective-permute-start.6 = (bf16[512,128]{1,0:T(8,128)(2,1)S(1)}, bf16[512,128]{1,0:T(8,128)(2,1)S(1)}, u32[]{:S(2)}, u32[]{:S(2)}) collective-permute-start(bf16[512,128]{1,0:T(8,128)(2,1)S(1)} %collective-permute-done.5.p2), channel_id=1, source_target_pairs={{0,1},{1,0},{2,3},{3,2},{4,5},{5,4},{6,7},{7,6},{8,9},{9,8},{10,11... | collective-permute-start | bytes 393224 | tf_op jit(solution)/shard_map/ppermute | solution.py:337
  26.9 4.2 %copy-start.6 = (f32[1,32]{1,0:T(1,128)S(1)}, f32[1,32]{1,0:T(1,128)}, u32[]{:S(2)}) copy-start(f32[1,32]{1,0:T(1,128)} %param.18) | copy-start | bytes 388
  26.9 4.3 %copy-start.7 = (f32[1,32]{1,0:T(1,128)S(1)}, f32[1,32]{1,0:T(1,128)}, u32[]{:S(2)}) copy-start(f32[1,32]{1,0:T(1,128)} %param.19) | copy-start | bytes 388
  31.3 2.3 %copy-start.1 = (bf16[4,768,768]{2,1,0:T(8,128)(2,1)S(1)}, bf16[4,768,768]{2,1,0:T(8,128)(2,1)}, u32[]{:S(2)}) copy-start(bf16[4,768,768]{2,1,0:T(8,128)(2,1)} %copy-done) | copy-start | bytes 14155780
  44.5 8.0 %collective-permute-start.14 = (f32[1,3456]{1,0:T(1,128)S(1)}, f32[1,3456]{1,0:T(1,128)S(1)}, u32[]{:S(2)}, u32[]{:S(2)}) collective-permute-start(f32[1,3456]{1,0:T(1,128)S(1)} %dynamic-slice_bitcast_fusion.1), channel_id=1, source_target_pairs={{0,4},{4,0},{1,5},{5,1},{2,6},{6,2},{3,7},{7,3},{8,12},{12,8},{9,1... | collective-permute-start | bytes 41480 | tf_op jit(solution)/shard_map/ppermute | solution.py:363
  46.1 7.1 %collective-permute-start.15 = (f32[1,6912]{1,0:T(1,128)S(1)}, f32[1,6912]{1,0:T(1,128)S(1)}, u32[]{:S(2)}, u32[]{:S(2)}) collective-permute-start(f32[1,6912]{1,0:T(1,128)S(1)} %dynamic-slice_bitcast_fusion), channel_id=1, source_target_pairs={{0,4},{4,0},{1,5},{5,1},{2,6},{6,2},{3,7},{7,3},{8,12},{12,8},{9,1... | collective-permute-start | bytes 82952 | tf_op jit(solution)/shard_map/ppermute | solution.py:363
  46.7 7.1 %collective-permute-start.7 = (bf16[8,64,128]{2,1,0:T(8,128)(2,1)S(1)}, bf16[8,64,128]{2,1,0:T(8,128)(2,1)S(1)}, u32[]{:S(2)}, u32[]{:S(2)}) collective-permute-start(bf16[8,64,128]{2,1,0:T(8,128)(2,1)S(1)} %get-tuple-element.16), channel_id=1, source_target_pairs={{8,0},{16,8},{24,16},{9,1},{17,9},{25,17},{10,2},{18,10},{26,18},{... | collective-permute-start | bytes 393224 | tf_op jit(solution)/shard_map/ppermute | solution.py:345
  47.9 7.1 %collective-permute-start.3 = (bf16[2,256,128]{2,1,0:T(8,128)(2,1)S(1)}, bf16[2,256,128]{2,1,0:T(8,128)(2,1)S(1)}, u32[]{:S(2)}, u32[]{:S(2)}) collective-permute-start(bf16[2,256,128]{2,1,0:T(8,128)(2,1)S(1)} %get-tuple-element.14), channel_id=1, source_target_pairs={{0,8},{8,16},{16,24},{1,9},{9,17},{17,25},{2,10},{10,18},{18,26},{... | collective-permute-start | bytes 393224 | tf_op jit(solution)/shard_map/ppermute | solution.py:345

commit v2 on v1

v2 whole, which is shorter than its diff:
```python
import functools
import math

import jax
import jax.numpy as jnp
from jax import lax
from jax.experimental import pallas as pl
from jax.experimental.pallas import tpu as pltpu
from jax.sharding import PartitionSpec as P


EPS = 1e-05
TAPS = 3
PAIR = 2
LIMIT = 12 * 1024 * 1024
BF16 = jnp.bfloat16
F32 = jnp.float32


def call(body, outs, scratch, after=0, in_specs=None, out_specs=None):
    count = len(outs) if isinstance(outs, tuple) else 1

    def kernel(*refs):
        inputs = len(refs) - count - len(scratch)
        body(*refs[: inputs - after], *refs[inputs:])

    specs = {} if in_specs is None else {"in_specs": in_specs}
    specs |= {} if out_specs is None else {"out_specs": out_specs}
    return pl.pallas_call(
        kernel,
        out_shape=outs,
        scratch_shapes=scratch,
        compiler_params=pltpu.CompilerParams(vmem_limit_bytes=LIMIT),
        cost_estimate=pl.CostEstimate(flops=1 << 12, bytes_accessed=1 << 10, transcendentals=0),
        **specs,
    )


def width_shifts(rows):
    width = rows.shape[1]
    lane = lax.broadcasted_iota(jnp.int32, rows.shape, 1)
    none = jnp.zeros_like(rows)
    left = jnp.where(lane == 0, none, pltpu.roll(rows, 1, 1))
    right = jnp.where(lane == width - 1, none, pltpu.roll(rows, width - 1, 1))
    return (left, rows, right)


def row_turn(size, outer, inner):
    shift = inner.bit_length() - 1
    assert 1 << shift == inner and outer * inner == size
    row = lax.broadcasted_iota(jnp.int32, (size, size), 0)
    source = (row & (inner - 1)) * outer + (row >> shift)
    return jnp.where(lax.broadcasted_iota(jnp.int32, (size, size), 1) == source, 1.0, 0.0).astype(BF16)


def prepare_kernel(
    enc_hbm, dec_hbm, g0, g1, g2, g3, own_hbm, cot_hbm, dec_in_hbm, deep_hbm,
    enc_out, flip_out, up_out, down_out, turn_out, back_out, columns_out, own_out, mine_out,
    enc_ref, dec_ref, row0, row1, row2, row3, sems, enc_wide, dec_wide,
):
    size = own_hbm.shape[0]
    rows_of = (row0, row1, row2, row3)
    copies = [
        pltpu.make_async_copy(source, target, sems.at[at])
        for at, (source, target) in enumerate(
            (
                (enc_hbm, enc_ref), (dec_hbm, dec_ref), *zip((g0, g1, g2, g3), rows_of, strict=True),
                (own_hbm, own_out), (cot_hbm, mine_out.at[:size]), (dec_in_hbm, mine_out.at[size : 2 * size]),
                (deep_hbm, mine_out.at[2 * size :]),
            )
        )
    ]
    for copy in copies:
        copy.start()
    channels = enc_ref.shape[1]
    rows = enc_out.shape[0] // TAPS
    lanes = enc_wide.shape[-1]
    lane = lax.broadcasted_iota(jnp.int32, (channels, lanes), 1)
    turn_out[...] = row_turn(turn_out.shape[0], turn_out.shape[0] // channels, channels)
    back_out[...] = row_turn(back_out.shape[0], channels, back_out.shape[0] // channels)
    for copy in copies[:2]:
        copy.wait()
    for wide, source in ((enc_wide, enc_ref), (dec_wide, dec_ref)):
        wide[...] = jnp.zeros_like(wide)
        for tap in range(source.shape[0]):
            wide[tap, :, : source.shape[2]] = source[tap].astype(F32)

    def strip(blocks):
        total = blocks[0]
        for place, block in enumerate(blocks[1:], 1):
            total = total + pltpu.roll(block, place * channels, 1)
        return total

    def first_half(block):
        return jnp.where(lane < channels, block, 0.0)

    def second_half(block):
        return first_half(pltpu.roll(block, lanes - channels, 1))

    def turned(blocks):
        stacked = jnp.concatenate(blocks + [jnp.zeros_like(blocks[0])] * (lanes // channels - TAPS), axis=0)
        return stacked.T[:channels]

    @pl.loop(0, TAPS)
    def _(depth_tap):
        first = pl.multiple_of(depth_tap * rows, rows)
        for width_tap in range(TAPS):
            taps = [TAPS * TAPS * depth_tap + TAPS * b + width_tap for b in range(TAPS)]
            last = dec_wide.shape[0] - 1
            found = (
                (enc_out, strip([enc_wide[tap] for tap in taps])),
                (up_out, strip([first_half(dec_wide[tap]) for tap in taps])),
                (down_out, strip([second_half(dec_wide[tap]) for tap in taps])),
                (flip_out, turned([second_half(dec_wide[last - tap]) for tap in taps])),
            )
            for out_ref, block in found:
                rolled = {}
                for height in range(rows // channels):
                    offset = channels * (height - 1)
                    turn = offset % lanes
                    if turn not in rolled:
                        rolled[turn] = pltpu.roll(block, turn, 1) if turn else block
                    for tile in range(rows // lanes):
                        place = lane + (lanes * tile - offset)
                        inside = (place >= 0) & (place < TAPS * channels)
                        out_ref[
                            pl.ds(first + height * channels, channels),
                            width_tap * rows + tile * lanes : width_tap * rows + (tile + 1) * lanes,
                        ] = jnp.where(inside, rolled[turn], 0.0).astype(BF16)

    for copy in copies[2:]:
        copy.wait()
    for place, row in enumerate(rows_of):
        columns_out[place] = jnp.broadcast_to(column(row), columns_out.shape[1:])


def column(row_ref):
    count = row_ref.shape[1]
    wide = jnp.broadcast_to(row_ref[...], (count, count))
    here = lax.broadcasted_iota(jnp.int32, (count, count), 0) == lax.broadcasted_iota(
        jnp.int32, (count, count), 1
    )
    return jnp.sum(jnp.where(here, wide, 0.0), axis=1, keepdims=True)


def turned_rows(pieces, turn_ref, turned_ref):
    side_by_side = jnp.concatenate([piece[...] for piece in pieces], axis=1)
    turned_ref[...] = jnp.dot(turn_ref[...], side_by_side, preferred_element_type=F32).astype(BF16)


def spread_depth(me, pieces, turn_ref, turned_ref, shifted_ref):
    rows = shifted_ref.shape[1] // TAPS
    width = shifted_ref.shape[2]
    depth = pieces[0].shape[0] // rows
    turned_rows(pieces, turn_ref, turned_ref)
    for distance in range(len(pieces)):
        owner = me ^ distance
        for layer in range(depth):
            cells = turned_ref[layer * rows : (layer + 1) * rows, distance * width : (distance + 1) * width]
            for tap, block in enumerate(width_shifts(cells)):
                shifted_ref[owner * depth + layer, tap * rows : (tap + 1) * rows, :] = block


def spread_height(me, pieces, turn_ref, turned_ref, shifted_ref):
    depth, rows, width = shifted_ref.shape
    rows = rows // TAPS
    part = pieces[0].shape[0] // depth
    turned_rows(pieces, turn_ref, turned_ref)
    for distance in range(len(pieces)):
        owner = me ^ distance
        for layer in range(depth):
            cells = turned_ref[layer * part : (layer + 1) * part, distance * width : (distance + 1) * width]
            for tap, block in enumerate(width_shifts(cells)):
                first = pl.multiple_of(tap * rows + owner * part, part)
                shifted_ref[layer, pl.ds(first, part), :] = block


def taps_product(pairs, parts_ref):
    depth = parts_ref.shape[0] - 2
    rows = parts_ref.shape[2]
    width = parts_ref.shape[3]
    for tap in range(TAPS):
        parts_ref[0, tap] = jnp.zeros((rows, width), F32)
        parts_ref[depth + 1, tap] = jnp.zeros((rows, width), F32)

    @pl.loop(0, depth // 2)
    def _(step):
        total = None
        for weights_ref, shifted_ref in pairs:
            cells = jnp.concatenate([shifted_ref[2 * step], shifted_ref[2 * step + 1]], axis=1)
            product = jnp.dot(weights_ref[...], cells, preferred_element_type=F32)
            total = product if total is None else total + product
        for tap in range(TAPS):
            block = total[tap * rows : (tap + 1) * rows]
            parts_ref[2 * step + 1, tap] = block[:, :width]
            parts_ref[2 * step + 2, tap] = block[:, width:]


def combined(parts_ref, layer):
    total = parts_ref[layer, 0]
    for tap in range(1, TAPS):
        total = total + parts_ref[layer + tap, tap]
    return total


def over_channels(sums, channels):
    total = sums[:channels]
    for first in range(channels, sums.shape[0], channels):
        total = total + sums[first : first + channels]
    return jnp.sum(total, axis=1, keepdims=True)


def tiled(values, count):
    return jnp.concatenate([values] * count, axis=0)


def normalized(parts_ref, pre_ref, sums_ref, channels):
    depth, rows, width = pre_ref.shape
    sums_ref[...] = jnp.zeros_like(sums_ref)

    @pl.loop(0, depth)
    def _(layer):
        pre = combined(parts_ref, layer)
        pre_ref[layer] = pre
        sums_ref[0] += pre
        sums_ref[1] += pre * pre

    cells = depth * (rows // channels) * width
    mean = over_channels(sums_ref[0], channels) * (1.0 / cells)
    square = over_channels(sums_ref[1], channels) * (1.0 / cells)
    return mean, lax.rsqrt(square - mean * mean + EPS)


def enc_kernel(
    channels, me_ref, p0, p1, p2, p3, weights_ref, turn_ref, back_ref, columns_ref,
    shifted_ref, hat_ref, skip_ref, own_ref, scale_ref, turned_ref, parts_ref, pre_ref, sums_ref,
):
    me = me_ref[0]
    depth, rows, _ = pre_ref.shape
    spread_depth(me, (p0, p1, p2, p3), turn_ref, turned_ref, shifted_ref)
    taps_product([(weights_ref, shifted_ref)], parts_ref)
    mean, scale = normalized(parts_ref, pre_ref, sums_ref, channels)
    scale_ref[...] = jnp.broadcast_to(scale, scale_ref.shape)
    count = rows // channels
    means, scales = tiled(mean, count), tiled(scale, count)
    gains, biases = tiled(columns_ref[0, :, :1], count), tiled(columns_ref[1, :, :1], count)

    @pl.loop(0, depth)
    def _(layer):
        hat = (pre_ref[layer] - means) * scales
        hat_ref[layer] = hat
        skip_ref[layer] = jnp.maximum(gains * hat + biases, 0.0).astype(BF16)

    layers = own_ref.shape[0] // rows
    own = jnp.concatenate([skip_ref[me * layers + layer] for layer in range(layers)], axis=0)
    own_ref[...] = jnp.dot(back_ref[...], own, preferred_element_type=F32).astype(BF16)


def piece_views(refs, size, places):
    return [ref.at[place * size : (place + 1) * size] for ref, place in zip(refs, places, strict=True)]


def skip_grad_kernel(
    size, me_ref, p0, p1, p2, p3, weights_ref, turn_ref, grad_ref, cot_ref, shifted_ref, turned_ref, parts_ref
):
    rows = grad_ref.shape[1]
    spread_height(me_ref[0], piece_views((p0, p1, p2, p3), size, (0, 0, 0, 0)), turn_ref, turned_ref, shifted_ref)
    taps_product([(weights_ref, shifted_ref)], parts_ref)

    @pl.loop(0, grad_ref.shape[0])
    def _(layer):
        grad_ref[layer] = combined(parts_ref, layer).astype(BF16)
        cot_ref[layer] = shifted_ref[layer, rows : 2 * rows, :]


def dec_kernel(
    channels, size, me_ref, p0, p1, p2, p3, skip_ref, up_weights_ref, down_weights_ref, turn_ref, back_ref,
    columns_ref, own_ref, up_ref, down_ref, turned_ref, parts_ref, pre_ref, sums_ref,
):
    me = me_ref[0]
    depth, rows, _ = pre_ref.shape
    spread_height(me, piece_views((p0, p1, p2, p3), size, (1, 1, 0, 0)), turn_ref, turned_ref, up_ref)

    for layer in range(depth):
        for tap, block in enumerate(width_shifts(skip_ref[layer])):
            down_ref[layer, tap * rows : (tap + 1) * rows, :] = block

    taps_product([(up_weights_ref, up_ref), (down_weights_ref, down_ref)], parts_ref)
    mean, scale = normalized(parts_ref, pre_ref, sums_ref, channels)
    part = own_ref.shape[0] // depth
    count = part // channels
    means, scales = tiled(mean, count), tiled(scale, count)
    gains, biases = tiled(columns_ref[2, :, :1], count), tiled(columns_ref[3, :, :1], count)

    own = []
    for layer in range(depth):
        pre = pre_ref[layer, pl.ds(pl.multiple_of(me * part, part), part), :]
        hat = (pre - means) * scales
        own.append(jnp.maximum(gains * hat + biases, 0.0).astype(BF16))
    own = jnp.concatenate(own, axis=0)
    own_ref[...] = jnp.dot(back_ref[...], own, preferred_element_type=F32).astype(BF16)


def outer_sums(channels, outers, padded_ref, shifted_refs, sums_ref):
    depth = shifted_refs[0].shape[0]
    rows = shifted_refs[0].shape[1] // TAPS
    lanes = len(shifted_refs) * TAPS * channels

    @pl.loop(0, rows // channels)
    def _(height):
        left = []
        for depth_tap, height_tap in outers:
            first = pl.multiple_of((height + 2 - height_tap) * channels, channels)
            left.append(
                jnp.concatenate(
                    [padded_ref[layer + 2 - depth_tap, pl.ds(first, channels), :] for layer in range(depth)],
                    axis=1,
                )
            )
        right = []
        for width_tap in range(TAPS):
            for shifted_ref in shifted_refs:
                first = pl.multiple_of(width_tap * rows + height * channels, channels)
                right.append(
                    jnp.concatenate(
                        [shifted_ref[layer, pl.ds(first, channels), :] for layer in range(depth)], axis=1
                    )
                )
        product = lax.dot_general(
            jnp.concatenate(left, axis=0),
            jnp.concatenate(right, axis=0),
            (((1,), (1,)), ((), ())),
            preferred_element_type=F32,
        )
        for tile in range(sums_ref.shape[0]):
            block = product[:, tile * 128 : min(lanes, (tile + 1) * 128)]
            old = sums_ref[tile, :, : block.shape[1]]
            sums_ref[tile, :, : block.shape[1]] = jnp.where(height == 0, 0.0, old) + block


def flattened(channels, sources, factor, sums_ref, flat_ref):
    lanes = flat_ref.shape[1]
    span = sources * channels
    merged = lanes // span
    count = channels // merged
    lane = lax.broadcasted_iota(jnp.int32, (count, lanes), 1)
    for outer in range(sums_ref.shape[1] // channels):
        for width_tap in range(TAPS):
            first = width_tap * span
            tile, inner = first // lanes, first % lanes
            total = None
            for row in range(merged):
                block = sums_ref[tile, pl.ds(outer * channels + row, count, stride=merged), :]
                turn = (row * span - inner) % lanes
                block = pltpu.roll(block, turn, 1) if turn else block
                total = block if total is None else jnp.where(lane >= row * span, block, total)
            start = (outer * TAPS + width_tap) * count
            flat_ref[start : start + count, :] = total * factor


def tap_sums(channels, factor, slabs, me_ref, padded_ref, shifted_refs, out_refs, sums_ref, flat_ref):
    blocks = TAPS * TAPS
    if len(out_refs) == 1:
        outers = [(outer // TAPS, outer % TAPS) for outer in range(blocks)]
    else:
        outers, offsets = [], []
        part = out_refs[0].shape[0]
        held = flat_ref.shape[0] // (PAIR * len(out_refs))
        for distance in range(len(out_refs)):
            place = ((me_ref[1] ^ distance) * slabs + me_ref[0]) * part
            first = place // held
            offsets.append(PAIR * distance * held + place - first * held)
            for outer in (first, jnp.minimum(first + 1, blocks - 1)):
                outers.append((outer // TAPS, outer % TAPS))
    outer_sums(channels, outers, padded_ref, shifted_refs, sums_ref)
    flattened(channels, len(shifted_refs), factor, sums_ref, flat_ref)
    if len(out_refs) == 1:
        out_refs[0][...] = flat_ref[...]
    else:
        for out_ref, offset in zip(out_refs, offsets, strict=True):
            out_ref[...] = flat_ref[pl.ds(offset, part), :]


def padded_cells(channels, cells_ref, padded_ref):
    depth, rows, _ = cells_ref.shape
    padded_ref[...] = jnp.zeros_like(padded_ref)

    @pl.loop(0, depth)
    def _(layer):
        padded_ref[layer + 1, channels : channels + rows, :] = cells_ref[layer]


def dec_grad_kernel(channels, factor, slabs, me_ref, cot_ref, up_ref, down_ref, *refs):
    *out_refs, padded_ref, sums_ref, flat_ref = refs
    padded_cells(channels, cot_ref, padded_ref)
    shifted_refs = (up_ref, down_ref)
    tap_sums(channels, factor, slabs, me_ref, padded_ref, shifted_refs, out_refs, sums_ref, flat_ref)


def enc_grad_kernel(
    channels, factor, slabs, me_ref, p0, p1, p2, p3, turn_ref, grad_ref, hat_ref, scale_ref, columns_ref,
    shifted_ref, *refs,
):
    *out_refs, turned_ref, gated_ref, acc_ref, padded_ref, sums_ref, flat_ref = refs
    me = me_ref[0]
    depth, rows, width = hat_ref.shape
    count = rows // channels
    gains, biases = tiled(columns_ref[0, :, :1], count), tiled(columns_ref[1, :, :1], count)
    acc_ref[...] = jnp.zeros_like(acc_ref)
    size = turn_ref.shape[0]
    layers = size // rows
    turned_rows(piece_views((p0, p1, p2, p3), size, (2, 2, 1, 1)), turn_ref, turned_ref)
    for distance in range(turned_ref.shape[1] // width):
        owner = me ^ distance
        piece = turned_ref.at[:, distance * width : (distance + 1) * width]
        for inner in range(layers):
            layer = owner * layers + inner
            hat = hat_ref[layer]
            upstream = grad_ref[layer].astype(F32) + piece[inner * rows : (inner + 1) * rows, :].astype(F32)
            gated = jnp.where(gains * hat + biases > 0, upstream, 0.0) * gains
            gated_ref[layer] = gated
            acc_ref[0] += gated
            acc_ref[1] += gated * hat
    cells = depth * count * width
    first = tiled(over_channels(acc_ref[0], channels) * (1.0 / cells), count)
    second = tiled(over_channels(acc_ref[1], channels) * (1.0 / cells), count)
    scales = tiled(scale_ref[:, :1], count)
    padded_ref[...] = jnp.zeros_like(padded_ref)

    @pl.loop(0, depth)
    def _(layer):
        grad = (gated_ref[layer] - first - hat_ref[layer] * second) * scales
        padded_ref[layer + 1, channels : channels + rows, :] = grad.astype(BF16)

    tap_sums(channels, factor, slabs, me_ref, padded_ref, (shifted_ref,), out_refs, sums_ref, flat_ref)


def swapped(block, distance):
    count = lax.axis_size("space")
    return lax.ppermute(block, "space", [(i, i ^ distance) for i in range(count)])


def shifted_2(block, axis, distance):
    devices = range(lax.axis_size(axis))
    route = [(i - distance, i) for i in devices if i - distance in devices]
    return lax.ppermute(block, axis, route)


def halves(rows):
    count = lax.axis_size("dp") * lax.axis_size("space")
    blocks = TAPS * TAPS
    part, held = rows // count, rows // blocks
    return (
        lax.axis_size("dp") == PAIR
        and rows % count == 0
        and all((place + 1) * part <= (place * part // held + PAIR) * held for place in range(count))
    )


def scattered(flat):
    count, slabs = lax.axis_size("dp"), lax.axis_size("space")
    every = flat.reshape(count, slabs, -1)
    mine = lax.dynamic_index_in_dim(every, lax.axis_index("space"), 1, keepdims=False)
    return lax.psum_scatter(mine, "dp", scatter_dimension=0, tiled=True)


def finish_kernel(sums, *refs):
    moved = refs[:2]
    parts = refs[2 : 2 + 2 * sums]
    *outs, sems = refs[2 + 2 * sums :]
    copies = [
        pltpu.make_async_copy(source, target, sems.at[at])
        for at, (source, target) in enumerate(zip(moved, outs[:2], strict=True))
    ]
    for copy in copies:
        copy.start()
    for at, out in enumerate(outs[2:]):
        kept, received = parts[2 * at : 2 * at + 2]
        total = kept[...] + received[...]
        lanes = total.shape[1]
        for row in range(total.shape[0]):
            out[:, row * lanes : (row + 1) * lanes] = total[row : row + 1]
    for copy in copies:
        copy.wait()


def body(
    enc_input, dec_input, dec_cotangent, deep_cotangent, enc_weight, dec_weight,
    enc_gain, enc_bias, dec_gain, dec_bias,
):
    _, _, channels, slab_depth, height, width = enc_input.shape
    slabs = lax.axis_size("space")
    depth = slab_depth * slabs
    slab_height = height // slabs
    rows = channels * height
    voxels = depth * height * width
    factor = 1.0 / math.sqrt(lax.axis_size("dp") * voxels)
    me = jnp.stack([lax.axis_index("space"), lax.axis_index("dp")]).astype(jnp.int32)

    shape = pltpu.VMEM
    size = channels * slab_depth * height
    far, near = slabs // 2, slabs // 4
    enc_raw, cot_raw, dec_raw, deep_raw = (
        cells.reshape(size, width) for cells in (enc_input, dec_cotangent, dec_input, deep_cotangent)
    )
    enc_far = swapped(enc_raw, far)
    enc_near = swapped(enc_raw, near)
    cot_far = swapped(cot_raw, far)

    square = shape((size, size), BF16)
    matrix = shape((TAPS * rows, TAPS * rows), BF16)
    small = pltpu.VMEM((1, channels), F32)
    wide = pltpu.VMEM((enc_weight.shape[1], channels, 128), F32)
    enc_banded, flip_banded, up_banded, down_banded, turn, back, columns, enc_own, mine = call(
        prepare_kernel,
        (
            matrix, matrix, matrix, matrix, square, square, shape((4, channels, 128), F32),
            shape((size, width), BF16), shape((3 * size, width), BF16),
        ),
        [
            pltpu.VMEM(enc_weight.shape[1:], BF16), pltpu.VMEM(dec_weight.shape[1:], BF16),
            small, small, small, small, pltpu.SemaphoreType.DMA((10,)), wide, wide,
        ],
        1,
        [pl.BlockSpec(memory_space=pltpu.HBM)] * 10 + [pl.BlockSpec(memory_space=pltpu.SMEM)],
    )(
        *(
            pltpu.with_memory_space_constraint(array, pltpu.HBM)
            for array in (
                enc_weight[0], dec_weight[0], enc_gain, enc_bias, dec_gain, dec_bias,
                enc_raw, cot_raw, dec_raw, deep_raw,
            )
        ),
        me,
    )
    others_far = swapped(mine[size:], far)
    others_near = swapped(mine, near)
    enc_relay = swapped(enc_far, near)
    cot_relay = swapped(cot_far, near)
    others_relay = swapped(others_far, near)

    shifted_shape = (depth, TAPS * rows, width)
    cell_shape = (depth, rows, width)
    turned = pltpu.VMEM((size, slabs * width), BF16)
    parts = pltpu.VMEM((depth + 2, TAPS, rows, width), F32)
    padded = pltpu.VMEM((depth + 2, rows + 2 * channels, width), BF16)
    pre, line_sums = pltpu.VMEM(cell_shape, F32), pltpu.VMEM((2, rows, width), F32)
    enc_shifted, hat, skip, skip_own, scale = call(
        functools.partial(enc_kernel, channels),
        (
            shape(shifted_shape, BF16),
            shape(cell_shape, F32),
            shape(cell_shape, BF16),
            shape((size, width), BF16),
            shape((channels, 128), F32),
        ),
        [turned, parts, pre, line_sums],
    )(me, enc_own, enc_near, enc_far, enc_relay, enc_banded, turn, back, columns)
    enc_moved = shifted_2(skip_own, "section", 1)

    skip_grad, cot = call(
        functools.partial(skip_grad_kernel, size),
        (shape(cell_shape, BF16), shape(cell_shape, BF16)),
        [pltpu.VMEM(shifted_shape, BF16), turned, parts],
        1,
    )(me, mine, others_near, cot_far, cot_relay, flip_banded, turn, scale)

    dec_act, up, down = call(
        functools.partial(dec_kernel, channels, size),
        (shape((size, width), BF16), shape(shifted_shape, BF16), shape(shifted_shape, BF16)),
        [turned, parts, pre, line_sums],
        1,
    )(
        me, mine, others_near, others_far, others_relay, skip, up_banded, down_banded, turn, back, columns,
        skip_grad,
    )
    dec_moved = shifted_2(dec_act, "section", -1)

    flat_rows = TAPS * TAPS * TAPS * channels * channels // 128
    pair = halves(flat_rows) and halves(2 * flat_rows)

    def grad_shapes(total):
        if not pair:
            return (shape((total, 128), F32),)
        return (shape((total // (PAIR * slabs), 128), F32),) * 2

    def grad_scratch(total, tiles):
        outers = 2 * PAIR if pair else TAPS * TAPS
        held = total // (TAPS * TAPS) * outers
        return [padded, pltpu.VMEM((tiles, outers * channels, 128), F32), pltpu.VMEM((held, 128), F32)]

    dec_flat = call(
        functools.partial(dec_grad_kernel, channels, factor, slabs),
        grad_shapes(2 * flat_rows),
        grad_scratch(2 * flat_rows, 2),
    )(me, cot, up, down)
    enc_flat = call(
        functools.partial(enc_grad_kernel, channels, factor, slabs),
        grad_shapes(flat_rows),
        [turned, pre, line_sums, *grad_scratch(flat_rows, 1)],
        1,
    )(
        me, mine, others_near, others_far, others_relay, turn, skip_grad, hat, scale, columns, enc_shifted,
        dec_flat[0],
    )

    operands, sums, ends = [enc_moved, dec_moved], 0, []
    if pair:
        for (kept, sent) in (enc_flat, dec_flat):
            operands += [kept, lax.ppermute(sent, "dp", [(0, 1), (1, 0)])]
            ends.append(jax.ShapeDtypeStruct((1, kept.size), F32))
            sums += 1
    moved = jax.ShapeDtypeStruct((size, width), BF16)
    enc_handoff, dec_handoff, *grads = call(
        functools.partial(finish_kernel, sums),
        (moved, moved, *ends),
        [pltpu.SemaphoreType.DMA((2,))],
        0,
        None,
        (pl.BlockSpec(memory_space=pl.ANY),) * 2 + (pl.BlockSpec(memory_space=pltpu.VMEM),) * sums,
    )(*operands)
    if not pair:
        grads = [scattered(enc_flat[0]), scattered(dec_flat[0])]
    enc_handoff = enc_handoff.reshape(1, 1, channels, slab_depth, height, width)
    dec_handoff = dec_handoff.reshape(1, 1, channels, depth, slab_height, width)
    return (enc_handoff, dec_handoff, grads[0].reshape(1, -1), grads[1].reshape(1, -1))


def solution(mesh):
    in_specs = (
        P("section", "dp", None, "space", None, None),
        P("section", "dp", None, None, "space", None),
        P("section", "dp", None, None, "space", None),
        P("section", "dp", None, "space", None, None),
        P("section", None, None, None),
        P("section", None, None, None),
        P("section", None),
        P("section", None),
        P("section", None),
        P("section", None),
    )
    out_specs = (
        P("section", "dp", None, "space", None, None),
        P("section", "dp", None, None, "space", None),
        P("section", ("dp", "space")),
        P("section", ("dp", "space")),
    )

    return jax.shard_map(body, mesh=mesh, in_specs=in_specs, out_specs=out_specs, check_vma=False)
```

time: 56 us -> 50.2 us (0.90)
  local copies, waits for them, and re-layouts: 9.75 us -> 0.03 us
  waiting for transfers between devices: 3.12 us -> 12.6 us
  starting transfers between devices: 15.9 us -> 12.8 us
  other arithmetic: 1.31 us -> 0.08 us
  Pallas kernels: 24.7 us -> 23.8 us
    ppermute x14 -> x10, waiting for transfers between devices: 2.67 us -> 12.6 us  [the longest x8 9.39 us: swapped(): lax.ppermute(block, 'space', [(i, i ^ distance) for i in range(count)])]
    transpose x4 -> x0, local copies, waits for them, and re-layouts: 2.89 us -> none  [canonical(): return cells[0, 0].transpose(1, 2, 0, 3).reshape(-1, width)]
    reshape x11 -> x0, local copies, waits for them, and re-layouts: 2.75 us -> none  [the longest x1 0.76 us: body(): dec_moved.reshape(depth, slab_height, channels, width).transpose(2, 0, 1, 3)]
    unnamed x16 -> x4, local copies, waits for them, and re-layouts: 2.38 us -> 0.01 us
    ppermute x14 -> x10, starting transfers between devices: 10 us -> 7.76 us  [the longest x8 5.6 us: swapped(): lax.ppermute(block, 'space', [(i, i ^ distance) for i in range(count)])]
    pallas_call x5 -> x6, Pallas kernels: 21.1 us -> 19.6 us  [the longest x1 4.84 us: body(): call(functools.partial(dec_kernel, channels, size), (shape((size, width),...]
    add x2 -> x0, other arithmetic: 1.27 us -> none  [summed_part(): return kept + lax.ppermute(sent, name_dp, [(0, 1), (1, 0)])]
    slice x1, local copies, waits for them, and re-layouts: 1.16 us -> 0.02 us  [body(): others_far = swapped(mine[size:], far)]
  transfers between devices with their start and end apart: 16 -> 12, of which waited for: 2 -> 4; matrix products, arithmetic and copies ran while one was open for 12% -> 0% of each run, Pallas kernels for 25% -> 37%
where the time goes in v2:
time: 50.2 us; the launch traced here: 50 us
  Pallas kernels  23.8 us (47%)
  starting transfers between devices  12.8 us (25%)
  waiting for transfers between devices  12.6 us (25%)
  between operations  0.75 us (1%)
    ppermute x8, waiting for transfers between devices, swapped(): lax.ppermute(block, 'space', [(i, i ^ distance) for i in range(count)])  9.39 us
    ppermute x8, starting transfers between devices, swapped(): lax.ppermute(block, 'space', [(i, i ^ distance) for i in range(count)])  5.6 us
    ppermute x2, starting transfers between devices, shifted_2(): return lax.ppermute(block, axis, route)  5 us
    pallas_call x1, Pallas kernels, body(): call(functools.partial(dec_kernel, channels, size), (shape((size, width),...  4.84 us
    pallas_call x1, Pallas kernels, body(): call(functools.partial(enc_kernel, channels), (shape(shifted_shape, BF16)...  4.26 us
    pallas_call x1, Pallas kernels, body(): call(prepare_kernel, (matrix, matrix, matrix, matrix, square, square, sha...  4.08 us
    pallas_call x1, Pallas kernels, body(): call(functools.partial(enc_grad_kernel, channels, factor, slabs), grad_sh...  3.74 us
    ppermute x2, waiting for transfers between devices, body(): operands += [kept, lax.ppermute(sent, 'dp', [(0, 1), (1, 0)])]  3.2 us
  transfers between devices with their start and end apart: 12, of which 4 were waited for; matrix products, arithmetic and copies ran while one was open for 0% of the time, Pallas kernels for 37%

profile of v2, /device:TPU:0, one launch (start us, length us, event | category | flops | bytes accessed | tf_op | source)
XLA Modules:
  0.0 50.0 jit_solution(13025721485119639080)
XLA Ops:
  0.6 0.0 copy-start
  0.6 0.0 copy-start.1
  0.7 0.1 pad_add_fusion.refs_10_.refs_0_
  0.7 4.1 %shard_map.129 = (bf16[768,768]{1,0:T(8,128)(2,1)S(1)}, bf16[768,768]{1,0:T(8,128)(2,1)S(1)}, bf16[768,768]{1,0:T(8,128)(2,1)S(1)}, bf16[768,768]{1,0:T(8,128)(2...) custom-call(bf16[27,32,32]{2,1,0:T(8,128)(2,1)} %bitcast.10, ...), custom_call_target="tpu_custom_call" | custom-call | flops 4096 | bytes 1024 | tf_op jit(solution)/shard_map/pallas_call | solution.py:514
  4.8 3.1 %collective-permute-start.5 = (bf16[1024,128]{1,0:T(8,128)(2,1)S(1)}, bf16[1024,128]{1,0:T(8,128)(2,1)S(1)}, u32[]{:S(2)}, u32[]{:S(2)}) collective-permute-start(bf16[1024,128]{1,0:T(8,128)(2,1)S(1)} %slice.3), channel_id=1, source_target_pairs={{0,2},{1,3},{2,0},{3,1},{4,6},{5,7},{6,4},{7,5},{8,10},{9,11},{10,... | collective-permute-start | bytes 786440 | tf_op jit(solution)/shard_map/ppermute | solution.py:440
  7.9 0.0 collective-permute-start.4
  7.9 0.2 collective-permute-start.1
  8.1 1.9 %collective-permute-start.7 = (bf16[512,128]{1,0:T(8,128)(2,1)S(1)}, bf16[512,128]{1,0:T(8,128)(2,1)S(1)}, u32[]{:S(2)}, u32[]{:S(2)}) collective-permute-start(bf16[512,128]{1,0:T(8,128)(2,1)S(1)} %bitcast.15), channel_id=1, source_target_pairs={{0,2},{1,3},{2,0},{3,1},{4,6},{5,7},{6,4},{7,5},{8,10},{9,11},{10,... | collective-permute-start | bytes 393224 | tf_op jit(solution)/shard_map/ppermute | solution.py:440
  9.9 5.1 %collective-permute-done.5.refs_3_ = bf16[1024,128]{1,0:T(8,128)(2,1)S(1)} collective-permute-done((bf16[1024,128]{1,0:T(8,128)(2,1)S(1)}, bf16[1024,128]{1,0:T(8,128)(2,1)S(1)}, u32[]{:S(2)}, u32[]{:S(2)}) %collective-permute-start.5) | collective-permute-done | bytes 262176 | tf_op jit(solution)/shard_map/ppermute | solution.py:440
  15.1 0.5 %collective-permute-start = (bf16[512,128]{1,0:T(8,128)(2,1)S(1)}, bf16[512,128]{1,0:T(8,128)(2,1)S(1)}, u32[]{:S(2)}, u32[]{:S(2)}) collective-permute-start(bf16[512,128]{1,0:T(8,128)(2,1)S(1)} %bitcast.18), channel_id=1, source_target_pairs={{0,1},{1,0},{2,3},{3,2},{4,5},{5,4},{6,7},{7,6},{8,9},{9,8},{10,11... | collective-permute-start | bytes 393224 | tf_op jit(solution)/shard_map/ppermute | solution.py:440
  15.6 2.3 %collective-permute-done.1.refs_3_ = bf16[512,128]{1,0:T(8,128)(2,1)S(1)} collective-permute-done((bf16[512,128]{1,0:T(8,128)(2,1)S(1)}, bf16[512,128]{1,0:T(8,128)(2,1)S(1)}, u32[]{:S(2)}, u32[]{:S(2)}) %collective-permute-start.1) | collective-permute-done | bytes 131104 | tf_op jit(solution)/shard_map/ppermute | solution.py:440
  17.9 0.0 collective-permute-start.2
  17.9 2.0 %collective-permute-done.7.refs_3_ = bf16[512,128]{1,0:T(8,128)(2,1)S(1)} collective-permute-done((bf16[512,128]{1,0:T(8,128)(2,1)S(1)}, bf16[512,128]{1,0:T(8,128)(2,1)S(1)}, u32[]{:S(2)}, u32[]{:S(2)}) %collective-permute-start.7) | collective-permute-done | bytes 131104 | tf_op jit(solution)/shard_map/ppermute | solution.py:440
  19.8 0.0 collective-permute-start.8
  19.8 0.0 collective-permute-done.refs_2_
  19.8 0.0 collective-permute-done.2.refs_4_
  19.8 4.3 %shard_map.130 = (bf16[8,768,128]{2,1,0:T(8,128)(2,1)S(1)}, f32[8,256,128]{2,1,0:T(8,128)S(1)}, bf16[8,256,128]{2,1,0:T(8,128)(2,1)S(1)}, bf16[512,128]{1,0:T(8,128)(2,1)S(1)}, f32[32,128]{1,0:T(8,128)S(1)}) custom-call(s32[2]{0:T(128)S(1)} %pad_add_fusion.refs_10_.refs_0_, bf16[512,128]{1,0:T(8,128)(2,1)S(1)} %get-tuple-element.31.refs_1_, ...), custom_call_target="tpu_custom_call" | custom-call | flops 4096 | bytes 1024 | tf_op jit(solution)/shard_map/pallas_call | solution.py:548
  24.1 3.7 %collective-permute-start.3 = (bf16[512,128]{1,0:T(8,128)(2,1)S(1)}, bf16[512,128]{1,0:T(8,128)(2,1)S(1)}, u32[]{:S(2)}, u32[]{:S(2)}) collective-permute-start(bf16[512,128]{1,0:T(8,128)(2,1)S(1)} %get-tuple-element.36), channel_id=1, source_target_pairs={{0,8},{8,16},{16,24},{1,9},{9,17},{17,25},{2,10},{10,18},{18,26},{... | collective-permute-start | bytes 393224 | tf_op jit(solution)/shard_map/ppermute | solution.py:446
  27.8 0.0 collective-permute-done.8.refs_4_
  27.8 3.0 %shard_map.131 = (bf16[8,256,128]{2,1,0:T(8,128)(2,1)S(1)}, bf16[8,256,128]{2,1,0:T(8,128)(2,1)S(1)}) custom-call(s32[2]{0:T(128)S(1)} %pad_add_fusion.refs_10_.refs_0_, bf16[1536,128]{1,0:T(8,128)(2,1)S(1)} %get-tuple-element.37.refs_1_, bf16[1536,128]{1,0:T(8,128)(2,1)S(1)} %collective-permute-done.4.refs_2_, ...), custom_call_target="tpu_custom_call" | custom-call | flops 4096 | bytes 1024 | tf_op jit(solution)/shard_map/pallas_call | solution.py:561
  30.8 0.0 collective-permute-done.6.refs_4_
  30.8 4.8 %shard_map.132 = (bf16[512,128]{1,0:T(8,128)(2,1)S(1)}, bf16[8,768,128]{2,1,0:T(8,128)(2,1)S(1)}, bf16[8,768,128]{2,1,0:T(8,128)(2,1)S(1)}) custom-call(s32[2]{0:T(128)S(1)} %pad_add_fusion.refs_10_.refs_0_, bf16[1536,128]{1,0:T(8,128)(2,1)S(1)} %get-tuple-element.37.refs_1_, bf16[1536,128]{1,0:T(8,128)(2,1)S(1)} %collective-permute-done.4.refs_2_, ...), custom_call_target="tpu_custom_call" | custom-call | flops 4096 | bytes 1024 | tf_op jit(solution)/shard_map/pallas_call | solution.py:568
  35.7 1.3 %collective-permute-start.9 = (bf16[512,128]{1,0:T(8,128)(2,1)S(1)}, bf16[512,128]{1,0:T(8,128)(2,1)S(1)}, u32[]{:S(2)}, u32[]{:S(2)}) collective-permute-start(bf16[512,128]{1,0:T(8,128)(2,1)S(1)} %get-tuple-element.44), channel_id=1, source_target_pairs={{8,0},{16,8},{24,16},{9,1},{17,9},{25,17},{10,2},{18,10},{26,18},{... | collective-permute-start | bytes 393224 | tf_op jit(solution)/shard_map/ppermute | solution.py:446
  37.0 2.6 %shard_map.133 = (f32[54,128]{1,0:T(8,128)S(1)}, f32[54,128]{1,0:T(8,128)S(1)}) custom-call(s32[2]{0:T(128)S(1)} %pad_add_fusion.refs_10_.refs_0_, bf16[8,256,128]{2,1,0:T(8,128)(2,1)S(1)} %get-tuple-element.47.refs_1_, bf16[8,768,128]{2,1,0:T(8,128)(2,1)S(1)} %get-tuple-element.48.refs_2_, bf16[8,768,128]{2,1,0:T(8,128)(2,1)S(1)} %get-tuple-element.49.refs_3_), custom_call_target="tpu_custom_call" | custom-call | flops 4096 | bytes 1024 | tf_op jit(solution)/shard_map/pallas_call | solution.py:592
  39.6 1.6 %collective-permute-start.11 = (f32[54,128]{1,0:T(8,128)S(1)}, f32[54,128]{1,0:T(8,128)S(1)}, u32[]{:S(2)}, u32[]{:S(2)}) collective-permute-start(f32[54,128]{1,0:T(8,128)S(1)} %get-tuple-element.53), channel_id=1, source_target_pairs={{0,4},{4,0},{1,5},{5,1},{2,6},{6,2},{3,7},{7,3},{8,12},{12,8},{9,1... | collective-permute-start | bytes 82952 | tf_op jit(solution)/shard_map/ppermute | solution.py:610
  41.1 3.7 %shard_map.134 = (f32[27,128]{1,0:T(8,128)S(1)}, f32[27,128]{1,0:T(8,128)S(1)}) custom-call(s32[2]{0:T(128)S(1)} %pad_add_fusion.refs_10_.refs_0_, bf16[1536,128]{1,0:T(8,128)(2,1)S(1)} %get-tuple-element.37.refs_1_, bf16[1536,128]{1,0:T(8,128)(2,1)S(1)} %collective-permute-done.4.refs_2_, bf16[1024,128]{1,0:T(8,128)(2,1)S(1)} %collective-permute-done.5.refs_3_, ...), custom_call_target="tpu_custom_call" | custom-call | flops 4096 | bytes 1024 | tf_op jit(solution)/shard_map/pallas_call | solution.py:597
  44.9 0.6 %collective-permute-start.10 = (f32[27,128]{1,0:T(8,128)S(1)}, f32[27,128]{1,0:T(8,128)S(1)}, u32[]{:S(2)}, u32[]{:S(2)}) collective-permute-start(f32[27,128]{1,0:T(8,128)S(1)} %get-tuple-element.52), channel_id=1, source_target_pairs={{0,4},{4,0},{1,5},{5,1},{2,6},{6,2},{3,7},{7,3},{8,12},{12,8},{9,1... | collective-permute-start | bytes 41480 | tf_op jit(solution)/shard_map/ppermute | solution.py:610
  45.5 0.0 collective-permute-done.3.refs_0_
  45.5 3.2 %collective-permute-done.10.refs_3_ = f32[27,128]{1,0:T(8,128)S(1)} collective-permute-done((f32[27,128]{1,0:T(8,128)S(1)}, f32[27,128]{1,0:T(8,128)S(1)}, u32[]{:S(2)}, u32[]{:S(2)}) %collective-permute-start.10) | collective-permute-done | bytes 13856 | tf_op jit(solution)/shard_map/ppermute | solution.py:610
  48.7 0.0 collective-permute-done.11.refs_5_
  48.7 0.0 collective-permute-done.9.refs_1_
  48.7 1.3 %shard_map.135 = (bf16[512,128]{1,0:T(8,128)(2,1)}, bf16[512,128]{1,0:T(8,128)(2,1)}, f32[1,3456]{1,0:T(1,128)}, f32[1,6912]{1,0:T(1,128)}) custom-call(bf16[512,128]{1,0:T(8,128)(2,1)S(1)} %collective-permute-done.3.refs_0_, bf16[512,128]{1,0:T(8,128)(2,1)S(1)} %collective-permute-done.9.refs_1_, f32[27,128]{1,0:T(8,128)S(1)} %get-tuple-element.51.refs_2_, ...), custom_call_target="tpu_custom_call" | custom-call | flops 4096 | bytes 1024 | tf_op jit(solution)/shard_map/pallas_call | solution.py:614
  (5 shorter events, 0.0 us)
Async XLA Ops:
  0.6 7.4 %copy-start = (bf16[1,1,32,8,2,128]{5,4,3,2,1,0:T(2,128)(2,1)S(1)}, bf16[1,1,32,8,2,128]{5,4,3,2,1,0:T(2,128)(2,1)}, u32[]{:S(2)}) copy-start(bf16[1,1,32,8,2,128]{5,4,3,2,1,0:T(2,128)(2,1)} %param.12) | copy-start | bytes 393220
  0.6 7.3 %copy-start.1 = (bf16[1,1,32,2,8,128]{5,4,3,2,1,0:T(8,128)(2,1)S(1)}, bf16[1,1,32,2,8,128]{5,4,3,2,1,0:T(8,128)(2,1)}, u32[]{:S(2)}) copy-start(bf16[1,1,32,2,8,128]{5,4,3,2,1,0:T(8,128)(2,1)} %param.10) | copy-start | bytes 393220
  4.8 10.2 %collective-permute-start.5 = (bf16[1024,128]{1,0:T(8,128)(2,1)S(1)}, bf16[1024,128]{1,0:T(8,128)(2,1)S(1)}, u32[]{:S(2)}, u32[]{:S(2)}) collective-permute-start(bf16[1024,128]{1,0:T(8,128)(2,1)S(1)} %slice.3), channel_id=1, source_target_pairs={{0,2},{1,3},{2,0},{3,1},{4,6},{5,7},{6,4},{7,5},{8,10},{9,11},{10,... | collective-permute-start | bytes 786440 | tf_op jit(solution)/shard_map/ppermute | solution.py:440
  7.9 19.9 %collective-permute-start.4 = (bf16[1536,128]{1,0:T(8,128)(2,1)S(1)}, bf16[1536,128]{1,0:T(8,128)(2,1)S(1)}, u32[]{:S(2)}, u32[]{:S(2)}) collective-permute-start(bf16[1536,128]{1,0:T(8,128)(2,1)S(1)} %get-tuple-element.37.refs_1_), channel_id=1, source_target_pairs={{0,1},{1,0},{2,3},{3,2},{4,5},{5,4},{6,7},{7,6},{8,9},{9,8},{10,11... | collective-permute-start | bytes 1179656 | tf_op jit(solution)/shard_map/ppermute | solution.py:440
  7.9 10.0 %collective-permute-start.1 = (bf16[512,128]{1,0:T(8,128)(2,1)S(1)}, bf16[512,128]{1,0:T(8,128)(2,1)S(1)}, u32[]{:S(2)}, u32[]{:S(2)}) collective-permute-start(bf16[512,128]{1,0:T(8,128)(2,1)S(1)} %bitcast.17), channel_id=1, source_target_pairs={{0,2},{1,3},{2,0},{3,1},{4,6},{5,7},{6,4},{7,5},{8,10},{9,11},{10,... | collective-permute-start | bytes 393224 | tf_op jit(solution)/shard_map/ppermute | solution.py:440
  8.1 11.8 %collective-permute-start.7 = (bf16[512,128]{1,0:T(8,128)(2,1)S(1)}, bf16[512,128]{1,0:T(8,128)(2,1)S(1)}, u32[]{:S(2)}, u32[]{:S(2)}) collective-permute-start(bf16[512,128]{1,0:T(8,128)(2,1)S(1)} %bitcast.15), channel_id=1, source_target_pairs={{0,2},{1,3},{2,0},{3,1},{4,6},{5,7},{6,4},{7,5},{8,10},{9,11},{10,... | collective-permute-start | bytes 393224 | tf_op jit(solution)/shard_map/ppermute | solution.py:440
  15.1 15.8 %collective-permute-start.6 = (bf16[1024,128]{1,0:T(8,128)(2,1)S(1)}, bf16[1024,128]{1,0:T(8,128)(2,1)S(1)}, u32[]{:S(2)}, u32[]{:S(2)}) collective-permute-start(bf16[1024,128]{1,0:T(8,128)(2,1)S(1)} %collective-permute-done.5.refs_3_), channel_id=1, source_target_pairs={{0,1},{1,0},{2,3},{3,2},{4,5},{5,4},{6,7},{7,6},{8,9},{9,8},{10,11... | collective-permute-start | bytes 786440 | tf_op jit(solution)/shard_map/ppermute | solution.py:440
  15.1 4.8 %collective-permute-start = (bf16[512,128]{1,0:T(8,128)(2,1)S(1)}, bf16[512,128]{1,0:T(8,128)(2,1)S(1)}, u32[]{:S(2)}, u32[]{:S(2)}) collective-permute-start(bf16[512,128]{1,0:T(8,128)(2,1)S(1)} %bitcast.18), channel_id=1, source_target_pairs={{0,1},{1,0},{2,3},{3,2},{4,5},{5,4},{6,7},{7,6},{8,9},{9,8},{10,11... | collective-permute-start | bytes 393224 | tf_op jit(solution)/shard_map/ppermute | solution.py:440
  17.9 2.0 %collective-permute-start.2 = (bf16[512,128]{1,0:T(8,128)(2,1)S(1)}, bf16[512,128]{1,0:T(8,128)(2,1)S(1)}, u32[]{:S(2)}, u32[]{:S(2)}) collective-permute-start(bf16[512,128]{1,0:T(8,128)(2,1)S(1)} %collective-permute-done.1.refs_3_), channel_id=1, source_target_pairs={{0,1},{1,0},{2,3},{3,2},{4,5},{5,4},{6,7},{7,6},{8,9},{9,8},{10,11... | collective-permute-start | bytes 393224 | tf_op jit(solution)/shard_map/ppermute | solution.py:440
  19.8 8.0 %collective-permute-start.8 = (bf16[512,128]{1,0:T(8,128)(2,1)S(1)}, bf16[512,128]{1,0:T(8,128)(2,1)S(1)}, u32[]{:S(2)}, u32[]{:S(2)}) collective-permute-start(bf16[512,128]{1,0:T(8,128)(2,1)S(1)} %collective-permute-done.7.refs_3_), channel_id=1, source_target_pairs={{0,1},{1,0},{2,3},{3,2},{4,5},{5,4},{6,7},{7,6},{8,9},{9,8},{10,11... | collective-permute-start | bytes 393224 | tf_op jit(solution)/shard_map/ppermute | solution.py:440
  24.1 21.4 %collective-permute-start.3 = (bf16[512,128]{1,0:T(8,128)(2,1)S(1)}, bf16[512,128]{1,0:T(8,128)(2,1)S(1)}, u32[]{:S(2)}, u32[]{:S(2)}) collective-permute-start(bf16[512,128]{1,0:T(8,128)(2,1)S(1)} %get-tuple-element.36), channel_id=1, source_target_pairs={{0,8},{8,16},{16,24},{1,9},{9,17},{17,25},{2,10},{10,18},{18,26},{... | collective-permute-start | bytes 393224 | tf_op jit(solution)/shard_map/ppermute | solution.py:446
  35.7 13.0 %collective-permute-start.9 = (bf16[512,128]{1,0:T(8,128)(2,1)S(1)}, bf16[512,128]{1,0:T(8,128)(2,1)S(1)}, u32[]{:S(2)}, u32[]{:S(2)}) collective-permute-start(bf16[512,128]{1,0:T(8,128)(2,1)S(1)} %get-tuple-element.44), channel_id=1, source_target_pairs={{8,0},{16,8},{24,16},{9,1},{17,9},{25,17},{10,2},{18,10},{26,18},{... | collective-permute-start | bytes 393224 | tf_op jit(solution)/shard_map/ppermute | solution.py:446
  39.6 9.1 %collective-permute-start.11 = (f32[54,128]{1,0:T(8,128)S(1)}, f32[54,128]{1,0:T(8,128)S(1)}, u32[]{:S(2)}, u32[]{:S(2)}) collective-permute-start(f32[54,128]{1,0:T(8,128)S(1)} %get-tuple-element.53), channel_id=1, source_target_pairs={{0,4},{4,0},{1,5},{5,1},{2,6},{6,2},{3,7},{7,3},{8,12},{12,8},{9,1... | collective-permute-start | bytes 82952 | tf_op jit(solution)/shard_map/ppermute | solution.py:610
  44.9 3.8 %collective-permute-start.10 = (f32[27,128]{1,0:T(8,128)S(1)}, f32[27,128]{1,0:T(8,128)S(1)}, u32[]{:S(2)}, u32[]{:S(2)}) collective-permute-start(f32[27,128]{1,0:T(8,128)S(1)} %get-tuple-element.52), channel_id=1, source_target_pairs={{0,4},{4,0},{1,5},{5,1},{2,6},{6,2},{3,7},{7,3},{8,12},{12,8},{9,1... | collective-permute-start | bytes 41480 | tf_op jit(solution)/shard_map/ppermute | solution.py:610

commit v3 on v2

--- a/solution.py
+++ b/solution.py
@@ -53,12 +53,49 @@
     return jnp.where(lax.broadcasted_iota(jnp.int32, (size, size), 1) == source, 1.0, 0.0).astype(BF16)
 
 
+def banded(first, width_tap, found, lane):
+    channels, lanes = lane.shape
+    for out_ref, block in found:
+        rows = out_ref.shape[0] // TAPS
+        rolled = {}
+        for height in range(rows // channels):
+            offset = channels * (height - 1)
+            turn = offset % lanes
+            if turn not in rolled:
+                rolled[turn] = pltpu.roll(block, turn, 1) if turn else block
+            for tile in range(rows // lanes):
+                place = lane + (lanes * tile - offset)
+                inside = (place >= 0) & (place < TAPS * channels)
+                out_ref[
+                    pl.ds(first + height * channels, channels),
+                    width_tap * rows + tile * lanes : width_tap * rows + (tile + 1) * lanes,
+                ] = jnp.where(inside, rolled[turn], 0.0).astype(BF16)
+
+
+def strip(blocks):
+    total = blocks[0]
+    for place, block in enumerate(blocks[1:], 1):
+        total = total + pltpu.roll(block, place * block.shape[0], 1)
+    return total
+
+
+def widened(source, wide):
+    wide[...] = jnp.zeros_like(wide)
+    for tap in range(source.shape[0]):
+        wide[tap, :, : source.shape[2]] = source[tap].astype(F32)
+
+
+def height_taps(depth_tap, width_tap):
+    return [TAPS * TAPS * depth_tap + TAPS * height_tap + width_tap for height_tap in range(TAPS)]
+
+
 def prepare_kernel(
     enc_hbm, dec_hbm, g0, g1, g2, g3, own_hbm, cot_hbm, dec_in_hbm, deep_hbm,
-    enc_out, flip_out, up_out, down_out, turn_out, back_out, columns_out, own_out, mine_out,
-    enc_ref, dec_ref, row0, row1, row2, row3, sems, enc_wide, dec_wide,
+    enc_out, turn_out, back_out, columns_out, own_out, mine_out, dec_ref,
+    enc_ref, row0, row1, row2, row3, sems, enc_wide,
 ):
     size = own_hbm.shape[0]
+    channels = enc_ref.shape[1]
     rows_of = (row0, row1, row2, row3)
     copies = [
         pltpu.make_async_copy(source, target, sems.at[at])
@@ -72,24 +109,31 @@
     ]
     for copy in copies:
         copy.start()
-    channels = enc_ref.shape[1]
-    rows = enc_out.shape[0] // TAPS
-    lanes = enc_wide.shape[-1]
-    lane = lax.broadcasted_iota(jnp.int32, (channels, lanes), 1)
+    lane = lax.broadcasted_iota(jnp.int32, (channels, enc_wide.shape[-1]), 1)
     turn_out[...] = row_turn(turn_out.shape[0], turn_out.shape[0] // channels, channels)
     back_out[...] = row_turn(back_out.shape[0], channels, back_out.shape[0] // channels)
-    for copy in copies[:2]:
+    copies[0].wait()
+    widened(enc_ref, enc_wide)
+
+    @pl.loop(0, TAPS)
+    def _(depth_tap):
+        first = pl.multiple_of(depth_tap * (enc_out.shape[0] // TAPS), enc_out.shape[0] // TAPS)
+        for width_tap in range(TAPS):
+            taps = height_taps(depth_tap, width_tap)
+            banded(first, width_tap, [(enc_out, strip([enc_wide[tap] for tap in taps]))], lane)
+
+    for copy in copies[1:]:
         copy.wait()
-    for wide, source in ((enc_wide, enc_ref), (dec_wide, dec_ref)):
-        wide[...] = jnp.zeros_like(wide)
-        for tap in range(source.shape[0]):
-            wide[tap, :, : source.shape[2]] = source[tap].astype(F32)
-
-    def strip(blocks):
-        total = blocks[0]
-        for place, block in enumerate(blocks[1:], 1):
-            total = total + pltpu.roll(block, place * channels, 1)
-        return total
+    for place, row in enumerate(rows_of):
+        columns_out[place] = jnp.broadcast_to(column(row), columns_out.shape[1:])
+
+
+def weights_kernel(dec_ref, flip_out, up_out, down_out, wide):
+    channels = dec_ref.shape[1]
+    lanes = wide.shape[-1]
+    lane = lax.broadcasted_iota(jnp.int32, (channels, lanes), 1)
+    last = dec_ref.shape[0] - 1
+    widened(dec_ref, wide)
 
     def first_half(block):
         return jnp.where(lane < channels, block, 0.0)
@@ -103,35 +147,15 @@
 
     @pl.loop(0, TAPS)
     def _(depth_tap):
-        first = pl.multiple_of(depth_tap * rows, rows)
+        first = pl.multiple_of(depth_tap * (flip_out.shape[0] // TAPS), flip_out.shape[0] // TAPS)
         for width_tap in range(TAPS):
-            taps = [TAPS * TAPS * depth_tap + TAPS * b + width_tap for b in range(TAPS)]
-            last = dec_wide.shape[0] - 1
-            found = (
-                (enc_out, strip([enc_wide[tap] for tap in taps])),
-                (up_out, strip([first_half(dec_wide[tap]) for tap in taps])),
-                (down_out, strip([second_half(dec_wide[tap]) for tap in taps])),
-                (flip_out, turned([second_half(dec_wide[last - tap]) for tap in taps])),
-            )
-            for out_ref, block in found:
-                rolled = {}
-                for height in range(rows // channels):
-                    offset = channels * (height - 1)
-                    turn = offset % lanes
-                    if turn not in rolled:
-                        rolled[turn] = pltpu.roll(block, turn, 1) if turn else block
-                    for tile in range(rows // lanes):
-                        place = lane + (lanes * tile - offset)
-                        inside = (place >= 0) & (place < TAPS * channels)
-                        out_ref[
-                            pl.ds(first + height * channels, channels),
-                            width_tap * rows + tile * lanes : width_tap * rows + (tile + 1) * lanes,
-                        ] = jnp.where(inside, rolled[turn], 0.0).astype(BF16)
-
-    for copy in copies[2:]:
-        copy.wait()
-    for place, row in enumerate(rows_of):
-        columns_out[place] = jnp.broadcast_to(column(row), columns_out.shape[1:])
+            taps = height_taps(depth_tap, width_tap)
+            found = [
+                (up_out, strip([first_half(wide[tap]) for tap in taps])),
+                (down_out, strip([second_half(wide[tap]) for tap in taps])),
+                (flip_out, turned([second_half(wide[last - tap]) for tap in taps])),
+            ]
+            banded(first, width_tap, found, lane)
 
 
 def column(row_ref):
@@ -275,7 +299,7 @@
 
 def dec_kernel(
     channels, size, me_ref, p0, p1, p2, p3, skip_ref, up_weights_ref, down_weights_ref, turn_ref, back_ref,
-    columns_ref, own_ref, up_ref, down_ref, turned_ref, parts_ref, pre_ref, sums_ref,
+    columns_ref, skip_own_ref, first_ref, second_ref, up_ref, down_ref, turned_ref, parts_ref, pre_ref, sums_ref,
 ):
     me = me_ref[0]
     depth, rows, _ = pre_ref.shape
@@ -287,7 +311,7 @@
 
     taps_product([(up_weights_ref, up_ref), (down_weights_ref, down_ref)], parts_ref)
     mean, scale = normalized(parts_ref, pre_ref, sums_ref, channels)
-    part = own_ref.shape[0] // depth
+    part = size // depth
     count = part // channels
     means, scales = tiled(mean, count), tiled(scale, count)
     gains, biases = tiled(columns_ref[2, :, :1], count), tiled(columns_ref[3, :, :1], count)
@@ -298,7 +322,18 @@
         hat = (pre - means) * scales
         own.append(jnp.maximum(gains * hat + biases, 0.0).astype(BF16))
     own = jnp.concatenate(own, axis=0)
-    own_ref[...] = jnp.dot(back_ref[...], own, preferred_element_type=F32).astype(BF16)
+    own = jnp.dot(back_ref[...], own, preferred_element_type=F32).astype(BF16)
+    even = (me_ref[2] & 1) == 0
+
+    @pl.when(even)
+    def _():
+        first_ref[...] = skip_own_ref[...]
+        second_ref[...] = own
+
+    @pl.when(jnp.logical_not(even))
+    def _():
+        first_ref[...] = own
+        second_ref[...] = skip_own_ref[...]
 
 
 def outer_sums(channels, outers, padded_ref, shifted_refs, sums_ref):
@@ -402,6 +437,9 @@
     shifted_ref, *refs,
 ):
     *out_refs, turned_ref, gated_ref, acc_ref, padded_ref, sums_ref, flat_ref = refs
+    dec_refs = []
+    if len(out_refs) > 1:
+        dec_refs, out_refs = out_refs[:PAIR], out_refs[PAIR:]
     me = me_ref[0]
     depth, rows, width = hat_ref.shape
     count = rows // channels
@@ -432,7 +470,12 @@
         grad = (gated_ref[layer] - first - hat_ref[layer] * second) * scales
         padded_ref[layer + 1, channels : channels + rows, :] = grad.astype(BF16)
 
-    tap_sums(channels, factor, slabs, me_ref, padded_ref, (shifted_ref,), out_refs, sums_ref, flat_ref)
+    own_refs = list(out_refs)
+    for at, dec_ref in enumerate(dec_refs):
+        count = dec_ref.shape[0]
+        out_refs[at][:count, :] = dec_ref[...]
+        own_refs[at] = out_refs[at].at[count:]
+    tap_sums(channels, factor, slabs, me_ref, padded_ref, (shifted_ref,), own_refs, sums_ref, flat_ref)
 
 
 def swapped(block, distance):
@@ -440,10 +483,17 @@
     return lax.ppermute(block, "space", [(i, i ^ distance) for i in range(count)])
 
 
-def shifted_2(block, axis, distance):
-    devices = range(lax.axis_size(axis))
-    route = [(i - distance, i) for i in devices if i - distance in devices]
-    return lax.ppermute(block, axis, route)
+def paired(block, start):
+    count, copies = lax.axis_size("section"), lax.axis_size("dp")
+    route = []
+    for section in range(count):
+        upper = (section - start) % 2
+        partner = section - 1 if upper else section + 1
+        for copy in range(copies):
+            to = (partner, copy) if start <= min(section, partner) and partner < count else (section, copy ^ 1)
+            if to[1] < copies:
+                route.append((section * copies + copy, to[0] * copies + to[1]))
+    return lax.ppermute(block, ("section", "dp"), route)
 
 
 def halves(rows):
@@ -464,24 +514,42 @@
     return lax.psum_scatter(mine, "dp", scatter_dimension=0, tiled=True)
 
 
-def finish_kernel(sums, *refs):
-    moved = refs[:2]
-    parts = refs[2 : 2 + 2 * sums]
-    *outs, sems = refs[2 + 2 * sums :]
-    copies = [
-        pltpu.make_async_copy(source, target, sems.at[at])
-        for at, (source, target) in enumerate(zip(moved, outs[:2], strict=True))
-    ]
-    for copy in copies:
-        copy.start()
-    for at, out in enumerate(outs[2:]):
-        kept, received = parts[2 * at : 2 * at + 2]
-        total = kept[...] + received[...]
-        lanes = total.shape[1]
-        for row in range(total.shape[0]):
+def put_kernel(sections, me_ref, first_ref, second_ref, enc_out, dec_out, none_ref, sems):
+    none_ref[...] = jnp.zeros_like(none_ref)
+    section = me_ref[2]
+    last = section == sections - 1
+    even = (section & 1) == 0
+
+    def put(case, enc_from, dec_from):
+        @pl.when(case)
+        def _():
+            copies = (
+                pltpu.make_async_copy(enc_from, enc_out, sems.at[0]),
+                pltpu.make_async_copy(dec_from, dec_out, sems.at[1]),
+            )
+            for copy in copies:
+                copy.start()
+            for copy in copies:
+                copy.wait()
+
+    inner = (section > 0) & jnp.logical_not(last)
+    put((section == 0) & jnp.logical_not(last), none_ref, first_ref)
+    put(inner & even, second_ref, first_ref)
+    put(inner & jnp.logical_not(even), first_ref, second_ref)
+    put(last & even & (section > 0), second_ref, none_ref)
+    put(last & jnp.logical_not(even), first_ref, none_ref)
+    put(last & (section == 0), none_ref, none_ref)
+
+
+def finish_kernel(kept_ref, received_ref, *outs):
+    first = 0
+    for out in outs:
+        lanes = kept_ref.shape[1]
+        count = out.shape[1] // lanes
+        total = kept_ref[first : first + count, :] + received_ref[first : first + count, :]
+        for row in range(count):
             out[:, row * lanes : (row + 1) * lanes] = total[row : row + 1]
-    for copy in copies:
-        copy.wait()
+        first += count
 
 
 def body(
@@ -495,7 +563,7 @@
     rows = channels * height
     voxels = depth * height * width
     factor = 1.0 / math.sqrt(lax.axis_size("dp") * voxels)
-    me = jnp.stack([lax.axis_index("space"), lax.axis_index("dp")]).astype(jnp.int32)
+    me = jnp.stack([lax.axis_index("space"), lax.axis_index("dp"), lax.axis_index("section")]).astype(jnp.int32)
 
     shape = pltpu.VMEM
     size = channels * slab_depth * height
@@ -511,15 +579,15 @@
     matrix = shape((TAPS * rows, TAPS * rows), BF16)
     small = pltpu.VMEM((1, channels), F32)
     wide = pltpu.VMEM((enc_weight.shape[1], channels, 128), F32)
-    enc_banded, flip_banded, up_banded, down_banded, turn, back, columns, enc_own, mine = call(
+    enc_banded, turn, back, columns, enc_own, mine, dec_taps = call(
         prepare_kernel,
         (
-            matrix, matrix, matrix, matrix, square, square, shape((4, channels, 128), F32),
-            shape((size, width), BF16), shape((3 * size, width), BF16),
+            matrix, square, square, shape((4, channels, 128), F32), shape((size, width), BF16),
+            shape((3 * size, width), BF16), shape(dec_weight.shape[1:], BF16),
         ),
         [
-            pltpu.VMEM(enc_weight.shape[1:], BF16), pltpu.VMEM(dec_weight.shape[1:], BF16),
-            small, small, small, small, pltpu.SemaphoreType.DMA((10,)), wide, wide,
+            pltpu.VMEM(enc_weight.shape[1:], BF16), small, small, small, small,
+            pltpu.SemaphoreType.DMA((10,)), wide,
         ],
         1,
         [pl.BlockSpec(memory_space=pltpu.HBM)] * 10 + [pl.BlockSpec(memory_space=pltpu.SMEM)],
@@ -556,7 +624,7 @@
         ),
         [turned, parts, pre, line_sums],
     )(me, enc_own, enc_near, enc_far, enc_relay, enc_banded, turn, back, columns)
-    enc_moved = shifted_2(skip_own, "section", 1)
+    flip_banded, up_banded, down_banded = call(weights_kernel, (matrix, matrix, matrix), [wide], 1)(dec_taps, scale)
 
     skip_grad, cot = call(
         functools.partial(skip_grad_kernel, size),
@@ -565,16 +633,16 @@
         1,
     )(me, mine, others_near, cot_far, cot_relay, flip_banded, turn, scale)
 
-    dec_act, up, down = call(
+    first, second, up, down = call(
         functools.partial(dec_kernel, channels, size),
-        (shape((size, width), BF16), shape(shifted_shape, BF16), shape(shifted_shape, BF16)),
+        (shape((size, width), BF16),) * 2 + (shape(shifted_shape, BF16),) * 2,
         [turned, parts, pre, line_sums],
         1,
     )(
         me, mine, others_near, others_far, others_relay, skip, up_banded, down_banded, turn, back, columns,
-        skip_grad,
-    )
-    dec_moved = shifted_2(dec_act, "section", -1)
+        skip_own, skip_grad,
+    )
+    first = paired(first, 0)
 
     flat_rows = TAPS * TAPS * TAPS * channels * channels // 128
     pair = halves(flat_rows) and halves(2 * flat_rows)
@@ -594,36 +662,41 @@
         grad_shapes(2 * flat_rows),
         grad_scratch(2 * flat_rows, 2),
     )(me, cot, up, down)
+    second = paired(lax.optimization_barrier((second, dec_flat[0]))[0], 1)
     enc_flat = call(
         functools.partial(enc_grad_kernel, channels, factor, slabs),
-        grad_shapes(flat_rows),
+        tuple(shape((3 * flat_rows // (PAIR * slabs), 128), F32) for _ in range(PAIR))
+        if pair
+        else grad_shapes(flat_rows),
         [turned, pre, line_sums, *grad_scratch(flat_rows, 1)],
-        1,
+        0 if pair else 1,
     )(
         me, mine, others_near, others_far, others_relay, turn, skip_grad, hat, scale, columns, enc_shifted,
-        dec_flat[0],
-    )
-
-    operands, sums, ends = [enc_moved, dec_moved], 0, []
+        *dec_flat,
+    )
+
+    moved = jax.ShapeDtypeStruct((size, width), BF16)
+    enc_handoff, dec_handoff = call(
+        functools.partial(put_kernel, lax.axis_size("section")),
+        (moved, moved),
+        [pltpu.VMEM((size, width), BF16), pltpu.SemaphoreType.DMA((2,))],
+        1,
+        None,
+        (pl.BlockSpec(memory_space=pl.ANY),) * 2,
+    )(me, first, second, enc_flat[0])
     if pair:
-        for (kept, sent) in (enc_flat, dec_flat):
-            operands += [kept, lax.ppermute(sent, "dp", [(0, 1), (1, 0)])]
-            ends.append(jax.ShapeDtypeStruct((1, kept.size), F32))
-            sums += 1
-    moved = jax.ShapeDtypeStruct((size, width), BF16)
-    enc_handoff, dec_handoff, *grads = call(
-        functools.partial(finish_kernel, sums),
-        (moved, moved, *ends),
-        [pltpu.SemaphoreType.DMA((2,))],
-        0,
-        None,
-        (pl.BlockSpec(memory_space=pl.ANY),) * 2 + (pl.BlockSpec(memory_space=pltpu.VMEM),) * sums,
-    )(*operands)
-    if not pair:
-        grads = [scattered(enc_flat[0]), scattered(dec_flat[0])]
+        kept, sent = enc_flat
+        received = lax.ppermute(sent, "dp", [(0, 1), (1, 0)])
+        ends = tuple(
+            jax.ShapeDtypeStruct((1, rows * 128), F32)
+            for rows in (dec_flat[0].shape[0], kept.shape[0] - dec_flat[0].shape[0])
+        )
+        grads = call(finish_kernel, ends, [])(kept, received)
+    else:
+        grads = [scattered(dec_flat[0]), scattered(enc_flat[0])]
     enc_handoff = enc_handoff.reshape(1, 1, channels, slab_depth, height, width)
     dec_handoff = dec_handoff.reshape(1, 1, channels, depth, slab_height, width)
-    return (enc_handoff, dec_handoff, grads[0].reshape(1, -1), grads[1].reshape(1, -1))
+    return (enc_handoff, dec_handoff, grads[1].reshape(1, -1), grads[0].reshape(1, -1))
 
 
 def solution(mesh):

time: 50.2 us -> 47.7 us (0.950)
  starting transfers between devices: 12.8 us -> 10.6 us
  waiting for transfers between devices: 12.6 us -> 11.9 us
    ppermute x4 -> x3, starting transfers between devices: 7.16 us -> 4.99 us  [the longest x2 3.44 us: paired(): return lax.ppermute(block, ('section', 'dp'), route)]
    ppermute x4 -> x3, waiting for transfers between devices: 3.2 us -> 2.56 us  [the longest x1 2.56 us: body(): received = lax.ppermute(sent, 'dp', [(0, 1), (1, 0)])]
    pallas_call x3 -> x5, Pallas kernels: 9.14 us -> 9.41 us  [the longest x1 3.74 us: body(): call(functools.partial(enc_grad_kernel, channels, factor, slabs), tuple((...]
  transfers between devices with their start and end apart: 12 -> 11, of which waited for: 4 -> 4; matrix products, arithmetic and copies ran while one was open for 0% -> 0% of each run, Pallas kernels for 37% -> 28%
where the time goes in v3:
time: 47.7 us; the launch traced here: 47.5 us
  Pallas kernels  24.1 us (51%)
  waiting for transfers between devices  11.9 us (25%)
  starting transfers between devices  10.6 us (22%)
  between operations  0.75 us (2%)
    ppermute x8, waiting for transfers between devices, swapped(): lax.ppermute(block, 'space', [(i, i ^ distance) for i in range(count)])  9.39 us
    ppermute x8, starting transfers between devices, swapped(): lax.ppermute(block, 'space', [(i, i ^ distance) for i in range(count)])  5.6 us
    pallas_call x1, Pallas kernels, body(): call(functools.partial(dec_kernel, channels, size), (shape((size, width),...  4.87 us
    pallas_call x1, Pallas kernels, body(): call(functools.partial(enc_kernel, channels), (shape(shifted_shape, BF16)...  4.27 us
    pallas_call x1, Pallas kernels, body(): call(functools.partial(enc_grad_kernel, channels, factor, slabs), tuple((...  3.74 us
    ppermute x2, starting transfers between devices, paired(): return lax.ppermute(block, ('section', 'dp'), route)  3.44 us
    pallas_call x1, Pallas kernels, body(): call(functools.partial(skip_grad_kernel, size), (shape(cell_shape, BF16),...  2.96 us
    pallas_call x1, Pallas kernels, body(): call(functools.partial(dec_grad_kernel, channels, factor, slabs), grad_sh...  2.61 us
  transfers between devices with their start and end apart: 11, of which 4 were waited for; matrix products, arithmetic and copies ran while one was open for 0% of the time, Pallas kernels for 28%

profile of v3, /device:TPU:0, one launch (start us, length us, event | category | flops | bytes accessed | tf_op | source)
XLA Modules:
  0.0 47.5 jit_solution(11859412876992976994)
XLA Ops:
  0.6 0.0 copy-start
  0.6 0.0 copy-start.1
  0.7 0.1 pad_add_fusion.refs_10_.refs_0_
  0.7 2.3 %shard_map.129 = (bf16[768,768]{1,0:T(8,128)(2,1)S(1)}, bf16[512,512]{1,0:T(8,128)(2,1)S(1)}, bf16[512,512]{1,0:T(8,128)(2,1)S(1)}, f32[4,32,128]{2,1,0:T(8,128)...) custom-call(bf16[27,32,32]{2,1,0:T(8,128)(2,1)} %bitcast.11, ...), custom_call_target="tpu_custom_call" | custom-call | flops 4096 | bytes 1024 | tf_op jit(solution)/shard_map/pallas_call | solution.py:582
  3.1 3.1 %collective-permute-start.1 = (bf16[1024,128]{1,0:T(8,128)(2,1)S(1)}, bf16[1024,128]{1,0:T(8,128)(2,1)S(1)}, u32[]{:S(2)}, u32[]{:S(2)}) collective-permute-start(bf16[1024,128]{1,0:T(8,128)(2,1)S(1)} %slice.3), channel_id=1, source_target_pairs={{0,2},{1,3},{2,0},{3,1},{4,6},{5,7},{6,4},{7,5},{8,10},{9,11},{10,... | collective-permute-start | bytes 786440 | tf_op jit(solution)/shard_map/ppermute | solution.py:483
  6.1 0.0 collective-permute-start
  6.1 0.2 collective-permute-start.4
  6.3 1.9 %collective-permute-start.6 = (bf16[512,128]{1,0:T(8,128)(2,1)S(1)}, bf16[512,128]{1,0:T(8,128)(2,1)S(1)}, u32[]{:S(2)}, u32[]{:S(2)}) collective-permute-start(bf16[512,128]{1,0:T(8,128)(2,1)S(1)} %bitcast.16), channel_id=1, source_target_pairs={{0,2},{1,3},{2,0},{3,1},{4,6},{5,7},{6,4},{7,5},{8,10},{9,11},{10,... | collective-permute-start | bytes 393224 | tf_op jit(solution)/shard_map/ppermute | solution.py:483
  8.2 5.1 %collective-permute-done.1.refs_3_ = bf16[1024,128]{1,0:T(8,128)(2,1)S(1)} collective-permute-done((bf16[1024,128]{1,0:T(8,128)(2,1)S(1)}, bf16[1024,128]{1,0:T(8,128)(2,1)S(1)}, u32[]{:S(2)}, u32[]{:S(2)}) %collective-permute-start.1) | collective-permute-done | bytes 262176 | tf_op jit(solution)/shard_map/ppermute | solution.py:483
  13.3 0.0 collective-permute-start.2
  13.3 0.5 %collective-permute-start.3 = (bf16[512,128]{1,0:T(8,128)(2,1)S(1)}, bf16[512,128]{1,0:T(8,128)(2,1)S(1)}, u32[]{:S(2)}, u32[]{:S(2)}) collective-permute-start(bf16[512,128]{1,0:T(8,128)(2,1)S(1)} %bitcast.19), channel_id=1, source_target_pairs={{0,1},{1,0},{2,3},{3,2},{4,5},{5,4},{6,7},{7,6},{8,9},{9,8},{10,11... | collective-permute-start | bytes 393224 | tf_op jit(solution)/shard_map/ppermute | solution.py:483
  13.8 2.3 %collective-permute-done.4.refs_3_ = bf16[512,128]{1,0:T(8,128)(2,1)S(1)} collective-permute-done((bf16[512,128]{1,0:T(8,128)(2,1)S(1)}, bf16[512,128]{1,0:T(8,128)(2,1)S(1)}, u32[]{:S(2)}, u32[]{:S(2)}) %collective-permute-start.4) | collective-permute-done | bytes 131104 | tf_op jit(solution)/shard_map/ppermute | solution.py:483
  16.1 0.0 collective-permute-start.5
  16.1 2.0 %collective-permute-done.6.refs_3_ = bf16[512,128]{1,0:T(8,128)(2,1)S(1)} collective-permute-done((bf16[512,128]{1,0:T(8,128)(2,1)S(1)}, bf16[512,128]{1,0:T(8,128)(2,1)S(1)}, u32[]{:S(2)}, u32[]{:S(2)}) %collective-permute-start.6) | collective-permute-done | bytes 131104 | tf_op jit(solution)/shard_map/ppermute | solution.py:483
  18.1 0.0 collective-permute-start.7
  18.1 0.0 collective-permute-done.3.refs_2_
  18.1 0.0 collective-permute-done.5.refs_4_
  18.1 4.3 %shard_map.130 = (bf16[8,768,128]{2,1,0:T(8,128)(2,1)S(1)}, f32[8,256,128]{2,1,0:T(8,128)S(1)}, bf16[8,256,128]{2,1,0:T(8,128)(2,1)S(1)}, bf16[512,128]{1,0:T(8,128)(2,1)S(1)}, f32[32,128]{1,0:T(8,128)S(1)}) custom-call(s32[3]{0:T(128)S(1)} %pad_add_fusion.refs_10_.refs_0_, bf16[512,128]{1,0:T(8,128)(2,1)S(1)} %get-tuple-element.35.refs_1_, ...), custom_call_target="tpu_custom_call" | custom-call | flops 4096 | bytes 1024 | tf_op jit(solution)/shard_map/pallas_call | solution.py:616
  22.4 1.9 %shard_map.131 = (bf16[768,768]{1,0:T(8,128)(2,1)S(1)}, bf16[768,768]{1,0:T(8,128)(2,1)S(1)}, bf16[768,768]{1,0:T(8,128)(2,1)S(1)}) custom-call(bf16[27,32,64]{2,1,0:T(8,128)(2,1)S(1)} %get-tuple-element.41.refs_0_, f32[32,128]{1,0:T(8,128)S(1)} %get-tuple-element.42.refs_1_.refs_7_.refs_8_), custom_call_target="tpu_custom_call" | custom-call | flops 4096 | bytes 1024 | tf_op jit(solution)/shard_map/pallas_call | solution.py:627
  24.3 0.0 collective-permute-done.refs_2_
  24.3 3.0 %shard_map.132 = (bf16[8,256,128]{2,1,0:T(8,128)(2,1)S(1)}, bf16[8,256,128]{2,1,0:T(8,128)(2,1)S(1)}) custom-call(s32[3]{0:T(128)S(1)} %pad_add_fusion.refs_10_.refs_0_, bf16[1536,128]{1,0:T(8,128)(2,1)S(1)} %get-tuple-element.34.refs_1_, bf16[1536,128]{1,0:T(8,128)(2,1)S(1)} %collective-permute-done.refs_2_, ...), custom_call_target="tpu_custom_call" | custom-call | flops 4096 | bytes 1024 | tf_op jit(solution)/shard_map/pallas_call | solution.py:629
  27.2 0.0 collective-permute-done.2.refs_4_
  27.3 4.9 %shard_map.133 = (bf16[512,128]{1,0:T(8,128)(2,1)S(1)}, bf16[512,128]{1,0:T(8,128)(2,1)S(1)}, bf16[8,768,128]{2,1,0:T(8,128)(2,1)S(1)}, bf16[8,768,128]{2,1,0:T(8,128)(2,1)S(1)}) custom-call(s32[3]{0:T(128)S(1)} %pad_add_fusion.refs_10_.refs_0_, bf16[1536,128]{1,0:T(8,128)(2,1)S(1)} %get-tuple-element.34.refs_1_, ...), custom_call_target="tpu_custom_call" | custom-call | flops 4096 | bytes 1024 | tf_op jit(solution)/shard_map/pallas_call | solution.py:636
  32.1 2.6 %shard_map.134 = (f32[54,128]{1,0:T(8,128)S(1)}, f32[54,128]{1,0:T(8,128)S(1)}) custom-call(s32[3]{0:T(128)S(1)} %pad_add_fusion.refs_10_.refs_0_, bf16[8,256,128]{2,1,0:T(8,128)(2,1)S(1)} %get-tuple-element.50.refs_1_, bf16[8,768,128]{2,1,0:T(8,128)(2,1)S(1)} %get-tuple-element.51.refs_2_, bf16[8,768,128]{2,1,0:T(8,128)(2,1)S(1)} %get-tuple-element.52.refs_3_), custom_call_target="tpu_custom_call" | custom-call | flops 4096 | bytes 1024 | tf_op jit(solution)/shard_map/pallas_call | solution.py:660
  34.8 1.8 %collective-permute-start.9 = (bf16[512,128]{1,0:T(8,128)(2,1)S(1)}, bf16[512,128]{1,0:T(8,128)(2,1)S(1)}, u32[]{:S(2)}, u32[]{:S(2)}) collective-permute-start(bf16[512,128]{1,0:T(8,128)(2,1)S(1)} %get-tuple-element.54), channel_id=1, source_target_pairs={{0,4},{4,0},{8,16},{12,20},{16,8},{20,12},{24,28},{28,24},{1,5},{5... | collective-permute-start | bytes 393224 | tf_op jit(solution)/shard_map/ppermute | solution.py:496
  36.5 1.7 %collective-permute-start.8 = (bf16[512,128]{1,0:T(8,128)(2,1)S(1)}, bf16[512,128]{1,0:T(8,128)(2,1)S(1)}, u32[]{:S(2)}, u32[]{:S(2)}) collective-permute-start(bf16[512,128]{1,0:T(8,128)(2,1)S(1)} %get-tuple-element.48), channel_id=1, source_target_pairs={{0,8},{4,12},{8,0},{12,4},{16,24},{20,28},{24,16},{28,20},{1,9},{5... | collective-permute-start | bytes 393224 | tf_op jit(solution)/shard_map/ppermute | solution.py:496
  38.2 3.7 %shard_map.135 = (f32[81,128]{1,0:T(8,128)S(1)}, f32[81,128]{1,0:T(8,128)S(1)}) custom-call(s32[3]{0:T(128)S(1)} %pad_add_fusion.refs_10_.refs_0_, bf16[1536,128]{1,0:T(8,128)(2,1)S(1)} %get-tuple-element.34.refs_1_, bf16[1536,128]{1,0:T(8,128)(2,1)S(1)} %collective-permute-done.refs_2_, bf16[1024,128]{1,0:T(8,128)(2,1)S(1)} %collective-permute-done.1.refs_3_, ...), custom_call_target="tpu_custom_call" | custom-call | flops 4096 | bytes 1024 | tf_op jit(solution)/shard_map/pallas_call | solution.py:666
  42.0 1.6 %collective-permute-start.10 = (f32[81,128]{1,0:T(8,128)S(1)}, f32[81,128]{1,0:T(8,128)S(1)}, u32[]{:S(2)}, u32[]{:S(2)}) collective-permute-start(f32[81,128]{1,0:T(8,128)S(1)} %get-tuple-element.61), channel_id=1, source_target_pairs={{0,4},{4,0},{1,5},{5,1},{2,6},{6,2},{3,7},{7,3},{8,12},{12,8},{9,1... | collective-permute-start | bytes 124424 | tf_op jit(solution)/shard_map/ppermute | solution.py:689
  43.5 2.6 %collective-permute-done.10.refs_1_ = f32[81,128]{1,0:T(8,128)S(1)} collective-permute-done((f32[81,128]{1,0:T(8,128)S(1)}, f32[81,128]{1,0:T(8,128)S(1)}, u32[]{:S(2)}, u32[]{:S(2)}) %collective-permute-start.10) | collective-permute-done | bytes 41504 | tf_op jit(solution)/shard_map/ppermute | solution.py:689
  46.1 0.6 %shard_map.137 = (f32[1,6912]{1,0:T(1,128)}, f32[1,3456]{1,0:T(1,128)}) custom-call(f32[81,128]{1,0:T(8,128)S(1)} %get-tuple-element.58.refs_3_.refs_0_, f32[81,128]{1,0:T(8,128)S(1)} %collective-permute-done.10.refs_1_), custom_call_target="tpu_custom_call" | custom-call | flops 4096 | bytes 1024 | tf_op jit(solution)/shard_map/pallas_call | solution.py:694
  46.7 0.0 collective-permute-done.9.refs_2_
  46.7 0.8 %shard_map.136 = (bf16[512,128]{1,0:T(8,128)(2,1)}, bf16[512,128]{1,0:T(8,128)(2,1)}) custom-call(s32[3]{0:T(128)S(1)} %pad_add_fusion.refs_10_.refs_0_, bf16[512,128]{1,0:T(8,128)(2,1)S(1)} %collective-permute-done.8.refs_1_, bf16[512,128]{1,0:T(8,128)(2,1)S(1)} %collective-permute-done.9.refs_2_, f32[81,128]{1,0:T(8,128)S(1)} %get-tuple-element.58.refs_3_.refs_0_), custom_call_target="tpu_custom_call" | custom-call | flops 4096 | bytes 1024 | tf_op jit(solution)/shard_map/pallas_call | solution.py:679
  (5 shorter events, 0.0 us)
Async XLA Ops:
  0.6 5.7 %copy-start = (bf16[1,1,32,8,2,128]{5,4,3,2,1,0:T(2,128)(2,1)S(1)}, bf16[1,1,32,8,2,128]{5,4,3,2,1,0:T(2,128)(2,1)}, u32[]{:S(2)}) copy-start(bf16[1,1,32,8,2,128]{5,4,3,2,1,0:T(2,128)(2,1)} %param.12) | copy-start | bytes 393220
  0.6 5.5 %copy-start.1 = (bf16[1,1,32,2,8,128]{5,4,3,2,1,0:T(8,128)(2,1)S(1)}, bf16[1,1,32,2,8,128]{5,4,3,2,1,0:T(8,128)(2,1)}, u32[]{:S(2)}) copy-start(bf16[1,1,32,2,8,128]{5,4,3,2,1,0:T(8,128)(2,1)} %param.10) | copy-start | bytes 393220
  3.1 10.2 %collective-permute-start.1 = (bf16[1024,128]{1,0:T(8,128)(2,1)S(1)}, bf16[1024,128]{1,0:T(8,128)(2,1)S(1)}, u32[]{:S(2)}, u32[]{:S(2)}) collective-permute-start(bf16[1024,128]{1,0:T(8,128)(2,1)S(1)} %slice.3), channel_id=1, source_target_pairs={{0,2},{1,3},{2,0},{3,1},{4,6},{5,7},{6,4},{7,5},{8,10},{9,11},{10,... | collective-permute-start | bytes 786440 | tf_op jit(solution)/shard_map/ppermute | solution.py:483
  6.1 18.1 %collective-permute-start = (bf16[1536,128]{1,0:T(8,128)(2,1)S(1)}, bf16[1536,128]{1,0:T(8,128)(2,1)S(1)}, u32[]{:S(2)}, u32[]{:S(2)}) collective-permute-start(bf16[1536,128]{1,0:T(8,128)(2,1)S(1)} %get-tuple-element.34.refs_1_), channel_id=1, source_target_pairs={{0,1},{1,0},{2,3},{3,2},{4,5},{5,4},{6,7},{7,6},{8,9},{9,8},{10,11... | collective-permute-start | bytes 1179656 | tf_op jit(solution)/shard_map/ppermute | solution.py:483
  6.1 10.0 %collective-permute-start.4 = (bf16[512,128]{1,0:T(8,128)(2,1)S(1)}, bf16[512,128]{1,0:T(8,128)(2,1)S(1)}, u32[]{:S(2)}, u32[]{:S(2)}) collective-permute-start(bf16[512,128]{1,0:T(8,128)(2,1)S(1)} %bitcast.18), channel_id=1, source_target_pairs={{0,2},{1,3},{2,0},{3,1},{4,6},{5,7},{6,4},{7,5},{8,10},{9,11},{10,... | collective-permute-start | bytes 393224 | tf_op jit(solution)/shard_map/ppermute | solution.py:483
  6.3 11.8 %collective-permute-start.6 = (bf16[512,128]{1,0:T(8,128)(2,1)S(1)}, bf16[512,128]{1,0:T(8,128)(2,1)S(1)}, u32[]{:S(2)}, u32[]{:S(2)}) collective-permute-start(bf16[512,128]{1,0:T(8,128)(2,1)S(1)} %bitcast.16), channel_id=1, source_target_pairs={{0,2},{1,3},{2,0},{3,1},{4,6},{5,7},{6,4},{7,5},{8,10},{9,11},{10,... | collective-permute-start | bytes 393224 | tf_op jit(solution)/shard_map/ppermute | solution.py:483
  13.3 14.0 %collective-permute-start.2 = (bf16[1024,128]{1,0:T(8,128)(2,1)S(1)}, bf16[1024,128]{1,0:T(8,128)(2,1)S(1)}, u32[]{:S(2)}, u32[]{:S(2)}) collective-permute-start(bf16[1024,128]{1,0:T(8,128)(2,1)S(1)} %collective-permute-done.1.refs_3_), channel_id=1, source_target_pairs={{0,1},{1,0},{2,3},{3,2},{4,5},{5,4},{6,7},{7,6},{8,9},{9,8},{10,11... | collective-permute-start | bytes 786440 | tf_op jit(solution)/shard_map/ppermute | solution.py:483
  13.3 4.8 %collective-permute-start.3 = (bf16[512,128]{1,0:T(8,128)(2,1)S(1)}, bf16[512,128]{1,0:T(8,128)(2,1)S(1)}, u32[]{:S(2)}, u32[]{:S(2)}) collective-permute-start(bf16[512,128]{1,0:T(8,128)(2,1)S(1)} %bitcast.19), channel_id=1, source_target_pairs={{0,1},{1,0},{2,3},{3,2},{4,5},{5,4},{6,7},{7,6},{8,9},{9,8},{10,11... | collective-permute-start | bytes 393224 | tf_op jit(solution)/shard_map/ppermute | solution.py:483
  16.1 2.0 %collective-permute-start.5 = (bf16[512,128]{1,0:T(8,128)(2,1)S(1)}, bf16[512,128]{1,0:T(8,128)(2,1)S(1)}, u32[]{:S(2)}, u32[]{:S(2)}) collective-permute-start(bf16[512,128]{1,0:T(8,128)(2,1)S(1)} %collective-permute-done.4.refs_3_), channel_id=1, source_target_pairs={{0,1},{1,0},{2,3},{3,2},{4,5},{5,4},{6,7},{7,6},{8,9},{9,8},{10,11... | collective-permute-start | bytes 393224 | tf_op jit(solution)/shard_map/ppermute | solution.py:483
  18.1 6.2 %collective-permute-start.7 = (bf16[512,128]{1,0:T(8,128)(2,1)S(1)}, bf16[512,128]{1,0:T(8,128)(2,1)S(1)}, u32[]{:S(2)}, u32[]{:S(2)}) collective-permute-start(bf16[512,128]{1,0:T(8,128)(2,1)S(1)} %collective-permute-done.6.refs_3_), channel_id=1, source_target_pairs={{0,1},{1,0},{2,3},{3,2},{4,5},{5,4},{6,7},{7,6},{8,9},{9,8},{10,11... | collective-permute-start | bytes 393224 | tf_op jit(solution)/shard_map/ppermute | solution.py:483
  34.8 11.9 %collective-permute-start.9 = (bf16[512,128]{1,0:T(8,128)(2,1)S(1)}, bf16[512,128]{1,0:T(8,128)(2,1)S(1)}, u32[]{:S(2)}, u32[]{:S(2)}) collective-permute-start(bf16[512,128]{1,0:T(8,128)(2,1)S(1)} %get-tuple-element.54), channel_id=1, source_target_pairs={{0,4},{4,0},{8,16},{12,20},{16,8},{20,12},{24,28},{28,24},{1,5},{5... | collective-permute-start | bytes 393224 | tf_op jit(solution)/shard_map/ppermute | solution.py:496
  36.5 10.2 %collective-permute-start.8 = (bf16[512,128]{1,0:T(8,128)(2,1)S(1)}, bf16[512,128]{1,0:T(8,128)(2,1)S(1)}, u32[]{:S(2)}, u32[]{:S(2)}) collective-permute-start(bf16[512,128]{1,0:T(8,128)(2,1)S(1)} %get-tuple-element.48), channel_id=1, source_target_pairs={{0,8},{4,12},{8,0},{12,4},{16,24},{20,28},{24,16},{28,20},{1,9},{5... | collective-permute-start | bytes 393224 | tf_op jit(solution)/shard_map/ppermute | solution.py:496
  42.0 4.1 %collective-permute-start.10 = (f32[81,128]{1,0:T(8,128)S(1)}, f32[81,128]{1,0:T(8,128)S(1)}, u32[]{:S(2)}, u32[]{:S(2)}) collective-permute-start(f32[81,128]{1,0:T(8,128)S(1)} %get-tuple-element.61), channel_id=1, source_target_pairs={{0,4},{4,0},{1,5},{5,1},{2,6},{6,2},{3,7},{7,3},{8,12},{12,8},{9,1... | collective-permute-start | bytes 124424 | tf_op jit(solution)/shard_map/ppermute | solution.py:689

commit v4 on v3

--- a/solution.py
+++ b/solution.py
@@ -12,6 +12,7 @@
 EPS = 1e-05
 TAPS = 3
 PAIR = 2
+ROWS = 16
 LIMIT = 12 * 1024 * 1024
 BF16 = jnp.bfloat16
 F32 = jnp.float32
@@ -256,7 +257,7 @@
 
 
 def enc_kernel(
-    channels, me_ref, p0, p1, p2, p3, weights_ref, turn_ref, back_ref, columns_ref,
+    channels, me_ref, p0, p1, p2, p3, weights_ref, turn_ref, columns_ref,
     shifted_ref, hat_ref, skip_ref, own_ref, scale_ref, turned_ref, parts_ref, pre_ref, sums_ref,
 ):
     me = me_ref[0]
@@ -276,8 +277,8 @@
         skip_ref[layer] = jnp.maximum(gains * hat + biases, 0.0).astype(BF16)
 
     layers = own_ref.shape[0] // rows
-    own = jnp.concatenate([skip_ref[me * layers + layer] for layer in range(layers)], axis=0)
-    own_ref[...] = jnp.dot(back_ref[...], own, preferred_element_type=F32).astype(BF16)
+    for layer in range(layers):
+        own_ref[layer * rows : (layer + 1) * rows, :] = skip_ref[me * layers + layer]
 
 
 def piece_views(refs, size, places):
@@ -298,12 +299,12 @@
 
 
 def dec_kernel(
-    channels, size, me_ref, p0, p1, p2, p3, skip_ref, up_weights_ref, down_weights_ref, turn_ref, back_ref,
+    channels, size, me_ref, p0, p1, p2, p3, skip_ref, up_weights_ref, down_weights_ref, turn_ref,
     columns_ref, skip_own_ref, first_ref, second_ref, up_ref, down_ref, turned_ref, parts_ref, pre_ref, sums_ref,
 ):
     me = me_ref[0]
     depth, rows, _ = pre_ref.shape
-    spread_height(me, piece_views((p0, p1, p2, p3), size, (1, 1, 0, 0)), turn_ref, turned_ref, up_ref)
+    spread_height(me, piece_views((p0, p1, p2, p3), size, (1, 1, 1, 1)), turn_ref, turned_ref, up_ref)
 
     for layer in range(depth):
         for tap, block in enumerate(width_shifts(skip_ref[layer])):
@@ -322,7 +323,6 @@
         hat = (pre - means) * scales
         own.append(jnp.maximum(gains * hat + biases, 0.0).astype(BF16))
     own = jnp.concatenate(own, axis=0)
-    own = jnp.dot(back_ref[...], own, preferred_element_type=F32).astype(BF16)
     even = (me_ref[2] & 1) == 0
 
     @pl.when(even)
@@ -413,7 +413,11 @@
         out_refs[0][...] = flat_ref[...]
     else:
         for out_ref, offset in zip(out_refs, offsets, strict=True):
-            out_ref[...] = flat_ref[pl.ds(offset, part), :]
+            out_ref[...] = flat_ref[pl.ds(offset, part), :].astype(out_ref.dtype)
+
+
+def padded_rows(count):
+    return -(-count // ROWS) * ROWS
 
 
 def padded_cells(channels, cells_ref, padded_ref):
@@ -447,7 +451,7 @@
     acc_ref[...] = jnp.zeros_like(acc_ref)
     size = turn_ref.shape[0]
     layers = size // rows
-    turned_rows(piece_views((p0, p1, p2, p3), size, (2, 2, 1, 1)), turn_ref, turned_ref)
+    turned_rows(piece_views((p0, p1, p2, p3), size, (2, 2, 0, 0)), turn_ref, turned_ref)
     for distance in range(turned_ref.shape[1] // width):
         owner = me ^ distance
         piece = turned_ref.at[:, distance * width : (distance + 1) * width]
@@ -473,8 +477,10 @@
     own_refs = list(out_refs)
     for at, dec_ref in enumerate(dec_refs):
         count = dec_ref.shape[0]
-        out_refs[at][:count, :] = dec_ref[...]
-        own_refs[at] = out_refs[at].at[count:]
+        start = padded_rows(count)
+        out_refs[at][...] = jnp.zeros(out_refs[at].shape, out_refs[at].dtype)
+        out_refs[at][:count, :] = dec_ref[...].astype(out_refs[at].dtype)
+        own_refs[at] = out_refs[at].at[start : start + count // PAIR]
     tap_sums(channels, factor, slabs, me_ref, padded_ref, (shifted_ref,), own_refs, sums_ref, flat_ref)
 
 
@@ -514,31 +520,17 @@
     return lax.psum_scatter(mine, "dp", scatter_dimension=0, tiled=True)
 
 
-def put_kernel(sections, me_ref, first_ref, second_ref, enc_out, dec_out, none_ref, sems):
-    none_ref[...] = jnp.zeros_like(none_ref)
+def put_kernel(sections, me_ref, back_ref, first_ref, second_ref, enc_out, dec_out):
+    width = enc_out.shape[1]
     section = me_ref[2]
-    last = section == sections - 1
     even = (section & 1) == 0
-
-    def put(case, enc_from, dec_from):
-        @pl.when(case)
-        def _():
-            copies = (
-                pltpu.make_async_copy(enc_from, enc_out, sems.at[0]),
-                pltpu.make_async_copy(dec_from, dec_out, sems.at[1]),
-            )
-            for copy in copies:
-                copy.start()
-            for copy in copies:
-                copy.wait()
-
-    inner = (section > 0) & jnp.logical_not(last)
-    put((section == 0) & jnp.logical_not(last), none_ref, first_ref)
-    put(inner & even, second_ref, first_ref)
-    put(inner & jnp.logical_not(even), first_ref, second_ref)
-    put(last & even & (section > 0), second_ref, none_ref)
-    put(last & jnp.logical_not(even), first_ref, none_ref)
-    put(last & (section == 0), none_ref, none_ref)
+    both = jnp.concatenate([first_ref[...], second_ref[...]], axis=1)
+    both = jnp.dot(back_ref[...], both, preferred_element_type=F32)
+    first, second = both[:, :width], both[:, width:]
+    enc = jnp.where(even, second, first)
+    dec = jnp.where(even, first, second)
+    enc_out[...] = jnp.where(section == 0, 0.0, enc).astype(BF16)
+    dec_out[...] = jnp.where(section == sections - 1, 0.0, dec).astype(BF16)
 
 
 def finish_kernel(kept_ref, received_ref, *outs):
@@ -546,10 +538,11 @@
     for out in outs:
         lanes = kept_ref.shape[1]
         count = out.shape[1] // lanes
-        total = kept_ref[first : first + count, :] + received_ref[first : first + count, :]
+        end = first + padded_rows(count)
+        total = kept_ref[first:end, :] + received_ref[first:end, :].astype(F32)
         for row in range(count):
             out[:, row * lanes : (row + 1) * lanes] = total[row : row + 1]
-        first += count
+        first = end
 
 
 def body(
@@ -573,7 +566,6 @@
     )
     enc_far = swapped(enc_raw, far)
     enc_near = swapped(enc_raw, near)
-    cot_far = swapped(cot_raw, far)
 
     square = shape((size, size), BF16)
     matrix = shape((TAPS * rows, TAPS * rows), BF16)
@@ -601,11 +593,11 @@
         ),
         me,
     )
-    others_far = swapped(mine[size:], far)
+    pair_far = swapped(mine[: 2 * size], far)
     others_near = swapped(mine, near)
     enc_relay = swapped(enc_far, near)
-    cot_relay = swapped(cot_far, near)
-    others_relay = swapped(others_far, near)
+    flip_banded, up_banded, down_banded = call(weights_kernel, (matrix, matrix, matrix), [wide])(dec_taps)
+    pair_relay = swapped(pair_far, near)
 
     shifted_shape = (depth, TAPS * rows, width)
     cell_shape = (depth, rows, width)
@@ -623,15 +615,15 @@
             shape((channels, 128), F32),
         ),
         [turned, parts, pre, line_sums],
-    )(me, enc_own, enc_near, enc_far, enc_relay, enc_banded, turn, back, columns)
-    flip_banded, up_banded, down_banded = call(weights_kernel, (matrix, matrix, matrix), [wide], 1)(dec_taps, scale)
-
+    )(me, enc_own, enc_near, enc_far, enc_relay, enc_banded, turn, columns)
+    deep_far = swapped(lax.optimization_barrier((deep_raw, scale))[0], far)
+    deep_relay = swapped(deep_far, near)
     skip_grad, cot = call(
         functools.partial(skip_grad_kernel, size),
         (shape(cell_shape, BF16), shape(cell_shape, BF16)),
         [pltpu.VMEM(shifted_shape, BF16), turned, parts],
         1,
-    )(me, mine, others_near, cot_far, cot_relay, flip_banded, turn, scale)
+    )(me, mine, others_near, pair_far, pair_relay, flip_banded, turn, scale)
 
     first, second, up, down = call(
         functools.partial(dec_kernel, channels, size),
@@ -639,13 +631,16 @@
         [turned, parts, pre, line_sums],
         1,
     )(
-        me, mine, others_near, others_far, others_relay, skip, up_banded, down_banded, turn, back, columns,
+        me, mine, others_near, pair_far, pair_relay, skip, up_banded, down_banded, turn, columns,
         skip_own, skip_grad,
     )
     first = paired(first, 0)
 
     flat_rows = TAPS * TAPS * TAPS * channels * channels // 128
     pair = halves(flat_rows) and halves(2 * flat_rows)
+
+    dec_rows, enc_rows = 2 * flat_rows // (PAIR * slabs), flat_rows // (PAIR * slabs)
+    both_rows = padded_rows(dec_rows) + padded_rows(enc_rows)
 
     def grad_shapes(total):
         if not pair:
@@ -665,32 +660,24 @@
     second = paired(lax.optimization_barrier((second, dec_flat[0]))[0], 1)
     enc_flat = call(
         functools.partial(enc_grad_kernel, channels, factor, slabs),
-        tuple(shape((3 * flat_rows // (PAIR * slabs), 128), F32) for _ in range(PAIR))
+        (shape((both_rows, 128), F32), shape((both_rows, 128), BF16))
         if pair
         else grad_shapes(flat_rows),
         [turned, pre, line_sums, *grad_scratch(flat_rows, 1)],
         0 if pair else 1,
     )(
-        me, mine, others_near, others_far, others_relay, turn, skip_grad, hat, scale, columns, enc_shifted,
+        me, mine, others_near, deep_far, deep_relay, turn, skip_grad, hat, scale, columns, enc_shifted,
         *dec_flat,
     )
 
     moved = jax.ShapeDtypeStruct((size, width), BF16)
     enc_handoff, dec_handoff = call(
-        functools.partial(put_kernel, lax.axis_size("section")),
-        (moved, moved),
-        [pltpu.VMEM((size, width), BF16), pltpu.SemaphoreType.DMA((2,))],
-        1,
-        None,
-        (pl.BlockSpec(memory_space=pl.ANY),) * 2,
-    )(me, first, second, enc_flat[0])
+        functools.partial(put_kernel, lax.axis_size("section")), (moved, moved), [], 1
+    )(me, back, first, second, enc_flat[0])
     if pair:
         kept, sent = enc_flat
         received = lax.ppermute(sent, "dp", [(0, 1), (1, 0)])
-        ends = tuple(
-            jax.ShapeDtypeStruct((1, rows * 128), F32)
-            for rows in (dec_flat[0].shape[0], kept.shape[0] - dec_flat[0].shape[0])
-        )
+        ends = tuple(jax.ShapeDtypeStruct((1, count * 128), F32) for count in (dec_rows, enc_rows))
         grads = call(finish_kernel, ends, [])(kept, received)
     else:
         grads = [scattered(dec_flat[0]), scattered(enc_flat[0])]

time: 47.7 us -> 51.2 us (1.073)
  waiting for transfers between devices: 11.9 us -> 16.5 us
  starting transfers between devices: 10.6 us -> 9.99 us
    ppermute x8, waiting for transfers between devices: 9.39 us -> 13.2 us  [swapped(): lax.ppermute(block, 'space', [(i, i ^ distance) for i in range(count)])]
    ppermute x1, starting transfers between devices: 1.55 us -> 0.61 us  [body(): received = lax.ppermute(sent, 'dp', [(0, 1), (1, 0)])]
    ppermute x1, waiting for transfers between devices: 2.56 us -> 3.28 us  [body(): received = lax.ppermute(sent, 'dp', [(0, 1), (1, 0)])]
  transfers between devices with their start and end apart: 11 -> 11, of which waited for: 4 -> 4; matrix products, arithmetic and copies ran while one was open for 0% -> 0% of each run, Pallas kernels for 28% -> 40%
where the time goes in v4:
time: 51.2 us; the launch traced here: 51 us
  Pallas kernels  23.7 us (46%)
  waiting for transfers between devices  16.5 us (32%)
  starting transfers between devices  9.99 us (20%)
  between operations  0.75 us (1%)
    ppermute x8, waiting for transfers between devices, swapped(): lax.ppermute(block, 'space', [(i, i ^ distance) for i in range(count)])  13.2 us
    ppermute x8, starting transfers between devices, swapped(): lax.ppermute(block, 'space', [(i, i ^ distance) for i in range(count)])  5.97 us
    pallas_call x1, Pallas kernels, body(): call(functools.partial(dec_kernel, channels, size), (shape((size, width),...  4.6 us
    pallas_call x1, Pallas kernels, body(): call(functools.partial(enc_kernel, channels), (shape(shifted_shape, BF16)...  3.97 us
    pallas_call x1, Pallas kernels, body(): call(functools.partial(enc_grad_kernel, channels, factor, slabs), (shape(...  3.75 us
    ppermute x2, starting transfers between devices, paired(): return lax.ppermute(block, ('section', 'dp'), route)  3.4 us
    ppermute x1, waiting for transfers between devices, body(): received = lax.ppermute(sent, 'dp', [(0, 1), (1, 0)])  3.28 us
    pallas_call x1, Pallas kernels, body(): call(functools.partial(skip_grad_kernel, size), (shape(cell_shape, BF16),...  2.96 us
  transfers between devices with their start and end apart: 11, of which 4 were waited for; matrix products, arithmetic and copies ran while one was open for 0% of the time, Pallas kernels for 40%

profile of v4, /device:TPU:0, one launch (start us, length us, event | category | flops | bytes accessed | tf_op | source)
XLA Modules:
  0.0 51.0 jit_solution(3202938087983346053)
XLA Ops:
  0.6 0.0 copy-start
  0.6 0.1 pad_add_fusion.refs_10_.refs_0_
  0.7 2.3 %shard_map.129 = (bf16[768,768]{1,0:T(8,128)(2,1)S(1)}, bf16[512,512]{1,0:T(8,128)(2,1)S(1)}, bf16[512,512]{1,0:T(8,128)(2,1)S(1)}, f32[4,32,128]{2,1,0:T(8,128)...) custom-call(bf16[27,32,32]{2,1,0:T(8,128)(2,1)} %bitcast.11, ...), custom_call_target="tpu_custom_call" | custom-call | flops 4096 | bytes 1024 | tf_op jit(solution)/shard_map/pallas_call | solution.py:574
  3.1 0.0 copy-start.1
  3.1 3.1 %collective-permute-start.1 = (bf16[1024,128]{1,0:T(8,128)(2,1)S(1)}, bf16[1024,128]{1,0:T(8,128)(2,1)S(1)}, u32[]{:S(2)}, u32[]{:S(2)}) collective-permute-start(bf16[1024,128]{1,0:T(8,128)(2,1)S(1)} %slice.3), channel_id=1, source_target_pairs={{0,2},{1,3},{2,0},{3,1},{4,6},{5,7},{6,4},{7,5},{8,10},{9,11},{10,... | collective-permute-start | bytes 786440 | tf_op jit(solution)/shard_map/ppermute | solution.py:489
  6.1 0.1 collective-permute-start.4
  6.2 0.0 collective-permute-start
  6.2 0.5 collective-permute-start.3
  6.7 8.5 %collective-permute-done.4.refs_3_ = bf16[512,128]{1,0:T(8,128)(2,1)S(1)} collective-permute-done((bf16[512,128]{1,0:T(8,128)(2,1)S(1)}, bf16[512,128]{1,0:T(8,128)(2,1)S(1)}, u32[]{:S(2)}, u32[]{:S(2)}) %collective-permute-start.4) | collective-permute-done | bytes 131104 | tf_op jit(solution)/shard_map/ppermute | solution.py:489
  15.3 0.0 collective-permute-start.5
  15.3 0.0 collective-permute-done.1.refs_3_
  15.3 0.5 collective-permute-start.2
  15.8 0.0 collective-permute-done.3.refs_2_
  15.8 0.8 %collective-permute-done.5.refs_4_ = bf16[512,128]{1,0:T(8,128)(2,1)S(1)} collective-permute-done((bf16[512,128]{1,0:T(8,128)(2,1)S(1)}, bf16[512,128]{1,0:T(8,128)(2,1)S(1)}, u32[]{:S(2)}, u32[]{:S(2)}) %collective-permute-start.5) | collective-permute-done | bytes 131104 | tf_op jit(solution)/shard_map/ppermute | solution.py:489
  16.6 4.0 %shard_map.130 = (bf16[8,768,128]{2,1,0:T(8,128)(2,1)S(1)}, f32[8,256,128]{2,1,0:T(8,128)S(1)}, bf16[8,256,128]{2,1,0:T(8,128)(2,1)S(1)}, bf16[512,128]{1,0:T(8,128)(2,1)S(1)}, f32[32,128]{1,0:T(8,128)S(1)}) custom-call(s32[3]{0:T(128)S(1)} %pad_add_fusion.refs_10_.refs_0_, bf16[512,128]{1,0:T(8,128)(2,1)S(1)} %get-tuple-element.37.refs_1_, ...), custom_call_target="tpu_custom_call" | custom-call | flops 4096 | bytes 1024 | tf_op jit(solution)/shard_map/pallas_call | solution.py:608
  20.6 1.8 %collective-permute-start.8 = (bf16[512,128]{1,0:T(8,128)(2,1)S(1)}, bf16[512,128]{1,0:T(8,128)(2,1)S(1)}, u32[]{:S(2)}, u32[]{:S(2)}) collective-permute-start(bf16[512,128]{1,0:T(8,128)(2,1)S(1)} %bitcast.19), channel_id=1, source_target_pairs={{0,2},{1,3},{2,0},{3,1},{4,6},{5,7},{6,4},{7,5},{8,10},{9,11},{10,... | collective-permute-start | bytes 393224 | tf_op jit(solution)/shard_map/ppermute | solution.py:489
  22.4 3.8 %collective-permute-done.8.refs_3_ = bf16[512,128]{1,0:T(8,128)(2,1)S(1)} collective-permute-done((bf16[512,128]{1,0:T(8,128)(2,1)S(1)}, bf16[512,128]{1,0:T(8,128)(2,1)S(1)}, u32[]{:S(2)}, u32[]{:S(2)}) %collective-permute-start.8) | collective-permute-done | bytes 131104 | tf_op jit(solution)/shard_map/ppermute | solution.py:489
  26.2 0.0 collective-permute-start.9
  26.2 1.9 %shard_map.131 = (bf16[768,768]{1,0:T(8,128)(2,1)S(1)}, bf16[768,768]{1,0:T(8,128)(2,1)S(1)}, bf16[768,768]{1,0:T(8,128)(2,1)S(1)}) custom-call(bf16[27,32,64]{2,1,0:T(8,128)(2,1)S(1)} %get-tuple-element.42.refs_0_), custom_call_target="tpu_custom_call" | custom-call | flops 4096 | bytes 1024 | tf_op jit(solution)/shard_map/pallas_call | solution.py:599
  28.1 0.0 collective-permute-done.refs_2_
  28.1 0.0 collective-permute-done.2.refs_4_
  28.1 3.0 %shard_map.132 = (bf16[8,256,128]{2,1,0:T(8,128)(2,1)S(1)}, bf16[8,256,128]{2,1,0:T(8,128)(2,1)S(1)}) custom-call(s32[3]{0:T(128)S(1)} %pad_add_fusion.refs_10_.refs_0_, bf16[1536,128]{1,0:T(8,128)(2,1)S(1)} %get-tuple-element.36.refs_1_, bf16[1536,128]{1,0:T(8,128)(2,1)S(1)} %collective-permute-done.refs_2_, ...), custom_call_target="tpu_custom_call" | custom-call | flops 4096 | bytes 1024 | tf_op jit(solution)/shard_map/pallas_call | solution.py:621
  31.1 4.6 %shard_map.133 = (bf16[512,128]{1,0:T(8,128)(2,1)S(1)}, bf16[512,128]{1,0:T(8,128)(2,1)S(1)}, bf16[8,768,128]{2,1,0:T(8,128)(2,1)S(1)}, bf16[8,768,128]{2,1,0:T(8,128)(2,1)S(1)}) custom-call(s32[3]{0:T(128)S(1)} %pad_add_fusion.refs_10_.refs_0_, bf16[1536,128]{1,0:T(8,128)(2,1)S(1)} %get-tuple-element.36.refs_1_, ...), custom_call_target="tpu_custom_call" | custom-call | flops 4096 | bytes 1024 | tf_op jit(solution)/shard_map/pallas_call | solution.py:628
  35.7 1.9 %collective-permute-start.6 = (bf16[512,128]{1,0:T(8,128)(2,1)S(1)}, bf16[512,128]{1,0:T(8,128)(2,1)S(1)}, u32[]{:S(2)}, u32[]{:S(2)}) collective-permute-start(bf16[512,128]{1,0:T(8,128)(2,1)S(1)} %get-tuple-element.49), channel_id=1, source_target_pairs={{0,8},{4,12},{8,0},{12,4},{16,24},{20,28},{24,16},{28,20},{1,9},{5... | collective-permute-start | bytes 393224 | tf_op jit(solution)/shard_map/ppermute | solution.py:502
  37.6 2.6 %shard_map.134 = (f32[54,128]{1,0:T(8,128)S(1)}, f32[54,128]{1,0:T(8,128)S(1)}) custom-call(s32[3]{0:T(128)S(1)} %pad_add_fusion.refs_10_.refs_0_, bf16[8,256,128]{2,1,0:T(8,128)(2,1)S(1)} %get-tuple-element.51.refs_1_, bf16[8,768,128]{2,1,0:T(8,128)(2,1)S(1)} %get-tuple-element.52.refs_2_, bf16[8,768,128]{2,1,0:T(8,128)(2,1)S(1)} %get-tuple-element.53.refs_3_), custom_call_target="tpu_custom_call" | custom-call | flops 4096 | bytes 1024 | tf_op jit(solution)/shard_map/pallas_call | solution.py:655
  40.2 1.5 %collective-permute-start.7 = (bf16[512,128]{1,0:T(8,128)(2,1)S(1)}, bf16[512,128]{1,0:T(8,128)(2,1)S(1)}, u32[]{:S(2)}, u32[]{:S(2)}) collective-permute-start(bf16[512,128]{1,0:T(8,128)(2,1)S(1)} %get-tuple-element.55), channel_id=1, source_target_pairs={{0,4},{4,0},{8,16},{12,20},{16,8},{20,12},{24,28},{28,24},{1,5},{5... | collective-permute-start | bytes 393224 | tf_op jit(solution)/shard_map/ppermute | solution.py:502
  41.7 3.7 %shard_map.135 = (f32[96,128]{1,0:T(8,128)S(1)}, bf16[96,128]{1,0:T(8,128)(2,1)S(1)}) custom-call(s32[3]{0:T(128)S(1)} %pad_add_fusion.refs_10_.refs_0_, bf16[1536,128]{1,0:T(8,128)(2,1)S(1)} %get-tuple-element.36.refs_1_, bf16[1536,128]{1,0:T(8,128)(2,1)S(1)} %collective-permute-done.refs_2_, bf16[512,128]{1,0:T(8,128)(2,1)S(1)} %collective-permute-done.8.refs_3_, ...), custom_call_target="tpu_custom_call" | custom-call | flops 4096 | bytes 1024 | tf_op jit(solution)/shard_map/pallas_call | solution.py:661
  45.5 0.6 %collective-permute-start.10 = (bf16[96,128]{1,0:T(8,128)(2,1)S(1)}, bf16[96,128]{1,0:T(8,128)(2,1)S(1)}, u32[]{:S(2)}, u32[]{:S(2)}) collective-permute-start(bf16[96,128]{1,0:T(8,128)(2,1)S(1)} %get-tuple-element.63), channel_id=1, source_target_pairs={{0,4},{4,0},{1,5},{5,1},{2,6},{6,2},{3,7},{7,3},{8,12},{12,8},{9,1... | collective-permute-start | bytes 73736 | tf_op jit(solution)/shard_map/ppermute | solution.py:679
  46.1 3.3 %collective-permute-done.10.refs_1_ = bf16[96,128]{1,0:T(8,128)(2,1)S(1)} collective-permute-done((bf16[96,128]{1,0:T(8,128)(2,1)S(1)}, bf16[96,128]{1,0:T(8,128)(2,1)S(1)}, u32[]{:S(2)}, u32[]{:S(2)}) %collective-permute-start.10) | collective-permute-done | bytes 24608 | tf_op jit(solution)/shard_map/ppermute | solution.py:679
  49.4 0.6 %shard_map.137 = (f32[1,6912]{1,0:T(1,128)}, f32[1,3456]{1,0:T(1,128)}) custom-call(f32[96,128]{1,0:T(8,128)S(1)} %get-tuple-element.60.refs_4_.refs_0_, bf16[96,128]{1,0:T(8,128)(2,1)S(1)} %collective-permute-done.10.refs_1_), custom_call_target="tpu_custom_call" | custom-call | flops 4096 | bytes 1024 | tf_op jit(solution)/shard_map/pallas_call | solution.py:681
  50.0 0.0 collective-permute-done.6.refs_2_
  50.0 1.0 %shard_map.136 = (bf16[512,128]{1,0:T(8,128)(2,1)}, bf16[512,128]{1,0:T(8,128)(2,1)}) custom-call(s32[3]{0:T(128)S(1)} %pad_add_fusion.refs_10_.refs_0_, bf16[512,512]{1,0:T(8,128)(2,1)S(1)} %get-tuple-element.35.refs_1_, bf16[512,128]{1,0:T(8,128)(2,1)S(1)} %collective-permute-done.6.refs_2_, bf16[512,128]{1,0:T(8,128)(2,1)S(1)} %collective-permute-done.7.refs_3_, ...), custom_call_target="tpu_custom_call" | custom-call | flops 4096 | bytes 1024 | tf_op jit(solution)/shard_map/pallas_call | solution.py:674
  (5 shorter events, 0.0 us)
Async XLA Ops:
  0.6 5.5 %copy-start = (bf16[1,1,32,2,8,128]{5,4,3,2,1,0:T(8,128)(2,1)S(1)}, bf16[1,1,32,2,8,128]{5,4,3,2,1,0:T(8,128)(2,1)}, u32[]{:S(2)}) copy-start(bf16[1,1,32,2,8,128]{5,4,3,2,1,0:T(8,128)(2,1)} %param.10) | copy-start | bytes 393220
  3.1 17.5 %copy-start.1 = (bf16[1,1,32,2,8,128]{5,4,3,2,1,0:T(8,128)(2,1)S(1)}, bf16[1,1,32,2,8,128]{5,4,3,2,1,0:T(8,128)(2,1)}, u32[]{:S(2)}) copy-start(bf16[1,1,32,2,8,128]{5,4,3,2,1,0:T(8,128)(2,1)} %param.13) | copy-start | bytes 393220
  3.1 12.2 %collective-permute-start.1 = (bf16[1024,128]{1,0:T(8,128)(2,1)S(1)}, bf16[1024,128]{1,0:T(8,128)(2,1)S(1)}, u32[]{:S(2)}, u32[]{:S(2)}) collective-permute-start(bf16[1024,128]{1,0:T(8,128)(2,1)S(1)} %slice.3), channel_id=1, source_target_pairs={{0,2},{1,3},{2,0},{3,1},{4,6},{5,7},{6,4},{7,5},{8,10},{9,11},{10,... | collective-permute-start | bytes 786440 | tf_op jit(solution)/shard_map/ppermute | solution.py:489
  6.1 9.1 %collective-permute-start.4 = (bf16[512,128]{1,0:T(8,128)(2,1)S(1)}, bf16[512,128]{1,0:T(8,128)(2,1)S(1)}, u32[]{:S(2)}, u32[]{:S(2)}) collective-permute-start(bf16[512,128]{1,0:T(8,128)(2,1)S(1)} %bitcast.16), channel_id=1, source_target_pairs={{0,2},{1,3},{2,0},{3,1},{4,6},{5,7},{6,4},{7,5},{8,10},{9,11},{10,... | collective-permute-start | bytes 393224 | tf_op jit(solution)/shard_map/ppermute | solution.py:489
  6.2 21.9 %collective-permute-start = (bf16[1536,128]{1,0:T(8,128)(2,1)S(1)}, bf16[1536,128]{1,0:T(8,128)(2,1)S(1)}, u32[]{:S(2)}, u32[]{:S(2)}) collective-permute-start(bf16[1536,128]{1,0:T(8,128)(2,1)S(1)} %get-tuple-element.36.refs_1_), channel_id=1, source_target_pairs={{0,1},{1,0},{2,3},{3,2},{4,5},{5,4},{6,7},{7,6},{8,9},{9,8},{10,11... | collective-permute-start | bytes 1179656 | tf_op jit(solution)/shard_map/ppermute | solution.py:489
  6.2 9.5 %collective-permute-start.3 = (bf16[512,128]{1,0:T(8,128)(2,1)S(1)}, bf16[512,128]{1,0:T(8,128)(2,1)S(1)}, u32[]{:S(2)}, u32[]{:S(2)}) collective-permute-start(bf16[512,128]{1,0:T(8,128)(2,1)S(1)} %bitcast.17), channel_id=1, source_target_pairs={{0,1},{1,0},{2,3},{3,2},{4,5},{5,4},{6,7},{7,6},{8,9},{9,8},{10,11... | collective-permute-start | bytes 393224 | tf_op jit(solution)/shard_map/ppermute | solution.py:489
  15.3 1.3 %collective-permute-start.5 = (bf16[512,128]{1,0:T(8,128)(2,1)S(1)}, bf16[512,128]{1,0:T(8,128)(2,1)S(1)}, u32[]{:S(2)}, u32[]{:S(2)}) collective-permute-start(bf16[512,128]{1,0:T(8,128)(2,1)S(1)} %collective-permute-done.4.refs_3_), channel_id=1, source_target_pairs={{0,1},{1,0},{2,3},{3,2},{4,5},{5,4},{6,7},{7,6},{8,9},{9,8},{10,11... | collective-permute-start | bytes 393224 | tf_op jit(solution)/shard_map/ppermute | solution.py:489
  15.3 12.9 %collective-permute-start.2 = (bf16[1024,128]{1,0:T(8,128)(2,1)S(1)}, bf16[1024,128]{1,0:T(8,128)(2,1)S(1)}, u32[]{:S(2)}, u32[]{:S(2)}) collective-permute-start(bf16[1024,128]{1,0:T(8,128)(2,1)S(1)} %collective-permute-done.1.refs_3_), channel_id=1, source_target_pairs={{0,1},{1,0},{2,3},{3,2},{4,5},{5,4},{6,7},{7,6},{8,9},{9,8},{10,11... | collective-permute-start | bytes 786440 | tf_op jit(solution)/shard_map/ppermute | solution.py:489
  20.6 5.6 %collective-permute-start.8 = (bf16[512,128]{1,0:T(8,128)(2,1)S(1)}, bf16[512,128]{1,0:T(8,128)(2,1)S(1)}, u32[]{:S(2)}, u32[]{:S(2)}) collective-permute-start(bf16[512,128]{1,0:T(8,128)(2,1)S(1)} %bitcast.19), channel_id=1, source_target_pairs={{0,2},{1,3},{2,0},{3,1},{4,6},{5,7},{6,4},{7,5},{8,10},{9,11},{10,... | collective-permute-start | bytes 393224 | tf_op jit(solution)/shard_map/ppermute | solution.py:489
  26.2 15.5 %collective-permute-start.9 = (bf16[512,128]{1,0:T(8,128)(2,1)S(1)}, bf16[512,128]{1,0:T(8,128)(2,1)S(1)}, u32[]{:S(2)}, u32[]{:S(2)}) collective-permute-start(bf16[512,128]{1,0:T(8,128)(2,1)S(1)} %collective-permute-done.8.refs_3_), channel_id=1, source_target_pairs={{0,1},{1,0},{2,3},{3,2},{4,5},{5,4},{6,7},{7,6},{8,9},{9,8},{10,11... | collective-permute-start | bytes 393224 | tf_op jit(solution)/shard_map/ppermute | solution.py:489
  35.7 14.3 %collective-permute-start.6 = (bf16[512,128]{1,0:T(8,128)(2,1)S(1)}, bf16[512,128]{1,0:T(8,128)(2,1)S(1)}, u32[]{:S(2)}, u32[]{:S(2)}) collective-permute-start(bf16[512,128]{1,0:T(8,128)(2,1)S(1)} %get-tuple-element.49), channel_id=1, source_target_pairs={{0,8},{4,12},{8,0},{12,4},{16,24},{20,28},{24,16},{28,20},{1,9},{5... | collective-permute-start | bytes 393224 | tf_op jit(solution)/shard_map/ppermute | solution.py:502
  40.2 9.8 %collective-permute-start.7 = (bf16[512,128]{1,0:T(8,128)(2,1)S(1)}, bf16[512,128]{1,0:T(8,128)(2,1)S(1)}, u32[]{:S(2)}, u32[]{:S(2)}) collective-permute-start(bf16[512,128]{1,0:T(8,128)(2,1)S(1)} %get-tuple-element.55), channel_id=1, source_target_pairs={{0,4},{4,0},{8,16},{12,20},{16,8},{20,12},{24,28},{28,24},{1,5},{5... | collective-permute-start | bytes 393224 | tf_op jit(solution)/shard_map/ppermute | solution.py:502
  45.5 3.9 %collective-permute-start.10 = (bf16[96,128]{1,0:T(8,128)(2,1)S(1)}, bf16[96,128]{1,0:T(8,128)(2,1)S(1)}, u32[]{:S(2)}, u32[]{:S(2)}) collective-permute-start(bf16[96,128]{1,0:T(8,128)(2,1)S(1)} %get-tuple-element.63), channel_id=1, source_target_pairs={{0,4},{4,0},{1,5},{5,1},{2,6},{6,2},{3,7},{7,3},{8,12},{12,8},{9,1... | collective-permute-start | bytes 73736 | tf_op jit(solution)/shard_map/ppermute | solution.py:679

commit v5 on v4

--- a/solution.py
+++ b/solution.py
@@ -13,6 +13,8 @@
 TAPS = 3
 PAIR = 2
 ROWS = 16
+GROUP = 8
+HEIGHTS = 4
 LIMIT = 12 * 1024 * 1024
 BF16 = jnp.bfloat16
 F32 = jnp.float32
@@ -208,17 +210,19 @@
         parts_ref[0, tap] = jnp.zeros((rows, width), F32)
         parts_ref[depth + 1, tap] = jnp.zeros((rows, width), F32)
 
-    @pl.loop(0, depth // 2)
+    group = GROUP if depth % GROUP == 0 else 1
+
+    @pl.loop(0, depth // group)
     def _(step):
         total = None
         for weights_ref, shifted_ref in pairs:
-            cells = jnp.concatenate([shifted_ref[2 * step], shifted_ref[2 * step + 1]], axis=1)
+            cells = jnp.concatenate([shifted_ref[group * step + inner] for inner in range(group)], axis=1)
             product = jnp.dot(weights_ref[...], cells, preferred_element_type=F32)
             total = product if total is None else total + product
         for tap in range(TAPS):
             block = total[tap * rows : (tap + 1) * rows]
-            parts_ref[2 * step + 1, tap] = block[:, :width]
-            parts_ref[2 * step + 2, tap] = block[:, width:]
+            for inner in range(group):
+                parts_ref[group * step + 1 + inner, tap] = block[:, inner * width : (inner + 1) * width]
 
 
 def combined(parts_ref, layer):
@@ -243,16 +247,23 @@
     depth, rows, width = pre_ref.shape
     sums_ref[...] = jnp.zeros_like(sums_ref)
 
-    @pl.loop(0, depth)
-    def _(layer):
-        pre = combined(parts_ref, layer)
-        pre_ref[layer] = pre
-        sums_ref[0] += pre
-        sums_ref[1] += pre * pre
+    @pl.loop(0, rows // channels)
+    def _(height):
+        part = pl.ds(pl.multiple_of(height * channels, channels), channels)
+        total, squares = jnp.zeros((channels, width), F32), jnp.zeros((channels, width), F32)
+        for layer in range(depth):
+            pre = parts_ref[layer, 0, part, :]
+            for tap in range(1, TAPS):
+                pre = pre + parts_ref[layer + tap, tap, part, :]
+            pre_ref[layer, part, :] = pre
+            total = total + pre
+            squares = squares + pre * pre
+        sums_ref[0] += total
+        sums_ref[1] += squares
 
     cells = depth * (rows // channels) * width
-    mean = over_channels(sums_ref[0], channels) * (1.0 / cells)
-    square = over_channels(sums_ref[1], channels) * (1.0 / cells)
+    mean = jnp.sum(sums_ref[0], axis=1, keepdims=True) * (1.0 / cells)
+    square = jnp.sum(sums_ref[1], axis=1, keepdims=True) * (1.0 / cells)
     return mean, lax.rsqrt(square - mean * mean + EPS)
 
 
@@ -270,8 +281,7 @@
     means, scales = tiled(mean, count), tiled(scale, count)
     gains, biases = tiled(columns_ref[0, :, :1], count), tiled(columns_ref[1, :, :1], count)
 
-    @pl.loop(0, depth)
-    def _(layer):
+    for layer in range(depth):
         hat = (pre_ref[layer] - means) * scales
         hat_ref[layer] = hat
         skip_ref[layer] = jnp.maximum(gains * hat + biases, 0.0).astype(BF16)
@@ -341,26 +351,28 @@
     rows = shifted_refs[0].shape[1] // TAPS
     lanes = len(shifted_refs) * TAPS * channels
 
-    @pl.loop(0, rows // channels)
-    def _(height):
+    every = rows // channels
+    group = HEIGHTS * len(shifted_refs)
+    group = group if every % group == 0 else 1
+
+    @pl.loop(0, every // group)
+    def _(step):
+        heights = [group * step + inner for inner in range(group)]
         left = []
         for depth_tap, height_tap in outers:
-            first = pl.multiple_of((height + 2 - height_tap) * channels, channels)
-            left.append(
-                jnp.concatenate(
-                    [padded_ref[layer + 2 - depth_tap, pl.ds(first, channels), :] for layer in range(depth)],
-                    axis=1,
-                )
-            )
+            cells = []
+            for height in heights:
+                first = pl.multiple_of((height + 2 - height_tap) * channels, channels)
+                cells += [padded_ref[layer + 2 - depth_tap, pl.ds(first, channels), :] for layer in range(depth)]
+            left.append(jnp.concatenate(cells, axis=1))
         right = []
         for width_tap in range(TAPS):
             for shifted_ref in shifted_refs:
-                first = pl.multiple_of(width_tap * rows + height * channels, channels)
-                right.append(
-                    jnp.concatenate(
-                        [shifted_ref[layer, pl.ds(first, channels), :] for layer in range(depth)], axis=1
-                    )
-                )
+                cells = []
+                for height in heights:
+                    first = pl.multiple_of(width_tap * rows + height * channels, channels)
+                    cells += [shifted_ref[layer, pl.ds(first, channels), :] for layer in range(depth)]
+                right.append(jnp.concatenate(cells, axis=1))
         product = lax.dot_general(
             jnp.concatenate(left, axis=0),
             jnp.concatenate(right, axis=0),
@@ -370,7 +382,7 @@
         for tile in range(sums_ref.shape[0]):
             block = product[:, tile * 128 : min(lanes, (tile + 1) * 128)]
             old = sums_ref[tile, :, : block.shape[1]]
-            sums_ref[tile, :, : block.shape[1]] = jnp.where(height == 0, 0.0, old) + block
+            sums_ref[tile, :, : block.shape[1]] = jnp.where(step == 0, 0.0, old) + block
 
 
 def flattened(channels, sources, factor, sums_ref, flat_ref):
@@ -605,6 +617,7 @@
     parts = pltpu.VMEM((depth + 2, TAPS, rows, width), F32)
     padded = pltpu.VMEM((depth + 2, rows + 2 * channels, width), BF16)
     pre, line_sums = pltpu.VMEM(cell_shape, F32), pltpu.VMEM((2, rows, width), F32)
+    channel_sums = pltpu.VMEM((2, channels, width), F32)
     enc_shifted, hat, skip, skip_own, scale = call(
         functools.partial(enc_kernel, channels),
         (
@@ -614,7 +627,7 @@
             shape((size, width), BF16),
             shape((channels, 128), F32),
         ),
-        [turned, parts, pre, line_sums],
+        [turned, parts, pre, channel_sums],
     )(me, enc_own, enc_near, enc_far, enc_relay, enc_banded, turn, columns)
     deep_far = swapped(lax.optimization_barrier((deep_raw, scale))[0], far)
     deep_relay = swapped(deep_far, near)
@@ -628,7 +641,7 @@
     first, second, up, down = call(
         functools.partial(dec_kernel, channels, size),
         (shape((size, width), BF16),) * 2 + (shape(shifted_shape, BF16),) * 2,
-        [turned, parts, pre, line_sums],
+        [turned, parts, pre, channel_sums],
         1,
     )(
         me, mine, others_near, pair_far, pair_relay, skip, up_banded, down_banded, turn, columns,

time: 51.2 us -> 46.5 us (0.908)
  Pallas kernels: 23.7 us -> 19.1 us
    pallas_call x1, Pallas kernels: 2.61 us -> 1.46 us  [body(): call(functools.partial(dec_grad_kernel, channels, factor, slabs), grad_sh...]
    pallas_call x1, Pallas kernels: 4.6 us -> 3.58 us  [body(): call(functools.partial(dec_kernel, channels, size), (shape((size, width),...]
    pallas_call x1, Pallas kernels: 3.97 us -> 2.95 us  [body(): call(functools.partial(enc_kernel, channels), (shape(shifted_shape, BF16)...]
    pallas_call x1, Pallas kernels: 3.75 us -> 2.8 us  [body(): call(functools.partial(enc_grad_kernel, channels, factor, slabs), (shape(...]
    pallas_call x1, Pallas kernels: 2.96 us -> 2.43 us  [body(): call(functools.partial(skip_grad_kernel, size), (shape(cell_shape, BF16),...]
  transfers between devices with their start and end apart: 11 -> 11, of which waited for: 4 -> 4; matrix products, arithmetic and copies ran while one was open for 0% -> 0% of each run, Pallas kernels for 40% -> 34%
where the time goes in v5:
time: 46.5 us; the launch traced here: 46.4 us
  Pallas kernels  19.1 us (41%)
  waiting for transfers between devices  16.5 us (35%)
  starting transfers between devices  9.98 us (21%)
  between operations  0.75 us (2%)
    ppermute x8, waiting for transfers between devices, swapped(): lax.ppermute(block, 'space', [(i, i ^ distance) for i in range(count)])  13.2 us
    ppermute x8, starting transfers between devices, swapped(): lax.ppermute(block, 'space', [(i, i ^ distance) for i in range(count)])  5.97 us
    pallas_call x1, Pallas kernels, body(): call(functools.partial(dec_kernel, channels, size), (shape((size, width),...  3.58 us
    ppermute x2, starting transfers between devices, paired(): return lax.ppermute(block, ('section', 'dp'), route)  3.41 us
    ppermute x1, waiting for transfers between devices, body(): received = lax.ppermute(sent, 'dp', [(0, 1), (1, 0)])  3.29 us
    pallas_call x1, Pallas kernels, body(): call(functools.partial(enc_kernel, channels), (shape(shifted_shape, BF16)...  2.95 us
    pallas_call x1, Pallas kernels, body(): call(functools.partial(enc_grad_kernel, channels, factor, slabs), (shape(...  2.8 us
    pallas_call x1, Pallas kernels, body(): call(functools.partial(skip_grad_kernel, size), (shape(cell_shape, BF16),...  2.43 us
  transfers between devices with their start and end apart: 11, of which 4 were waited for; matrix products, arithmetic and copies ran while one was open for 0% of the time, Pallas kernels for 34%

profile of v5, /device:TPU:0, one launch (start us, length us, event | category | flops | bytes accessed | tf_op | source)
XLA Modules:
  0.0 46.4 jit_solution(1658090991037856860)
XLA Ops:
  0.6 0.0 copy-start
  0.6 0.1 pad_add_fusion.refs_10_.refs_0_
  0.7 2.3 %shard_map.129 = (bf16[768,768]{1,0:T(8,128)(2,1)S(1)}, bf16[512,512]{1,0:T(8,128)(2,1)S(1)}, bf16[512,512]{1,0:T(8,128)(2,1)S(1)}, f32[4,32,128]{2,1,0:T(8,128)...) custom-call(bf16[27,32,32]{2,1,0:T(8,128)(2,1)} %bitcast.11, ...), custom_call_target="tpu_custom_call" | custom-call | flops 4096 | bytes 1024 | tf_op jit(solution)/shard_map/pallas_call | solution.py:586
  3.1 0.0 copy-start.1
  3.1 3.1 %collective-permute-start.1 = (bf16[1024,128]{1,0:T(8,128)(2,1)S(1)}, bf16[1024,128]{1,0:T(8,128)(2,1)S(1)}, u32[]{:S(2)}, u32[]{:S(2)}) collective-permute-start(bf16[1024,128]{1,0:T(8,128)(2,1)S(1)} %slice.3), channel_id=1, source_target_pairs={{0,2},{1,3},{2,0},{3,1},{4,6},{5,7},{6,4},{7,5},{8,10},{9,11},{10,... | collective-permute-start | bytes 786440 | tf_op jit(solution)/shard_map/ppermute | solution.py:501
  6.1 0.1 collective-permute-start.4
  6.2 0.0 collective-permute-start
  6.2 0.5 %collective-permute-start.3 = (bf16[512,128]{1,0:T(8,128)(2,1)S(1)}, bf16[512,128]{1,0:T(8,128)(2,1)S(1)}, u32[]{:S(2)}, u32[]{:S(2)}) collective-permute-start(bf16[512,128]{1,0:T(8,128)(2,1)S(1)} %bitcast.17), channel_id=1, source_target_pairs={{0,1},{1,0},{2,3},{3,2},{4,5},{5,4},{6,7},{7,6},{8,9},{9,8},{10,11... | collective-permute-start | bytes 393224 | tf_op jit(solution)/shard_map/ppermute | solution.py:501
  6.7 8.5 %collective-permute-done.4.refs_3_ = bf16[512,128]{1,0:T(8,128)(2,1)S(1)} collective-permute-done((bf16[512,128]{1,0:T(8,128)(2,1)S(1)}, bf16[512,128]{1,0:T(8,128)(2,1)S(1)}, u32[]{:S(2)}, u32[]{:S(2)}) %collective-permute-start.4) | collective-permute-done | bytes 131104 | tf_op jit(solution)/shard_map/ppermute | solution.py:501
  15.3 0.0 collective-permute-start.5
  15.3 0.0 collective-permute-done.1.refs_3_
  15.3 0.5 %collective-permute-start.2 = (bf16[1024,128]{1,0:T(8,128)(2,1)S(1)}, bf16[1024,128]{1,0:T(8,128)(2,1)S(1)}, u32[]{:S(2)}, u32[]{:S(2)}) collective-permute-start(bf16[1024,128]{1,0:T(8,128)(2,1)S(1)} %collective-permute-done.1.refs_3_), channel_id=1, source_target_pairs={{0,1},{1,0},{2,3},{3,2},{4,5},{5,4},{6,7},{7,6},{8,9},{9,8},{10,11... | collective-permute-start | bytes 786440 | tf_op jit(solution)/shard_map/ppermute | solution.py:501
  15.8 0.0 collective-permute-done.3.refs_2_
  15.8 0.8 %collective-permute-done.5.refs_4_ = bf16[512,128]{1,0:T(8,128)(2,1)S(1)} collective-permute-done((bf16[512,128]{1,0:T(8,128)(2,1)S(1)}, bf16[512,128]{1,0:T(8,128)(2,1)S(1)}, u32[]{:S(2)}, u32[]{:S(2)}) %collective-permute-start.5) | collective-permute-done | bytes 131104 | tf_op jit(solution)/shard_map/ppermute | solution.py:501
  16.6 3.0 %shard_map.130 = (bf16[8,768,128]{2,1,0:T(8,128)(2,1)S(1)}, f32[8,256,128]{2,1,0:T(8,128)S(1)}, bf16[8,256,128]{2,1,0:T(8,128)(2,1)S(1)}, bf16[512,128]{1,0:T(8,128)(2,1)S(1)}, f32[32,128]{1,0:T(8,128)S(1)}) custom-call(s32[3]{0:T(128)S(1)} %pad_add_fusion.refs_10_.refs_0_, bf16[512,128]{1,0:T(8,128)(2,1)S(1)} %get-tuple-element.37.refs_1_, ...), custom_call_target="tpu_custom_call" | custom-call | flops 4096 | bytes 1024 | tf_op jit(solution)/shard_map/pallas_call | solution.py:621
  19.6 1.8 %collective-permute-start.8 = (bf16[512,128]{1,0:T(8,128)(2,1)S(1)}, bf16[512,128]{1,0:T(8,128)(2,1)S(1)}, u32[]{:S(2)}, u32[]{:S(2)}) collective-permute-start(bf16[512,128]{1,0:T(8,128)(2,1)S(1)} %bitcast.19), channel_id=1, source_target_pairs={{0,2},{1,3},{2,0},{3,1},{4,6},{5,7},{6,4},{7,5},{8,10},{9,11},{10,... | collective-permute-start | bytes 393224 | tf_op jit(solution)/shard_map/ppermute | solution.py:501
  21.4 3.8 %collective-permute-done.8.refs_3_ = bf16[512,128]{1,0:T(8,128)(2,1)S(1)} collective-permute-done((bf16[512,128]{1,0:T(8,128)(2,1)S(1)}, bf16[512,128]{1,0:T(8,128)(2,1)S(1)}, u32[]{:S(2)}, u32[]{:S(2)}) %collective-permute-start.8) | collective-permute-done | bytes 131104 | tf_op jit(solution)/shard_map/ppermute | solution.py:501
  25.2 0.0 collective-permute-start.9
  25.2 1.9 %shard_map.131 = (bf16[768,768]{1,0:T(8,128)(2,1)S(1)}, bf16[768,768]{1,0:T(8,128)(2,1)S(1)}, bf16[768,768]{1,0:T(8,128)(2,1)S(1)}) custom-call(bf16[27,32,64]{2,1,0:T(8,128)(2,1)S(1)} %get-tuple-element.42.refs_0_), custom_call_target="tpu_custom_call" | custom-call | flops 4096 | bytes 1024 | tf_op jit(solution)/shard_map/pallas_call | solution.py:611
  27.1 0.0 collective-permute-done.refs_2_
  27.1 0.0 collective-permute-done.2.refs_4_
  27.1 2.4 %shard_map.132 = (bf16[8,256,128]{2,1,0:T(8,128)(2,1)S(1)}, bf16[8,256,128]{2,1,0:T(8,128)(2,1)S(1)}) custom-call(s32[3]{0:T(128)S(1)} %pad_add_fusion.refs_10_.refs_0_, bf16[1536,128]{1,0:T(8,128)(2,1)S(1)} %get-tuple-element.36.refs_1_, bf16[1536,128]{1,0:T(8,128)(2,1)S(1)} %collective-permute-done.refs_2_, ...), custom_call_target="tpu_custom_call" | custom-call | flops 4096 | bytes 1024 | tf_op jit(solution)/shard_map/pallas_call | solution.py:634
  29.6 3.6 %shard_map.133 = (bf16[512,128]{1,0:T(8,128)(2,1)S(1)}, bf16[512,128]{1,0:T(8,128)(2,1)S(1)}, bf16[8,768,128]{2,1,0:T(8,128)(2,1)S(1)}, bf16[8,768,128]{2,1,0:T(8,128)(2,1)S(1)}) custom-call(s32[3]{0:T(128)S(1)} %pad_add_fusion.refs_10_.refs_0_, bf16[1536,128]{1,0:T(8,128)(2,1)S(1)} %get-tuple-element.36.refs_1_, ...), custom_call_target="tpu_custom_call" | custom-call | flops 4096 | bytes 1024 | tf_op jit(solution)/shard_map/pallas_call | solution.py:641
  33.2 1.9 %collective-permute-start.6 = (bf16[512,128]{1,0:T(8,128)(2,1)S(1)}, bf16[512,128]{1,0:T(8,128)(2,1)S(1)}, u32[]{:S(2)}, u32[]{:S(2)}) collective-permute-start(bf16[512,128]{1,0:T(8,128)(2,1)S(1)} %get-tuple-element.49), channel_id=1, source_target_pairs={{0,8},{4,12},{8,0},{12,4},{16,24},{20,28},{24,16},{28,20},{1,9},{5... | collective-permute-start | bytes 393224 | tf_op jit(solution)/shard_map/ppermute | solution.py:514
  35.0 1.5 %shard_map.134 = (f32[54,128]{1,0:T(8,128)S(1)}, f32[54,128]{1,0:T(8,128)S(1)}) custom-call(s32[3]{0:T(128)S(1)} %pad_add_fusion.refs_10_.refs_0_, bf16[8,256,128]{2,1,0:T(8,128)(2,1)S(1)} %get-tuple-element.51.refs_1_, bf16[8,768,128]{2,1,0:T(8,128)(2,1)S(1)} %get-tuple-element.52.refs_2_, bf16[8,768,128]{2,1,0:T(8,128)(2,1)S(1)} %get-tuple-element.53.refs_3_), custom_call_target="tpu_custom_call" | custom-call | flops 4096 | bytes 1024 | tf_op jit(solution)/shard_map/pallas_call | solution.py:668
  36.5 1.6 %collective-permute-start.7 = (bf16[512,128]{1,0:T(8,128)(2,1)S(1)}, bf16[512,128]{1,0:T(8,128)(2,1)S(1)}, u32[]{:S(2)}, u32[]{:S(2)}) collective-permute-start(bf16[512,128]{1,0:T(8,128)(2,1)S(1)} %get-tuple-element.55), channel_id=1, source_target_pairs={{0,4},{4,0},{8,16},{12,20},{16,8},{20,12},{24,28},{28,24},{1,5},{5... | collective-permute-start | bytes 393224 | tf_op jit(solution)/shard_map/ppermute | solution.py:514
  38.0 0.0 collective-permute-done.9.refs_4_
  38.0 2.8 %shard_map.135 = (f32[96,128]{1,0:T(8,128)S(1)}, bf16[96,128]{1,0:T(8,128)(2,1)S(1)}) custom-call(s32[3]{0:T(128)S(1)} %pad_add_fusion.refs_10_.refs_0_, bf16[1536,128]{1,0:T(8,128)(2,1)S(1)} %get-tuple-element.36.refs_1_, bf16[1536,128]{1,0:T(8,128)(2,1)S(1)} %collective-permute-done.refs_2_, bf16[512,128]{1,0:T(8,128)(2,1)S(1)} %collective-permute-done.8.refs_3_, ...), custom_call_target="tpu_custom_call" | custom-call | flops 4096 | bytes 1024 | tf_op jit(solution)/shard_map/pallas_call | solution.py:674
  40.8 0.6 %collective-permute-start.10 = (bf16[96,128]{1,0:T(8,128)(2,1)S(1)}, bf16[96,128]{1,0:T(8,128)(2,1)S(1)}, u32[]{:S(2)}, u32[]{:S(2)}) collective-permute-start(bf16[96,128]{1,0:T(8,128)(2,1)S(1)} %get-tuple-element.63), channel_id=1, source_target_pairs={{0,4},{4,0},{1,5},{5,1},{2,6},{6,2},{3,7},{7,3},{8,12},{12,8},{9,1... | collective-permute-start | bytes 73736 | tf_op jit(solution)/shard_map/ppermute | solution.py:692
  41.4 3.3 %collective-permute-done.10.refs_1_ = bf16[96,128]{1,0:T(8,128)(2,1)S(1)} collective-permute-done((bf16[96,128]{1,0:T(8,128)(2,1)S(1)}, bf16[96,128]{1,0:T(8,128)(2,1)S(1)}, u32[]{:S(2)}, u32[]{:S(2)}) %collective-permute-start.10) | collective-permute-done | bytes 24608 | tf_op jit(solution)/shard_map/ppermute | solution.py:692
  44.7 0.6 %shard_map.137 = (f32[1,6912]{1,0:T(1,128)}, f32[1,3456]{1,0:T(1,128)}) custom-call(f32[96,128]{1,0:T(8,128)S(1)} %get-tuple-element.60.refs_4_.refs_0_, bf16[96,128]{1,0:T(8,128)(2,1)S(1)} %collective-permute-done.10.refs_1_), custom_call_target="tpu_custom_call" | custom-call | flops 4096 | bytes 1024 | tf_op jit(solution)/shard_map/pallas_call | solution.py:694
  45.4 1.0 %shard_map.136 = (bf16[512,128]{1,0:T(8,128)(2,1)}, bf16[512,128]{1,0:T(8,128)(2,1)}) custom-call(s32[3]{0:T(128)S(1)} %pad_add_fusion.refs_10_.refs_0_, bf16[512,512]{1,0:T(8,128)(2,1)S(1)} %get-tuple-element.35.refs_1_, bf16[512,128]{1,0:T(8,128)(2,1)S(1)} %collective-permute-done.6.refs_2_, bf16[512,128]{1,0:T(8,128)(2,1)S(1)} %collective-permute-done.7.refs_3_, ...), custom_call_target="tpu_custom_call" | custom-call | flops 4096 | bytes 1024 | tf_op jit(solution)/shard_map/pallas_call | solution.py:687
  (5 shorter events, 0.0 us)
Async XLA Ops:
  0.6 5.5 %copy-start = (bf16[1,1,32,2,8,128]{5,4,3,2,1,0:T(8,128)(2,1)S(1)}, bf16[1,1,32,2,8,128]{5,4,3,2,1,0:T(8,128)(2,1)}, u32[]{:S(2)}) copy-start(bf16[1,1,32,2,8,128]{5,4,3,2,1,0:T(8,128)(2,1)} %param.10) | copy-start | bytes 393220
  3.1 16.5 %copy-start.1 = (bf16[1,1,32,2,8,128]{5,4,3,2,1,0:T(8,128)(2,1)S(1)}, bf16[1,1,32,2,8,128]{5,4,3,2,1,0:T(8,128)(2,1)}, u32[]{:S(2)}) copy-start(bf16[1,1,32,2,8,128]{5,4,3,2,1,0:T(8,128)(2,1)} %param.13) | copy-start | bytes 393220
  3.1 12.2 %collective-permute-start.1 = (bf16[1024,128]{1,0:T(8,128)(2,1)S(1)}, bf16[1024,128]{1,0:T(8,128)(2,1)S(1)}, u32[]{:S(2)}, u32[]{:S(2)}) collective-permute-start(bf16[1024,128]{1,0:T(8,128)(2,1)S(1)} %slice.3), channel_id=1, source_target_pairs={{0,2},{1,3},{2,0},{3,1},{4,6},{5,7},{6,4},{7,5},{8,10},{9,11},{10,... | collective-permute-start | bytes 786440 | tf_op jit(solution)/shard_map/ppermute | solution.py:501
  6.1 9.1 %collective-permute-start.4 = (bf16[512,128]{1,0:T(8,128)(2,1)S(1)}, bf16[512,128]{1,0:T(8,128)(2,1)S(1)}, u32[]{:S(2)}, u32[]{:S(2)}) collective-permute-start(bf16[512,128]{1,0:T(8,128)(2,1)S(1)} %bitcast.16), channel_id=1, source_target_pairs={{0,2},{1,3},{2,0},{3,1},{4,6},{5,7},{6,4},{7,5},{8,10},{9,11},{10,... | collective-permute-start | bytes 393224 | tf_op jit(solution)/shard_map/ppermute | solution.py:501
  6.2 20.9 %collective-permute-start = (bf16[1536,128]{1,0:T(8,128)(2,1)S(1)}, bf16[1536,128]{1,0:T(8,128)(2,1)S(1)}, u32[]{:S(2)}, u32[]{:S(2)}) collective-permute-start(bf16[1536,128]{1,0:T(8,128)(2,1)S(1)} %get-tuple-element.36.refs_1_), channel_id=1, source_target_pairs={{0,1},{1,0},{2,3},{3,2},{4,5},{5,4},{6,7},{7,6},{8,9},{9,8},{10,11... | collective-permute-start | bytes 1179656 | tf_op jit(solution)/shard_map/ppermute | solution.py:501
  6.2 9.5 %collective-permute-start.3 = (bf16[512,128]{1,0:T(8,128)(2,1)S(1)}, bf16[512,128]{1,0:T(8,128)(2,1)S(1)}, u32[]{:S(2)}, u32[]{:S(2)}) collective-permute-start(bf16[512,128]{1,0:T(8,128)(2,1)S(1)} %bitcast.17), channel_id=1, source_target_pairs={{0,1},{1,0},{2,3},{3,2},{4,5},{5,4},{6,7},{7,6},{8,9},{9,8},{10,11... | collective-permute-start | bytes 393224 | tf_op jit(solution)/shard_map/ppermute | solution.py:501
  15.3 1.3 %collective-permute-start.5 = (bf16[512,128]{1,0:T(8,128)(2,1)S(1)}, bf16[512,128]{1,0:T(8,128)(2,1)S(1)}, u32[]{:S(2)}, u32[]{:S(2)}) collective-permute-start(bf16[512,128]{1,0:T(8,128)(2,1)S(1)} %collective-permute-done.4.refs_3_), channel_id=1, source_target_pairs={{0,1},{1,0},{2,3},{3,2},{4,5},{5,4},{6,7},{7,6},{8,9},{9,8},{10,11... | collective-permute-start | bytes 393224 | tf_op jit(solution)/shard_map/ppermute | solution.py:501
  15.3 11.9 %collective-permute-start.2 = (bf16[1024,128]{1,0:T(8,128)(2,1)S(1)}, bf16[1024,128]{1,0:T(8,128)(2,1)S(1)}, u32[]{:S(2)}, u32[]{:S(2)}) collective-permute-start(bf16[1024,128]{1,0:T(8,128)(2,1)S(1)} %collective-permute-done.1.refs_3_), channel_id=1, source_target_pairs={{0,1},{1,0},{2,3},{3,2},{4,5},{5,4},{6,7},{7,6},{8,9},{9,8},{10,11... | collective-permute-start | bytes 786440 | tf_op jit(solution)/shard_map/ppermute | solution.py:501
  19.6 5.6 %collective-permute-start.8 = (bf16[512,128]{1,0:T(8,128)(2,1)S(1)}, bf16[512,128]{1,0:T(8,128)(2,1)S(1)}, u32[]{:S(2)}, u32[]{:S(2)}) collective-permute-start(bf16[512,128]{1,0:T(8,128)(2,1)S(1)} %bitcast.19), channel_id=1, source_target_pairs={{0,2},{1,3},{2,0},{3,1},{4,6},{5,7},{6,4},{7,5},{8,10},{9,11},{10,... | collective-permute-start | bytes 393224 | tf_op jit(solution)/shard_map/ppermute | solution.py:501
  25.2 12.8 %collective-permute-start.9 = (bf16[512,128]{1,0:T(8,128)(2,1)S(1)}, bf16[512,128]{1,0:T(8,128)(2,1)S(1)}, u32[]{:S(2)}, u32[]{:S(2)}) collective-permute-start(bf16[512,128]{1,0:T(8,128)(2,1)S(1)} %collective-permute-done.8.refs_3_), channel_id=1, source_target_pairs={{0,1},{1,0},{2,3},{3,2},{4,5},{5,4},{6,7},{7,6},{8,9},{9,8},{10,11... | collective-permute-start | bytes 393224 | tf_op jit(solution)/shard_map/ppermute | solution.py:501
  33.2 12.2 %collective-permute-start.6 = (bf16[512,128]{1,0:T(8,128)(2,1)S(1)}, bf16[512,128]{1,0:T(8,128)(2,1)S(1)}, u32[]{:S(2)}, u32[]{:S(2)}) collective-permute-start(bf16[512,128]{1,0:T(8,128)(2,1)S(1)} %get-tuple-element.49), channel_id=1, source_target_pairs={{0,8},{4,12},{8,0},{12,4},{16,24},{20,28},{24,16},{28,20},{1,9},{5... | collective-permute-start | bytes 393224 | tf_op jit(solution)/shard_map/ppermute | solution.py:514
  36.5 8.9 %collective-permute-start.7 = (bf16[512,128]{1,0:T(8,128)(2,1)S(1)}, bf16[512,128]{1,0:T(8,128)(2,1)S(1)}, u32[]{:S(2)}, u32[]{:S(2)}) collective-permute-start(bf16[512,128]{1,0:T(8,128)(2,1)S(1)} %get-tuple-element.55), channel_id=1, source_target_pairs={{0,4},{4,0},{8,16},{12,20},{16,8},{20,12},{24,28},{28,24},{1,5},{5... | collective-permute-start | bytes 393224 | tf_op jit(solution)/shard_map/ppermute | solution.py:514
  40.8 3.9 %collective-permute-start.10 = (bf16[96,128]{1,0:T(8,128)(2,1)S(1)}, bf16[96,128]{1,0:T(8,128)(2,1)S(1)}, u32[]{:S(2)}, u32[]{:S(2)}) collective-permute-start(bf16[96,128]{1,0:T(8,128)(2,1)S(1)} %get-tuple-element.63), channel_id=1, source_target_pairs={{0,4},{4,0},{1,5},{5,1},{2,6},{6,2},{3,7},{7,3},{8,12},{12,8},{9,1... | collective-permute-start | bytes 73736 | tf_op jit(solution)/shard_map/ppermute | solution.py:692
